TPU v7x, 32 devices: a whole 2x2x4 slice. The times are simulated.
32 devices in a mesh: gx: 4 (over y, x), gy: 8 (over z, core).
Axes of the slice: x: 2, y: 2, z: 4, core: 2. Of those that a mesh axis runs over, the one named last changes fastest.
Arguments:
- velocity: float32 [3, 128, 64, 128], P(None, 'gx', 'gy'), may hold values from -6 to 6
- stress: float32 [6, 128, 64, 128], P(None, 'gx', 'gy'), may hold values from -6 to 6
- lame_first: float32 [128, 64, 128], P('gx', 'gy'), may hold values from 0.5 to 2
- modulus: float32 [128, 64, 128], P('gx', 'gy'), may hold values from 0.5 to 2
- buoyancy: float32 [128, 64, 128], P('gx', 'gy'), may hold values from 0.5 to 2
- zone: int32 [128, 64, 128], P('gx', 'gy'), may hold values from 0 to 7
- eligible: int32 [128, 64, 128], P('gx', 'gy'), may hold values 0 or 1
- cohesion: float32 [8], replicated, may hold values from 0.2 to 2
- friction: float32 [8], replicated, may hold values from 0.1 to 0.6
- source_cell: int32 [16], replicated, may hold values from 0 to 1048575
- source_moment: float32 [6, 16], replicated, may hold values from -15 to 15
Outputs:
- velocity_out: float32 [3, 128, 64, 128], P(None, 'gx', 'gy')
- stress_out: float32 [6, 128, 64, 128], P(None, 'gx', 'gy')
All inputs are finite; a program needn't handle non-finite values. No bound on the sum of `eligible` on one device may be relied on, other than what follows from the above.
Results may differ from a plain program's by a relative error of at most 0.00011.
Values sent between devices are 32-bit elements; how exact they have to be, the bound alone decides.
No kernel may reach another device: no remote copies, remote signals or barrier semaphores. Data moves between devices by JAX's collectives and lax.ppermute only.
A program may use at most 64 MiB of HBM per device.

v0:
```python
import jax
import jax.numpy as jnp
from jax import lax
from jax.sharding import PartitionSpec as P

STEPS = 2


time_step = 0.1
near_weight = 9.0 / 8.0
far_weight = 1.0 / 24.0
shear_floor = 0.25


def extended(block, sides, width):
    for axis, dim in sides:
        count = lax.axis_size(axis)
        forward = [(i, i + 1) for i in range(count - 1)]
        backward = [(target, source) for source, target in forward]
        low = lax.ppermute(
            lax.slice_in_dim(block, block.shape[dim] - width, None, axis=dim), axis, forward
        )
        high = lax.ppermute(lax.slice_in_dim(block, 0, width, axis=dim), axis, backward)
        block = jnp.concatenate([low, block, high], axis=dim)
    return block


def crop(padded, axis, offset):
    result = padded
    for dim in range(3):
        begin = offset if dim == axis else 2
        length = padded.shape[dim] - 4
        result = lax.slice_in_dim(result, begin, begin + length, axis=dim)
    return result


def derivative(padded, axis, forward):
    if forward:
        return near_weight * (crop(padded, axis, 3) - crop(padded, axis, 2)) - far_weight * (
            crop(padded, axis, 4) - crop(padded, axis, 1)
        )
    return near_weight * (crop(padded, axis, 2) - crop(padded, axis, 1)) - far_weight * (
        crop(padded, axis, 3) - crop(padded, axis, 0)
    )


def split_velocity_update(along_x, along_y, along_z, velocity, buoyancy):
    force_x = (
        derivative(along_x[0], 0, True)
        + derivative(along_y[0], 1, False)
        + derivative(along_z[0], 2, False)
    )
    force_y = (
        derivative(along_x[1], 0, False)
        + derivative(along_y[1], 1, True)
        + derivative(along_z[1], 2, False)
    )
    force_z = (
        derivative(along_x[2], 0, False)
        + derivative(along_y[2], 1, False)
        + derivative(along_z[2], 2, True)
    )
    forces = jnp.stack([force_x, force_y, force_z])
    return velocity + time_step * buoyancy[None] * forces


def stress_update(flow_pad, stress, lame_first, modulus):
    strain_x = derivative(flow_pad[0], 0, False)
    strain_y = derivative(flow_pad[1], 1, False)
    strain_z = derivative(flow_pad[2], 2, False)
    dilation = strain_x + strain_y + strain_z
    shear_xy = derivative(flow_pad[0], 1, True) + derivative(flow_pad[1], 0, True)
    shear_xz = derivative(flow_pad[0], 2, True) + derivative(flow_pad[2], 0, True)
    shear_yz = derivative(flow_pad[1], 2, True) + derivative(flow_pad[2], 1, True)
    rates = jnp.stack(
        [
            lame_first * dilation + 2.0 * modulus * strain_x,
            lame_first * dilation + 2.0 * modulus * strain_y,
            lame_first * dilation + 2.0 * modulus * strain_z,
            modulus * shear_xy,
            modulus * shear_xz,
            modulus * shear_yz,
        ]
    )
    return stress + time_step * rates


def plastic(stress, cell_cohesion, cell_friction, eligible):
    pressure = (stress[0] + stress[1] + stress[2]) / 3.0
    dev_x = stress[0] - pressure
    dev_y = stress[1] - pressure
    dev_z = stress[2] - pressure
    second = (
        0.5 * (dev_x * dev_x + dev_y * dev_y + dev_z * dev_z)
        + stress[3] * stress[3]
        + stress[4] * stress[4]
        + stress[5] * stress[5]
    )
    strength = jnp.maximum(
        cell_cohesion * jnp.sqrt(1.0 - cell_friction * cell_friction) - pressure * cell_friction,
        0.0,
    )
    ratio = jnp.minimum(1.0, strength / jnp.maximum(jnp.sqrt(second), shear_floor))
    factor = jnp.where(eligible == 1, ratio, 1.0)
    return jnp.stack(
        [
            pressure + factor * dev_x,
            pressure + factor * dev_y,
            pressure + factor * dev_z,
            factor * stress[3],
            factor * stress[4],
            factor * stress[5],
        ]
    )


def pad_depth(field, width):
    return jnp.pad(field, ((0, 0), (0, 0), (0, 0), (width, width)))


def on_device(
    velocity,
    stress,
    lame_first,
    modulus,
    buoyancy,
    zone,
    eligible,
    cohesion,
    friction,
    source_cell,
    source_moment,
):
    rows_x, rows_y, depth = zone.shape
    total_y = rows_y * lax.axis_size("gy")
    start_x = lax.axis_index("gx") * rows_x
    start_y = lax.axis_index("gy") * rows_y
    cell_cohesion = jnp.zeros(zone.shape, jnp.float32)
    cell_friction = jnp.zeros(zone.shape, jnp.float32)
    for which in range(cohesion.shape[0]):
        hit = zone == which
        cell_cohesion = cell_cohesion + jnp.where(hit, cohesion[which], 0.0)
        cell_friction = cell_friction + jnp.where(hit, friction[which], 0.0)
    plane = total_y * depth
    src_x = source_cell // plane
    src_y = source_cell // depth % total_y
    src_z = source_cell % depth
    pick_x = (src_x[:, None] == start_x + jnp.arange(rows_x, dtype=jnp.int32)[None]).astype(
        jnp.float32
    )
    pick_y = (src_y[:, None] == start_y + jnp.arange(rows_y, dtype=jnp.int32)[None]).astype(
        jnp.float32
    )
    pick_z = (src_z[:, None] == jnp.arange(depth, dtype=jnp.int32)[None]).astype(jnp.float32)
    injection = jnp.einsum(
        "cs,sx,sy,sz->cxyz",
        time_step * source_moment,
        pick_x,
        pick_y,
        pick_z,
        precision=lax.Precision.HIGHEST,
    )
    for step in range(STEPS):
        strike_part = jnp.stack([stress[0], stress[3], stress[4]])
        normal_part = jnp.stack([stress[3], stress[1], stress[5]])
        depth_part = jnp.stack([stress[4], stress[5], stress[2]])
        along_x = extended(strike_part, (("gx", 1),), 2)
        along_y = extended(normal_part, (("gy", 2),), 2)
        along_x = jnp.pad(along_x, ((0, 0), (0, 0), (2, 2), (2, 2)))
        along_y = jnp.pad(along_y, ((0, 0), (2, 2), (0, 0), (2, 2)))
        along_z = jnp.pad(depth_part, ((0, 0), (2, 2), (2, 2), (2, 2)))
        velocity = split_velocity_update(along_x, along_y, along_z, velocity, buoyancy)
        flow_pad = extended(velocity, (("gx", 1), ("gy", 2)), 2)
        stress = stress_update(pad_depth(flow_pad, 2), stress, lame_first, modulus)
        stress = stress + injection
        stress = plastic(stress, cell_cohesion, cell_friction, eligible)
    return (velocity, stress)


def solution(mesh):
    placed = (
        P(None, "gx", "gy", None),
        P(None, "gx", "gy", None),
        P("gx", "gy", None),
        P("gx", "gy", None),
        P("gx", "gy", None),
        P("gx", "gy", None),
        P("gx", "gy", None),
        P(),
        P(),
        P(),
        P(),
    )
    return jax.shard_map(
        on_device,
        mesh=mesh,
        in_specs=placed,
        out_specs=(P(None, "gx", "gy", None), P(None, "gx", "gy", None)),
        check_vma=False,
    )
```

profile of v0, /device:TPU:1, one launch (start us, length us, event | category | flops | bytes accessed | tf_op | source)
XLA Modules:
  0.0 108.4 jit_solution(15015662236129044478)
XLA Ops:
  0.6 1.1 %fusion.184 = (f32[2,32,8,128]{3,2,1,0:T(8,128)S(1)}, f32[2,32,8,128]{3,2,1,0:T(8,128)S(1)}) fusion(f32[6,32,8,128]{3,2,1,0:T(8,128)} %param.12), kind=kLoop, calls=%fused_computation.440 | loop fusion | bytes 1048576 | tf_op jit(solution)/shard_map/slice | solution.py:164
  2.1 3.9 %collective-permute-start = (f32[3,2,8,128]{3,1,2,0:T(2,128)S(1)}, f32[3,2,8,128]{3,1,2,0:T(2,128)S(1)}, u32[]{:S(2)}, u32[]{:S(2)}) collective-permute-start(f32[3,2,8,128]{3,1,2,0:T(2,128)S(1)} %get-tuple-element.117), channel_id=1, source_target_pairs={{0,8},{8,16},{16,24},{1,9},{9,17},{17,25},{2,10},{10,18},{18,26},{... | collective-permute-start | bytes 73736 | tf_op jit(solution)/shard_map/ppermute | solution.py:20
  6.1 1.3 %collective-permute-start.1 = (f32[3,2,8,128]{3,1,2,0:T(2,128)S(1)}, f32[3,2,8,128]{3,1,2,0:T(2,128)S(1)}, u32[]{:S(2)}, u32[]{:S(2)}) collective-permute-start(f32[3,2,8,128]{3,1,2,0:T(2,128)S(1)} %get-tuple-element.118), channel_id=1, source_target_pairs={{8,0},{16,8},{24,16},{9,1},{17,9},{25,17},{10,2},{18,10},{26,18},{... | collective-permute-start | bytes 73736 | tf_op jit(solution)/shard_map/ppermute | solution.py:23
  7.5 4.0 %collective-permute-start.2 = (f32[3,32,2,128]{3,1,2,0:T(8,128)S(1)}, f32[3,32,2,128]{3,1,2,0:T(8,128)S(1)}, u32[]{:S(2)}, u32[]{:S(2)}) collective-permute-start(f32[3,32,2,128]{3,1,2,0:T(8,128)S(1)} %get-tuple-element.119), channel_id=1, source_target_pairs={{0,1},{1,2},{2,3},{3,4},{4,5},{5,6},{6,7},{8,9},{9,10},{10,11},{11... | collective-permute-start | bytes 294920 | tf_op jit(solution)/shard_map/ppermute | solution.py:20
  11.5 1.9 %collective-permute-start.3 = (f32[3,32,2,128]{3,1,2,0:T(8,128)S(1)}, f32[3,32,2,128]{3,1,2,0:T(8,128)S(1)}, u32[]{:S(2)}, u32[]{:S(2)}) collective-permute-start(f32[3,32,2,128]{3,1,2,0:T(8,128)S(1)} %get-tuple-element.120), channel_id=1, source_target_pairs={{1,0},{2,1},{3,2},{4,3},{5,4},{6,5},{7,6},{9,8},{10,9},{11,10},{12... | collective-permute-start | bytes 294920 | tf_op jit(solution)/shard_map/ppermute | solution.py:23
  14.4 1.0 convolution_bitcast_fusion
  15.4 0.5 select_maximum_fusion.23
  15.9 0.6 slice_bitcast_fusion.59
  16.5 0.9 collective-permute-done.3
  17.5 0.5 select_maximum_fusion.19
  18.1 0.4 fusion.142
  18.5 0.4 fusion.154
  19.0 0.5 fusion.130
  19.7 4.3 %collective-permute-start.4 = (f32[3,2,8,128]{3,1,2,0:T(2,128)S(1)}, f32[3,2,8,128]{3,1,2,0:T(2,128)S(1)}, u32[]{:S(2)}, u32[]{:S(2)}) collective-permute-start(f32[3,2,8,128]{3,1,2,0:T(2,128)S(1)} %get-tuple-element.115), channel_id=1, source_target_pairs={{0,8},{8,16},{16,24},{1,9},{9,17},{17,25},{2,10},{10,18},{18,26},{... | collective-permute-start | bytes 73736 | tf_op jit(solution)/shard_map/ppermute | solution.py:20
  24.0 1.3 %collective-permute-start.5 = (f32[3,2,8,128]{3,1,2,0:T(2,128)S(1)}, f32[3,2,8,128]{3,1,2,0:T(2,128)S(1)}, u32[]{:S(2)}, u32[]{:S(2)}) collective-permute-start(f32[3,2,8,128]{3,1,2,0:T(2,128)S(1)} %get-tuple-element.116), channel_id=1, source_target_pairs={{8,0},{16,8},{24,16},{9,1},{17,9},{25,17},{10,2},{18,10},{26,18},{... | collective-permute-start | bytes 73736 | tf_op jit(solution)/shard_map/ppermute | solution.py:23
  25.3 0.7 fusion.187
  25.9 3.3 %collective-permute-done.5 = f32[3,2,8,128]{3,1,2,0:T(2,128)S(1)} collective-permute-done((f32[3,2,8,128]{3,1,2,0:T(2,128)S(1)}, f32[3,2,8,128]{3,1,2,0:T(2,128)S(1)}, u32[]{:S(2)}, u32[]{:S(2)}) %collective-permute-start.5) | collective-permute-done | bytes 24608 | tf_op jit(solution)/shard_map/ppermute | solution.py:23
  29.2 4.0 %collective-permute-start.6 = (f32[3,36,2,128]{3,1,2,0:T(8,128)S(1)}, f32[3,36,2,128]{3,1,2,0:T(8,128)S(1)}, u32[]{:S(2)}, u32[]{:S(2)}) collective-permute-start(f32[3,36,2,128]{3,1,2,0:T(8,128)S(1)} %get-tuple-element.107), channel_id=1, source_target_pairs={{0,1},{1,2},{2,3},{3,4},{4,5},{5,6},{6,7},{8,9},{9,10},{10,11},{11... | collective-permute-start | bytes 331784 | tf_op jit(solution)/shard_map/ppermute | solution.py:20
  33.3 1.9 %collective-permute-start.7 = (f32[3,36,2,128]{3,1,2,0:T(8,128)S(1)}, f32[3,36,2,128]{3,1,2,0:T(8,128)S(1)}, u32[]{:S(2)}, u32[]{:S(2)}) collective-permute-start(f32[3,36,2,128]{3,1,2,0:T(8,128)S(1)} %get-tuple-element.108), channel_id=1, source_target_pairs={{1,0},{2,1},{3,2},{4,3},{5,4},{6,5},{7,6},{9,8},{10,9},{11,10},{12... | collective-permute-start | bytes 331784 | tf_op jit(solution)/shard_map/ppermute | solution.py:23
  35.2 0.7 fusion.188
  35.9 3.6 %collective-permute-done.7 = f32[3,36,2,128]{3,1,2,0:T(8,128)S(1)} collective-permute-done((f32[3,36,2,128]{3,1,2,0:T(8,128)S(1)}, f32[3,36,2,128]{3,1,2,0:T(8,128)S(1)}, u32[]{:S(2)}, u32[]{:S(2)}) %collective-permute-start.7) | collective-permute-done | bytes 110624 | tf_op jit(solution)/shard_map/ppermute | solution.py:23
  39.5 0.6 select_maximum_fusion.14
  40.1 0.6 slice_bitcast_fusion.32
  41.0 0.4 bitcast_dynamic-update-slice_fusion.11
  42.9 0.6 copy-done.4
  43.6 10.6 %constant_dynamic-update-slice_fusion.5 = (f32[6,32,8,128]{3,1,2,0:T(8,128)S(1)}, f32[1,32,8,128]{3,1,2,0:T(8,128)S(1)}, f32[32,8,128]{2,0,1:T(8,128)S(1)}, pred...) fusion(f32[6,32,8,128]{3,1,2,0:T(8,128)S(1)} %copy_add_fusion.1, ...), kind=kLoop, calls=%fused_computation.407 | loop fusion | flops 2260991 | bytes 1867840
  54.3 1.9 %collective-permute-start.10 = (f32[3,32,2,128]{3,1,2,0:T(8,128)S(1)}, f32[3,32,2,128]{3,1,2,0:T(8,128)S(1)}, u32[]{:S(2)}, u32[]{:S(2)}) collective-permute-start(f32[3,32,2,128]{3,1,2,0:T(8,128)S(1)} %get-tuple-element.113), channel_id=1, source_target_pairs={{0,1},{1,2},{2,3},{3,4},{4,5},{5,6},{6,7},{8,9},{9,10},{10,11},{11... | collective-permute-start | bytes 294920 | tf_op jit(solution)/shard_map/ppermute | solution.py:20
  56.3 2.4 %collective-permute-start.11 = (f32[3,32,2,128]{3,1,2,0:T(8,128)S(1)}, f32[3,32,2,128]{3,1,2,0:T(8,128)S(1)}, u32[]{:S(2)}, u32[]{:S(2)}) collective-permute-start(f32[3,32,2,128]{3,1,2,0:T(8,128)S(1)} %get-tuple-element.114), channel_id=1, source_target_pairs={{1,0},{2,1},{3,2},{4,3},{5,4},{6,5},{7,6},{9,8},{10,9},{11,10},{12... | collective-permute-start | bytes 294920 | tf_op jit(solution)/shard_map/ppermute | solution.py:23
  58.7 4.4 %collective-permute-start.8 = (f32[3,2,8,128]{3,1,2,0:T(2,128)S(1)}, f32[3,2,8,128]{3,1,2,0:T(2,128)S(1)}, u32[]{:S(2)}, u32[]{:S(2)}) collective-permute-start(f32[3,2,8,128]{3,1,2,0:T(2,128)S(1)} %get-tuple-element.111), channel_id=1, source_target_pairs={{0,8},{8,16},{16,24},{1,9},{9,17},{17,25},{2,10},{10,18},{18,26},{... | collective-permute-start | bytes 73736 | tf_op jit(solution)/shard_map/ppermute | solution.py:20
  63.1 1.5 %collective-permute-start.9 = (f32[3,2,8,128]{3,1,2,0:T(2,128)S(1)}, f32[3,2,8,128]{3,1,2,0:T(2,128)S(1)}, u32[]{:S(2)}, u32[]{:S(2)}) collective-permute-start(f32[3,2,8,128]{3,1,2,0:T(2,128)S(1)} %get-tuple-element.112), channel_id=1, source_target_pairs={{8,0},{16,8},{24,16},{9,1},{17,9},{25,17},{10,2},{18,10},{26,18},{... | collective-permute-start | bytes 73736 | tf_op jit(solution)/shard_map/ppermute | solution.py:23
  64.6 3.5 %collective-permute-done.9 = f32[3,2,8,128]{3,1,2,0:T(2,128)S(1)} collective-permute-done((f32[3,2,8,128]{3,1,2,0:T(2,128)S(1)}, f32[3,2,8,128]{3,1,2,0:T(2,128)S(1)}, u32[]{:S(2)}, u32[]{:S(2)}) %collective-permute-start.9) | collective-permute-done | bytes 24608 | tf_op jit(solution)/shard_map/ppermute | solution.py:23
  68.1 3.8 %select_maximum_fusion.10 = (f32[3,36,12,132]{3,1,2,0:T(8,128)S(1)}, f32[3,36,12,132]{3,1,2,0:T(8,128)S(1)}, f32[3,36,12,132]{3,1,2,0:T(8,128)S(1)}) fusion(f32[3,2,8,128]{3,1,2,0:T(2,128)S(1)} %collective-permute-done.9, f32[3,2,8,128]{3,1,2,0:T(2,128)S(1)} %collective-permute-done.8, f32[1,32,8,128]{3,1,2,0:T(8,128)S(1)} %get-tuple-element.14, ...), kind=kLoop, calls=%fused_computation.26 | loop fusion | flops 9408960 | bytes 3085056 | tf_op jit(solution)/shard_map/concatenate | solution.py:24
  71.9 0.6 slice_bitcast_fusion.29
  72.9 0.5 fusion.67
  73.3 0.4 fusion.79
  73.8 0.5 fusion.55
  74.4 2.6 %collective-permute-start.12 = (f32[3,2,8,128]{3,1,2,0:T(2,128)S(1)}, f32[3,2,8,128]{3,1,2,0:T(2,128)S(1)}, u32[]{:S(2)}, u32[]{:S(2)}) collective-permute-start(f32[3,2,8,128]{3,1,2,0:T(2,128)S(1)} %get-tuple-element.109), channel_id=1, source_target_pairs={{0,8},{8,16},{16,24},{1,9},{9,17},{17,25},{2,10},{10,18},{18,26},{... | collective-permute-start | bytes 73736 | tf_op jit(solution)/shard_map/ppermute | solution.py:20
  77.1 1.3 %collective-permute-start.13 = (f32[3,2,8,128]{3,1,2,0:T(2,128)S(1)}, f32[3,2,8,128]{3,1,2,0:T(2,128)S(1)}, u32[]{:S(2)}, u32[]{:S(2)}) collective-permute-start(f32[3,2,8,128]{3,1,2,0:T(2,128)S(1)} %get-tuple-element.110), channel_id=1, source_target_pairs={{8,0},{16,8},{24,16},{9,1},{17,9},{25,17},{10,2},{18,10},{26,18},{... | collective-permute-start | bytes 73736 | tf_op jit(solution)/shard_map/ppermute | solution.py:23
  78.4 3.3 %collective-permute-done.13 = f32[3,2,8,128]{3,1,2,0:T(2,128)S(1)} collective-permute-done((f32[3,2,8,128]{3,1,2,0:T(2,128)S(1)}, f32[3,2,8,128]{3,1,2,0:T(2,128)S(1)}, u32[]{:S(2)}, u32[]{:S(2)}) %collective-permute-start.13) | collective-permute-done | bytes 24608 | tf_op jit(solution)/shard_map/ppermute | solution.py:23
  81.7 5.5 %collective-permute-start.14 = (f32[3,36,2,128]{3,1,2,0:T(8,128)S(1)}, f32[3,36,2,128]{3,1,2,0:T(8,128)S(1)}, u32[]{:S(2)}, u32[]{:S(2)}) collective-permute-start(f32[3,36,2,128]{3,1,2,0:T(8,128)S(1)} %get-tuple-element.105), channel_id=1, source_target_pairs={{0,1},{1,2},{2,3},{3,4},{4,5},{5,6},{6,7},{8,9},{9,10},{10,11},{11... | collective-permute-start | bytes 331784 | tf_op jit(solution)/shard_map/ppermute | solution.py:20
  87.2 1.9 %collective-permute-start.15 = (f32[3,36,2,128]{3,1,2,0:T(8,128)S(1)}, f32[3,36,2,128]{3,1,2,0:T(8,128)S(1)}, u32[]{:S(2)}, u32[]{:S(2)}) collective-permute-start(f32[3,36,2,128]{3,1,2,0:T(8,128)S(1)} %get-tuple-element.106), channel_id=1, source_target_pairs={{1,0},{2,1},{3,2},{4,3},{5,4},{6,5},{7,6},{9,8},{10,9},{11,10},{12... | collective-permute-start | bytes 331784 | tf_op jit(solution)/shard_map/ppermute | solution.py:23
  89.1 1.0 copy.48
  90.1 3.3 %collective-permute-done.15 = f32[3,36,2,128]{3,1,2,0:T(8,128)S(1)} collective-permute-done((f32[3,36,2,128]{3,1,2,0:T(8,128)S(1)}, f32[3,36,2,128]{3,1,2,0:T(8,128)S(1)}, u32[]{:S(2)}, u32[]{:S(2)}) %collective-permute-start.15) | collective-permute-done | bytes 110624 | tf_op jit(solution)/shard_map/ppermute | solution.py:23
  93.4 0.6 select_maximum_fusion
  93.9 0.6 slice_bitcast_fusion.2
  94.6 0.4 bitcast_dynamic-update-slice_fusion.8
  96.4 10.5 %bitcast_dynamic-update-slice_fusion.5 = (f32[6,32,8,128]{3,1,2,0:T(8,128)S(1)}, f32[32,8,128]{2,0,1:T(8,128)S(1)}, f32[32,8,128]{2,0,1:T(8,128)S(1)}) fusion(f32[6,32,8,128]{3,1,0,2:T(8,128)S(1)} %copy_add_fusion, pred[32,8,128]{2,0,1:T(8,128)(4,1)S(1)} %get-tuple-element.32, pred[32,8,128]{2,0,1:T(8,128)(4,1)S(1)} %get-tuple-element.31, f32[]{:T(128)} %bitcast.62, ...), kind=kLoop, calls=%fused_computation.350 | loop fusion | flops 1966079 | bytes 1474624
  107.1 1.3 %copy.49 = f32[6,32,8,128]{3,2,1,0:T(8,128)} copy(f32[6,32,8,128]{3,1,2,0:T(8,128)S(1)} %bitcast_dynamic-update-slice_fusion) | data formatting | bytes 1572864
  (84 shorter events, 5.7 us)
Async XLA Ops:
  0.6 1.3 %copy-start.1 = (f32[6,32,8,128]{3,2,1,0:T(8,128)S(1)}, f32[6,32,8,128]{3,2,1,0:T(8,128)}, u32[]{:S(2)}) copy-start(f32[6,32,8,128]{3,2,1,0:T(8,128)} %param.12) | copy-start | bytes 2359300
  2.0 11.5 %copy-start.10 = (s32[16]{0:T(128)S(1)}, s32[16]{0:T(128)}, u32[]{:S(2)}) copy-start(s32[16]{0:T(128)} %param.20) | copy-start | bytes 196
  2.0 11.6 %copy-start.9 = (f32[6,16]{1,0:T(8,128)S(1)}, f32[6,16]{1,0:T(8,128)}, u32[]{:S(2)}) copy-start(f32[6,16]{1,0:T(8,128)} %param.21) | copy-start | bytes 1156
  2.1 13.3 %collective-permute-start = (f32[3,2,8,128]{3,1,2,0:T(2,128)S(1)}, f32[3,2,8,128]{3,1,2,0:T(2,128)S(1)}, u32[]{:S(2)}, u32[]{:S(2)}) collective-permute-start(f32[3,2,8,128]{3,1,2,0:T(2,128)S(1)} %get-tuple-element.117), channel_id=1, source_target_pairs={{0,8},{8,16},{16,24},{1,9},{9,17},{17,25},{2,10},{10,18},{18,26},{... | collective-permute-start | bytes 73736 | tf_op jit(solution)/shard_map/ppermute | solution.py:20
  6.1 9.4 %collective-permute-start.1 = (f32[3,2,8,128]{3,1,2,0:T(2,128)S(1)}, f32[3,2,8,128]{3,1,2,0:T(2,128)S(1)}, u32[]{:S(2)}, u32[]{:S(2)}) collective-permute-start(f32[3,2,8,128]{3,1,2,0:T(2,128)S(1)} %get-tuple-element.118), channel_id=1, source_target_pairs={{8,0},{16,8},{24,16},{9,1},{17,9},{25,17},{10,2},{18,10},{26,18},{... | collective-permute-start | bytes 73736 | tf_op jit(solution)/shard_map/ppermute | solution.py:23
  7.5 9.0 %collective-permute-start.2 = (f32[3,32,2,128]{3,1,2,0:T(8,128)S(1)}, f32[3,32,2,128]{3,1,2,0:T(8,128)S(1)}, u32[]{:S(2)}, u32[]{:S(2)}) collective-permute-start(f32[3,32,2,128]{3,1,2,0:T(8,128)S(1)} %get-tuple-element.119), channel_id=1, source_target_pairs={{0,1},{1,2},{2,3},{3,4},{4,5},{5,6},{6,7},{8,9},{9,10},{10,11},{11... | collective-permute-start | bytes 294920 | tf_op jit(solution)/shard_map/ppermute | solution.py:20
  11.5 5.9 %collective-permute-start.3 = (f32[3,32,2,128]{3,1,2,0:T(8,128)S(1)}, f32[3,32,2,128]{3,1,2,0:T(8,128)S(1)}, u32[]{:S(2)}, u32[]{:S(2)}) collective-permute-start(f32[3,32,2,128]{3,1,2,0:T(8,128)S(1)} %get-tuple-element.120), channel_id=1, source_target_pairs={{1,0},{2,1},{3,2},{4,3},{5,4},{6,5},{7,6},{9,8},{10,9},{11,10},{12... | collective-permute-start | bytes 294920 | tf_op jit(solution)/shard_map/ppermute | solution.py:23
  14.1 1.3 %copy-start.6 = (f32[32,8,128]{2,1,0:T(8,128)S(1)}, f32[32,8,128]{2,1,0:T(8,128)}, u32[]{:S(2)}) copy-start(f32[32,8,128]{2,1,0:T(8,128)} %param.15) | copy-start | bytes 393220
  18.5 1.0 copy-start.2
  19.0 6.3 %copy-start.7 = (f32[8]{0:T(128)S(1)}, f32[8]{0:T(128)}, u32[]{:S(2)}) copy-start(f32[8]{0:T(128)} %param.18) | copy-start | bytes 100
  19.5 15.7 %copy-start.8 = (f32[8]{0:T(128)S(1)}, f32[8]{0:T(128)}, u32[]{:S(2)}) copy-start(f32[8]{0:T(128)} %param.19) | copy-start | bytes 100
  19.7 6.3 %collective-permute-start.4 = (f32[3,2,8,128]{3,1,2,0:T(2,128)S(1)}, f32[3,2,8,128]{3,1,2,0:T(2,128)S(1)}, u32[]{:S(2)}, u32[]{:S(2)}) collective-permute-start(f32[3,2,8,128]{3,1,2,0:T(2,128)S(1)} %get-tuple-element.115), channel_id=1, source_target_pairs={{0,8},{8,16},{16,24},{1,9},{9,17},{17,25},{2,10},{10,18},{18,26},{... | collective-permute-start | bytes 73736 | tf_op jit(solution)/shard_map/ppermute | solution.py:20
  24.0 5.2 %collective-permute-start.5 = (f32[3,2,8,128]{3,1,2,0:T(2,128)S(1)}, f32[3,2,8,128]{3,1,2,0:T(2,128)S(1)}, u32[]{:S(2)}, u32[]{:S(2)}) collective-permute-start(f32[3,2,8,128]{3,1,2,0:T(2,128)S(1)} %get-tuple-element.116), channel_id=1, source_target_pairs={{8,0},{16,8},{24,16},{9,1},{17,9},{25,17},{10,2},{18,10},{26,18},{... | collective-permute-start | bytes 73736 | tf_op jit(solution)/shard_map/ppermute | solution.py:23
  29.2 6.7 %collective-permute-start.6 = (f32[3,36,2,128]{3,1,2,0:T(8,128)S(1)}, f32[3,36,2,128]{3,1,2,0:T(8,128)S(1)}, u32[]{:S(2)}, u32[]{:S(2)}) collective-permute-start(f32[3,36,2,128]{3,1,2,0:T(8,128)S(1)} %get-tuple-element.107), channel_id=1, source_target_pairs={{0,1},{1,2},{2,3},{3,4},{4,5},{5,6},{6,7},{8,9},{9,10},{10,11},{11... | collective-permute-start | bytes 331784 | tf_op jit(solution)/shard_map/ppermute | solution.py:20
  33.3 6.2 %collective-permute-start.7 = (f32[3,36,2,128]{3,1,2,0:T(8,128)S(1)}, f32[3,36,2,128]{3,1,2,0:T(8,128)S(1)}, u32[]{:S(2)}, u32[]{:S(2)}) collective-permute-start(f32[3,36,2,128]{3,1,2,0:T(8,128)S(1)} %get-tuple-element.108), channel_id=1, source_target_pairs={{1,0},{2,1},{3,2},{4,3},{5,4},{6,5},{7,6},{9,8},{10,9},{11,10},{12... | collective-permute-start | bytes 331784 | tf_op jit(solution)/shard_map/ppermute | solution.py:23
  40.0 0.9 copy-start
  40.0 1.0 copy-start.3
  42.6 0.9 copy-start.4
  42.6 1.0 copy-start.5
  54.3 13.7 %collective-permute-start.10 = (f32[3,32,2,128]{3,1,2,0:T(8,128)S(1)}, f32[3,32,2,128]{3,1,2,0:T(8,128)S(1)}, u32[]{:S(2)}, u32[]{:S(2)}) collective-permute-start(f32[3,32,2,128]{3,1,2,0:T(8,128)S(1)} %get-tuple-element.113), channel_id=1, source_target_pairs={{0,1},{1,2},{2,3},{3,4},{4,5},{5,6},{6,7},{8,9},{9,10},{10,11},{11... | collective-permute-start | bytes 294920 | tf_op jit(solution)/shard_map/ppermute | solution.py:20
  56.3 11.8 %collective-permute-start.11 = (f32[3,32,2,128]{3,1,2,0:T(8,128)S(1)}, f32[3,32,2,128]{3,1,2,0:T(8,128)S(1)}, u32[]{:S(2)}, u32[]{:S(2)}) collective-permute-start(f32[3,32,2,128]{3,1,2,0:T(8,128)S(1)} %get-tuple-element.114), channel_id=1, source_target_pairs={{1,0},{2,1},{3,2},{4,3},{5,4},{6,5},{7,6},{9,8},{10,9},{11,10},{12... | collective-permute-start | bytes 294920 | tf_op jit(solution)/shard_map/ppermute | solution.py:23
  58.7 5.9 %collective-permute-start.8 = (f32[3,2,8,128]{3,1,2,0:T(2,128)S(1)}, f32[3,2,8,128]{3,1,2,0:T(2,128)S(1)}, u32[]{:S(2)}, u32[]{:S(2)}) collective-permute-start(f32[3,2,8,128]{3,1,2,0:T(2,128)S(1)} %get-tuple-element.111), channel_id=1, source_target_pairs={{0,8},{8,16},{16,24},{1,9},{9,17},{17,25},{2,10},{10,18},{18,26},{... | collective-permute-start | bytes 73736 | tf_op jit(solution)/shard_map/ppermute | solution.py:20
  63.1 5.0 %collective-permute-start.9 = (f32[3,2,8,128]{3,1,2,0:T(2,128)S(1)}, f32[3,2,8,128]{3,1,2,0:T(2,128)S(1)}, u32[]{:S(2)}, u32[]{:S(2)}) collective-permute-start(f32[3,2,8,128]{3,1,2,0:T(2,128)S(1)} %get-tuple-element.112), channel_id=1, source_target_pairs={{8,0},{16,8},{24,16},{9,1},{17,9},{25,17},{10,2},{18,10},{26,18},{... | collective-permute-start | bytes 73736 | tf_op jit(solution)/shard_map/ppermute | solution.py:23
  74.4 3.9 %collective-permute-start.12 = (f32[3,2,8,128]{3,1,2,0:T(2,128)S(1)}, f32[3,2,8,128]{3,1,2,0:T(2,128)S(1)}, u32[]{:S(2)}, u32[]{:S(2)}) collective-permute-start(f32[3,2,8,128]{3,1,2,0:T(2,128)S(1)} %get-tuple-element.109), channel_id=1, source_target_pairs={{0,8},{8,16},{16,24},{1,9},{9,17},{17,25},{2,10},{10,18},{18,26},{... | collective-permute-start | bytes 73736 | tf_op jit(solution)/shard_map/ppermute | solution.py:20
  77.1 4.6 %collective-permute-start.13 = (f32[3,2,8,128]{3,1,2,0:T(2,128)S(1)}, f32[3,2,8,128]{3,1,2,0:T(2,128)S(1)}, u32[]{:S(2)}, u32[]{:S(2)}) collective-permute-start(f32[3,2,8,128]{3,1,2,0:T(2,128)S(1)} %get-tuple-element.110), channel_id=1, source_target_pairs={{8,0},{16,8},{24,16},{9,1},{17,9},{25,17},{10,2},{18,10},{26,18},{... | collective-permute-start | bytes 73736 | tf_op jit(solution)/shard_map/ppermute | solution.py:23
  81.7 8.4 %collective-permute-start.14 = (f32[3,36,2,128]{3,1,2,0:T(8,128)S(1)}, f32[3,36,2,128]{3,1,2,0:T(8,128)S(1)}, u32[]{:S(2)}, u32[]{:S(2)}) collective-permute-start(f32[3,36,2,128]{3,1,2,0:T(8,128)S(1)} %get-tuple-element.105), channel_id=1, source_target_pairs={{0,1},{1,2},{2,3},{3,4},{4,5},{5,6},{6,7},{8,9},{9,10},{10,11},{11... | collective-permute-start | bytes 331784 | tf_op jit(solution)/shard_map/ppermute | solution.py:20
  87.2 6.2 %collective-permute-start.15 = (f32[3,36,2,128]{3,1,2,0:T(8,128)S(1)}, f32[3,36,2,128]{3,1,2,0:T(8,128)S(1)}, u32[]{:S(2)}, u32[]{:S(2)}) collective-permute-start(f32[3,36,2,128]{3,1,2,0:T(8,128)S(1)} %get-tuple-element.106), channel_id=1, source_target_pairs={{1,0},{2,1},{3,2},{4,3},{5,4},{6,5},{7,6},{9,8},{10,9},{11,10},{12... | collective-permute-start | bytes 331784 | tf_op jit(solution)/shard_map/ppermute | solution.py:23
where the time goes:
time: 109 us; the launch traced here: 108 us
  starting transfers between devices  44.2 us (41%)
  other arithmetic  34.6 us (32%)
  waiting for transfers between devices  17.8 us (16%)
  local copies, waits for them, and re-layouts  9.41 us (9%)
  between operations  1.37 us (1%)
    ppermute x8, starting transfers between devices, extended(): lax.ppermute(lax.slice_in_dim(block, block.shape[dim] - width, None, axis...  30.7 us
    unnamed x20, other arithmetic  23.7 us
    ppermute x8, waiting for transfers between devices, extended(): lax.ppermute(lax.slice_in_dim(block, 0, width, axis=dim), axis, backward)  17.8 us
    ppermute x8, starting transfers between devices, extended(): lax.ppermute(lax.slice_in_dim(block, 0, width, axis=dim), axis, backward)  13.5 us
    concatenate x5, other arithmetic, extended(): block = jnp.concatenate([low, block, high], axis=dim)  5.83 us
    unnamed x31, local copies, waits for them, and re-layouts  3.74 us
    slice x7, local copies, waits for them, and re-layouts, crop(): result = lax.slice_in_dim(result, begin, begin + length, axis=dim)  3.06 us
    another operation x6, other arithmetic, split_velocity_update(): forces = jnp.stack([force_x, force_y, force_z])  2.74 us
  transfers between devices with their start and end apart: 16, of which 6 were waited for; matrix products, arithmetic and copies ran while one was open for 5% of the time, Pallas kernels for 0%

commit v1 on v0

v1 whole, which is shorter than its diff:
```python
import jax
import jax.numpy as jnp
from jax import lax
from jax.experimental import pallas as pl
from jax.experimental.pallas import tpu as pltpu
from jax.sharding import PartitionSpec as P

STEPS = 2

time_step = 0.1
near_weight = 9.0 / 8.0
far_weight = 1.0 / 24.0
shear_floor = 0.25

XX, YY, ZZ, XY, XZ, YZ = range(6)

LOW_Y = ((XX, 1), (XY, 3), (XZ, 1), (YY, 3), (YZ, 3), (ZZ, 1))
HIGH_Y = ((XX, 2), (XY, 3), (XZ, 2), (YY, 3), (YZ, 3), (ZZ, 2))
LOW_X = ((XX, 3), (XY, 3), (XZ, 3), (YY, 1), (YZ, 1), (ZZ, 1))
HIGH_X = ((XX, 3), (XY, 3), (XZ, 3), (YY, 2), (YZ, 2), (ZZ, 2))
LOW_FLOW_Y = ((0, 1), (1, 2), (2, 1))
HIGH_FLOW_Y = ((0, 2), (1, 1), (2, 2))
LOW_FLOW_X = ((0, 2), (1, 1), (2, 1))
HIGH_FLOW_X = ((0, 1), (1, 2), (2, 2))

PAD_X = 4
RIM = 8


class Shape:
    def __init__(self, rows_x, rows_y, depth):
        self.rows_x, self.rows_y, self.depth = rows_x, rows_y, depth
        self.pitch = rows_y + RIM
        self.rows = (rows_x + 2 * PAD_X + 1) * self.pitch

    def row(self, x, y):
        return (x + PAD_X) * self.pitch + RIM + y


def entries(spec):
    return [(c, k) for c, depth in spec for k in range(depth)]


def y_rows(low, high, rows_y):
    up = [(c, rows_y - 1 - k) for c, k in entries(low)]
    down = [(c, k) for c, k in entries(high)]
    return up, down


def got_y(low, high, rows_y):
    below = [(c, -1 - k) for c, k in entries(low)]
    above = [(c, rows_y + k) for c, k in entries(high)]
    return below, above


def pack_y(shape, pairs, out):
    for slot, (ref, y) in enumerate(pairs):
        for x in range(0, shape.rows_x, 8):
            out[slot, pl.ds(x, 8), :] = ref[pl.ds(shape.row(x, y), 8, stride=shape.pitch), :]


def unpack_y(shape, pairs, got):
    for slot, (ref, y) in enumerate(pairs):
        for x in range(0, shape.rows_x, 8):
            ref[pl.ds(shape.row(x, y), 8, stride=shape.pitch), :] = got[slot, pl.ds(x, 8), :]


def pack_x(shape, whole, inner, out):
    sub = lax.broadcasted_iota(jnp.int32, (8, shape.depth), 0)
    slot = 0
    for ref, x, rim in whole:
        for t in range(0, shape.rows_y, 8):
            out[slot] = ref[pl.ds(shape.row(x, t), 8), :]
            slot += 1
        if rim:
            after = ref[pl.ds(shape.row(x + 1, -RIM), 8), :]
            before = ref[pl.ds(shape.row(x, -RIM), 8), :]
            out[slot] = jnp.where(sub < 4, after, before)
            slot += 1
    return slot


def unpack_x(shape, whole, got):
    slot = 0
    for ref, x, rim in whole:
        for t in range(0, shape.rows_y, 8):
            ref[pl.ds(shape.row(x, t), 8), :] = got[slot]
            slot += 1
        if rim:
            ref[pl.ds(shape.row(x + 1, -RIM), 4), :] = got[slot, 0:4, :]
            ref[pl.ds(shape.row(x, -4), 4), :] = got[slot, 4:8, :]
            slot += 1


def x_slots(spec, rows_y, rim):
    count = 0
    for c, depth in spec:
        count += depth * (rows_y // 8 + (1 if rim and c != ZZ else 0))
    return count


def x_list(stress, flow, buoyancy, spec, flow_spec, place):
    whole = [(stress.at[c], place(k), c != ZZ) for c, k in entries(spec)]
    if flow is not None:
        whole += [(flow.at[c], place(k), False) for c, k in entries(flow_spec)]
        whole += [(buoyancy, place(k), False) for k in range(2)]
    return whole


def y_list(stress, flow, buoyancy, rows, flow_rows, rim_rows):
    pairs = [(stress.at[c], y) for c, y in rows]
    if flow is not None:
        pairs += [(flow.at[c], y) for c, y in flow_rows]
        pairs += [(buoyancy, y) for y in rim_rows]
    return pairs


def send_y(shape, stress, flow, buoyancy, first, second):
    rows_y = shape.rows_y
    up, down = y_rows(LOW_Y, HIGH_Y, rows_y)
    flow_up, flow_down = y_rows(LOW_FLOW_Y, HIGH_FLOW_Y, rows_y)
    up = y_list(stress, flow, buoyancy, up, flow_up, (rows_y - 1, rows_y - 2))
    down = y_list(stress, flow, buoyancy, down, flow_down, (0, 1))
    odd = lax.axis_index("gy") % 2

    @pl.when(odd == 0)
    def _():
        pack_y(shape, up, first)
        pack_y(shape, down, second)

    @pl.when(odd == 1)
    def _():
        pack_y(shape, down, first)
        pack_y(shape, up, second)


def receive_y(shape, stress, flow, buoyancy, first, second):
    rows_y = shape.rows_y
    below, above = got_y(LOW_Y, HIGH_Y, rows_y)
    flow_below, flow_above = got_y(LOW_FLOW_Y, HIGH_FLOW_Y, rows_y)
    below = y_list(stress, flow, buoyancy, below, flow_below, (-1, -2))
    above = y_list(stress, flow, buoyancy, above, flow_above, (rows_y, rows_y + 1))
    odd = lax.axis_index("gy") % 2

    @pl.when(odd == 0)
    def _():
        unpack_y(shape, above, first)
        unpack_y(shape, below, second)

    @pl.when(odd == 1)
    def _():
        unpack_y(shape, below, first)
        unpack_y(shape, above, second)


def send_x(shape, stress, flow, buoyancy, first, second):
    last = shape.rows_x - 1
    up = x_list(stress, flow, buoyancy, LOW_X, LOW_FLOW_X, lambda k: last - k)
    down = x_list(stress, flow, buoyancy, HIGH_X, HIGH_FLOW_X, lambda k: k)
    odd = lax.axis_index("gx") % 2

    @pl.when(odd == 0)
    def _():
        pack_x(shape, up, None, first)
        pack_x(shape, down, None, second)

    @pl.when(odd == 1)
    def _():
        pack_x(shape, down, None, first)
        pack_x(shape, up, None, second)


def receive_x(shape, stress, flow, buoyancy, first, second):
    below = x_list(stress, flow, buoyancy, LOW_X, LOW_FLOW_X, lambda k: -1 - k)
    above = x_list(stress, flow, buoyancy, HIGH_X, HIGH_FLOW_X, lambda k: shape.rows_x + k)
    odd = lax.axis_index("gx") % 2

    @pl.when(odd == 0)
    def _():
        unpack_x(shape, above, first)
        unpack_x(shape, below, second)

    @pl.when(odd == 1)
    def _():
        unpack_x(shape, below, first)
        unpack_x(shape, above, second)


class Lanes:
    def __init__(self, depth):
        self.depth = depth
        lane = lax.broadcasted_iota(jnp.int32, (8, depth), 1)
        zero = jnp.zeros((8, depth), jnp.float32)
        near = jnp.full((8, depth), near_weight, jnp.float32)
        far = jnp.full((8, depth), far_weight, jnp.float32)
        self.f_up = jnp.where(lane < depth - 1, near, zero)
        self.f_up2 = jnp.where(lane < depth - 2, far, zero)
        self.f_down = jnp.where(lane > 0, far, zero)
        self.b_down = jnp.where(lane > 0, near, zero)
        self.b_down2 = jnp.where(lane > 1, far, zero)
        self.b_up = jnp.where(lane < depth - 1, far, zero)

    def forward(self, f):
        up, up2, down = (pltpu.roll(f, s % self.depth, 1) for s in (-1, -2, 1))
        return (self.f_up * up - near_weight * f) - (self.f_up2 * up2 - self.f_down * down)

    def backward(self, f):
        up, down, down2 = (pltpu.roll(f, s % self.depth, 1) for s in (-1, 1, 2))
        return (near_weight * f - self.b_down * down) - (self.b_up * up - self.b_down2 * down2)


def forward(ref, row, step):
    a, b, c, d = (ref[pl.ds(row + k * step, 8), :] for k in (-1, 0, 1, 2))
    return near_weight * (c - b) - far_weight * (d - a)


def backward(ref, row, step):
    a, b, c, d = (ref[pl.ds(row + k * step, 8), :] for k in (-2, -1, 0, 1))
    return near_weight * (c - b) - far_weight * (d - a)


def tile(ref, row):
    return ref[pl.ds(row, 8), :]


def update_velocity(shape, stress, flow, buoyancy):
    lanes = Lanes(shape.depth)
    sx, sy = shape.pitch, 1
    xx, yy, zz, xy, xz, yz = (stress.at[c] for c in range(6))

    def layer(i, carry):
        base = pl.multiple_of(i * shape.pitch, 8)
        for t in range(0, shape.pitch, 8):
            row = base + t
            scale = time_step * tile(buoyancy, row)
            force_x = forward(xx, row, sx) + backward(xy, row, sy) + lanes.backward(tile(xz, row))
            flow[0, pl.ds(row, 8), :] += scale * force_x
            force_y = backward(xy, row, sx) + forward(yy, row, sy) + lanes.backward(tile(yz, row))
            flow[1, pl.ds(row, 8), :] += scale * force_y
            force_z = backward(xz, row, sx) + backward(yz, row, sy) + lanes.forward(tile(zz, row))
            flow[2, pl.ds(row, 8), :] += scale * force_z
        return carry

    lax.fori_loop(PAD_X - 2, PAD_X + shape.rows_x + 2, layer, 0)


def inject(shape, stress, source_cell, source_moment):
    rows_x, rows_y, depth = shape.rows_x, shape.rows_y, shape.depth
    total_y = rows_y * lax.axis_size("gy")
    start_x = lax.axis_index("gx") * rows_x
    start_y = lax.axis_index("gy") * rows_y
    sub = lax.broadcasted_iota(jnp.int32, (8, depth), 0)
    lane = lax.broadcasted_iota(jnp.int32, (8, depth), 1)
    for s in range(source_cell.shape[0]):
        cell = source_cell[s]
        x = cell // (total_y * depth) - start_x
        y = cell // depth % total_y - start_y
        z = cell % depth

        @pl.when((x >= 0) & (x < rows_x) & (y >= 0) & (y < rows_y))
        def _(x=x, y=y, z=z, s=s):
            row = pl.multiple_of((x + PAD_X) * shape.pitch + RIM + y // 8 * 8, 8)
            here = (sub == y % 8) & (lane == z)
            for c in range(6):
                amount = time_step * source_moment[c, s]
                stress[c, pl.ds(row, 8), :] += jnp.where(here, amount, 0.0)


def update_stress(shape, stress, flow, rock):
    lanes = Lanes(shape.depth)
    sx, sy = shape.pitch, 1
    vx, vy, vz = (flow.at[c] for c in range(3))

    def layer(i, carry):
        for t in range(0, shape.rows_y, 8):
            row = pl.multiple_of((i + PAD_X) * shape.pitch + RIM + t, 8)
            own = pl.multiple_of(i * shape.rows_y + t, 8)
            first = time_step * rock[0, pl.ds(own, 8), :]
            shear = time_step * rock[1, pl.ds(own, 8), :]
            strain_x = backward(vx, row, sx)
            strain_y = backward(vy, row, sy)
            here_z = tile(vz, row)
            strain_z = lanes.backward(here_z)
            volume = first * (strain_x + strain_y + strain_z)
            twice = 2.0 * shear
            xx = tile(stress.at[XX], row) + (volume + twice * strain_x)
            yy = tile(stress.at[YY], row) + (volume + twice * strain_y)
            zz = tile(stress.at[ZZ], row) + (volume + twice * strain_z)
            xy = tile(stress.at[XY], row) + shear * (forward(vx, row, sy) + forward(vy, row, sx))
            xz = tile(stress.at[XZ], row) + shear * (
                lanes.forward(tile(vx, row)) + forward(vz, row, sx)
            )
            yz = tile(stress.at[YZ], row) + shear * (
                lanes.forward(tile(vy, row)) + forward(vz, row, sy)
            )
            pressure = (xx + yy + zz) * (1.0 / 3.0)
            dx, dy, dz = xx - pressure, yy - pressure, zz - pressure
            second = 0.5 * (dx * dx + dy * dy + dz * dz) + xy * xy + xz * xz + yz * yz
            strength = jnp.maximum(
                rock[2, pl.ds(own, 8), :] - pressure * rock[3, pl.ds(own, 8), :], 0.0
            )
            ratio = strength * lax.rsqrt(jnp.maximum(second, shear_floor * shear_floor))
            factor = jnp.where(rock[4, pl.ds(own, 8), :] > 0.5, jnp.minimum(ratio, 1.0), 1.0)
            stress[XX, pl.ds(row, 8), :] = pressure + factor * dx
            stress[YY, pl.ds(row, 8), :] = pressure + factor * dy
            stress[ZZ, pl.ds(row, 8), :] = pressure + factor * dz
            stress[XY, pl.ds(row, 8), :] = factor * xy
            stress[XZ, pl.ds(row, 8), :] = factor * xz
            stress[YZ, pl.ds(row, 8), :] = factor * yz
        return carry

    lax.fori_loop(0, shape.rows_x, layer, 0)


def own_cells(shape, ref):
    lead = ref.shape[:-2]
    view = ref.reshape(*lead, shape.rows_x + 2 * PAD_X + 1, shape.pitch, shape.depth)
    return view.at[
        (slice(None),) * len(lead) + (pl.ds(PAD_X, shape.rows_x), pl.ds(RIM, shape.rows_y))
    ]


def vmem(shape):
    return pltpu.VMEM(shape, jnp.float32)


in_vmem = pl.BlockSpec(memory_space=pltpu.VMEM)
in_smem = pl.BlockSpec(memory_space=pltpu.SMEM)
in_hbm = pl.BlockSpec(memory_space=pl.ANY)


def call(body, ins, in_specs, out_shape, out_specs, name, flops, aliases=None, scratch=()):
    ins = [
        pltpu.with_memory_space_constraint(x, pltpu.VMEM) if s is in_vmem else x
        for x, s in zip(ins, in_specs)
    ]
    return pl.pallas_call(
        body,
        in_specs=in_specs,
        out_shape=out_shape,
        out_specs=out_specs,
        input_output_aliases=aliases or {},
        scratch_shapes=scratch,
        name=name,
        cost_estimate=pl.CostEstimate(flops=flops, bytes_accessed=1000000, transcendentals=0),
        compiler_params=pltpu.CompilerParams(vmem_limit_bytes=16 * 1024 * 1024),
    )(*ins)


def swaps(axis, first, second):
    count = lax.axis_size(axis)
    got = []
    for start, block in ((0, first), (1, second)):
        pairs = []
        for low in range(start, count - 1, 2):
            pairs += [(low, low + 1), (low + 1, low)]
        got.append(lax.ppermute(block, axis, pairs))
    return got


def on_device(
    velocity,
    stress,
    lame_first,
    modulus,
    buoyancy,
    zone,
    eligible,
    cohesion,
    friction,
    source_cell,
    source_moment,
):
    shape = Shape(*zone.shape)
    rows_x, rows_y, depth = zone.shape
    whole_s, whole_v = vmem((6, shape.rows, depth)), vmem((3, shape.rows, depth))
    whole_b = vmem((shape.rows, depth))
    stress_rows = max(len(entries(LOW_Y)), len(entries(HIGH_Y)))
    all_rows = stress_rows + 5 + 2
    stress_slots = max(x_slots(LOW_X, rows_y, True), x_slots(HIGH_X, rows_y, True))
    flow_slots = (max(x_slots(LOW_FLOW_X, rows_y, False), x_slots(HIGH_FLOW_X, rows_y, False))
                  + 2 * (rows_y // 8))

    def buffers(axis, first_round):
        if axis == "y":
            return vmem((all_rows if first_round else stress_rows, rows_x, depth))
        return vmem((stress_slots + (flow_slots if first_round else 0), 8, depth))

    def load(v_in, s_in, b_in, s, v, b, first, second, sems):
        copies = [
            pltpu.make_async_copy(s_in, own_cells(shape, s), sems.at[0]),
            pltpu.make_async_copy(v_in, own_cells(shape, v), sems.at[1]),
            pltpu.make_async_copy(b_in, own_cells(shape, b), sems.at[2]),
        ]
        for c in copies:
            c.start()
        for c in copies:
            c.wait()
        send_y(shape, s, v, b, first, second)

    s, v, b, first, second = call(
        load,
        [velocity, stress, buoyancy],
        [in_hbm] * 3,
        [whole_s, whole_v, whole_b, buffers("y", True), buffers("y", True)],
        [in_vmem] * 5,
        "load",
        1000000,
        scratch=[pltpu.SemaphoreType.DMA((3,))],
    )

    def prepare(lame_in, shear_in, zone_in, eligible_in, cohesion, friction, rock, zones, able, sems):
        flat = rock.reshape(5, rows_x, rows_y, depth)
        copies = [
            pltpu.make_async_copy(zone_in, zones, sems.at[0]),
            pltpu.make_async_copy(eligible_in, able, sems.at[1]),
            pltpu.make_async_copy(lame_in, flat.at[0], sems.at[2]),
            pltpu.make_async_copy(shear_in, flat.at[1], sems.at[3]),
        ]
        for c in copies:
            c.start()
        copies[0].wait()
        copies[1].wait()

        def layer(i, carry):
            for t in range(0, rows_y, 8):
                own = pl.multiple_of(i * rows_y + t, 8)
                which = zones[i, pl.ds(t, 8), :]
                hold = jnp.full((8, depth), cohesion[0], jnp.float32)
                rub = jnp.full((8, depth), friction[0], jnp.float32)
                for k in range(1, cohesion.shape[0]):
                    hit = which == k
                    hold = jnp.where(hit, cohesion[k], hold)
                    rub = jnp.where(hit, friction[k], rub)
                rock[2, pl.ds(own, 8), :] = hold * jnp.sqrt(1.0 - rub * rub)
                rock[3, pl.ds(own, 8), :] = rub
                rock[4, pl.ds(own, 8), :] = jnp.where(able[i, pl.ds(t, 8), :] == 1, 1.0, 0.0)
            return carry

        lax.fori_loop(0, rows_x, layer, 0)
        copies[2].wait()
        copies[3].wait()

    rock = call(
        prepare,
        [lame_first, modulus, zone, eligible, cohesion, friction],
        [in_hbm] * 4 + [in_smem] * 2,
        vmem((5, rows_x * rows_y, depth)),
        in_vmem,
        "prepare",
        1000000,
        scratch=[
            pltpu.VMEM((rows_x, rows_y, depth), jnp.int32),
            pltpu.VMEM((rows_x, rows_y, depth), jnp.int32),
            pltpu.SemaphoreType.DMA((4,)),
        ],
    )

    for step in range(STEPS):
        begin, end = step == 0, step == STEPS - 1
        first, second = swaps("gy", first, second)

        if begin:

            def turn(s_in, v_in, b_in, got_a, got_b, s, v, b, out_a, out_b):
                receive_y(shape, s, v, b, got_a, got_b)
                send_x(shape, s, v, b, out_a, out_b)

            s, v, b, first, second = call(
                turn,
                [s, v, b, first, second],
                [in_vmem] * 5,
                [whole_s, whole_v, whole_b, buffers("x", True), buffers("x", True)],
                [in_vmem] * 5,
                "turn_first",
                1000000,
                aliases={0: 0, 1: 1, 2: 2},
            )
        else:

            def turn(s_in, got_a, got_b, s, out_a, out_b):
                receive_y(shape, s, None, None, got_a, got_b)
                send_x(shape, s, None, None, out_a, out_b)

            s, first, second = call(
                turn,
                [s, first, second],
                [in_vmem] * 3,
                [whole_s, buffers("x", False), buffers("x", False)],
                [in_vmem] * 3,
                "turn",
                1000000,
                aliases={0: 0},
            )
        first, second = swaps("gx", first, second)

        if not end:

            def advance(s_in, v_in, b_in, rock, got_a, got_b, cell, moment, s, v, b, out_a, out_b):
                fields = (s, v, b) if begin else (s, None, None)
                receive_x(shape, *fields, got_a, got_b)
                update_velocity(shape, s, v, b)
                inject(shape, s, cell, moment)
                update_stress(shape, s, v, rock)
                send_y(shape, s, None, None, out_a, out_b)

            s, v, b, first, second = call(
                advance,
                [s, v, b, rock, first, second, source_cell, source_moment],
                [in_vmem] * 6 + [in_smem] * 2,
                [whole_s, whole_v, whole_b, buffers("y", False), buffers("y", False)],
                [in_vmem] * 5,
                "advance",
                10000000,
                aliases={0: 0, 1: 1, 2: 2},
            )
        else:

            def finish(s_in, v_in, b, rock, got_a, got_b, cell, moment, s, v, v_out, s_out, sems):
                receive_x(shape, s, None, None, got_a, got_b)
                update_velocity(shape, s, v, b)
                out_v = pltpu.make_async_copy(own_cells(shape, v), v_out, sems.at[0])
                out_v.start()
                inject(shape, s, cell, moment)
                update_stress(shape, s, v, rock)
                out_s = pltpu.make_async_copy(own_cells(shape, s), s_out, sems.at[1])
                out_s.start()
                out_v.wait()
                out_s.wait()

            _, _, velocity, stress = call(
                finish,
                [s, v, b, rock, first, second, source_cell, source_moment],
                [in_vmem] * 6 + [in_smem] * 2,
                [
                    whole_s,
                    whole_v,
                    jax.ShapeDtypeStruct(velocity.shape, jnp.float32),
                    jax.ShapeDtypeStruct(stress.shape, jnp.float32),
                ],
                [in_vmem, in_vmem, in_hbm, in_hbm],
                "finish",
                10000000,
                aliases={0: 0, 1: 1},
                scratch=[pltpu.SemaphoreType.DMA((2,))],
            )
    return (velocity, stress)


def solution(mesh):
    placed = (
        P(None, "gx", "gy", None),
        P(None, "gx", "gy", None),
        P("gx", "gy", None),
        P("gx", "gy", None),
        P("gx", "gy", None),
        P("gx", "gy", None),
        P("gx", "gy", None),
        P(),
        P(),
        P(),
        P(),
    )
    return jax.shard_map(
        on_device,
        mesh=mesh,
        in_specs=placed,
        out_specs=(P(None, "gx", "gy", None), P(None, "gx", "gy", None)),
        check_vma=False,
    )
```

time: 109 us -> 56.2 us (0.52)
  the two profiles are of different devices: /device:TPU:1 before, /device:TPU:12 now
where the time goes in v1:
time: 56.2 us; the launch traced here: 55.9 us
  waiting for transfers between devices  21.1 us (38%)
  Pallas kernels  19 us (34%)
  starting transfers between devices  11.9 us (21%)
  local copies, waits for them, and re-layouts  3.07 us (5%)
  between operations  0.84 us (1%)
    ppermute x8, waiting for transfers between devices, swaps(): got.append(lax.ppermute(block, axis, pairs))  21.1 us
    pallas_call x6, Pallas kernels, call(): pl.pallas_call(body, in_specs=in_specs, out_shape=out_shape, out_specs=ou...  19 us
    ppermute x8, starting transfers between devices, swaps(): got.append(lax.ppermute(block, axis, pairs))  11.9 us
    unnamed x22, local copies, waits for them, and re-layouts  3.07 us
  transfers between devices with their start and end apart: 8, of which 6 were waited for; matrix products, arithmetic and copies ran while one was open for 0% of the time, Pallas kernels for 3%

profile of v1, /device:TPU:12, one launch (start us, length us, event | category | flops | bytes accessed | tf_op | source)
XLA Modules:
  0.0 55.9 jit_solution(1009472155033758802)
XLA Ops:
  0.6 0.0 copy-start
  0.6 1.1 %copy-done = f32[6,32,8,128]{3,2,1,0:T(8,128)S(1)} copy-done((f32[6,32,8,128]{3,2,1,0:T(8,128)S(1)}, f32[6,32,8,128]{3,2,1,0:T(8,128)}, u32[]{:S(2)}) %copy-start) | copy-done | bytes 786456
  1.8 0.0 copy-start.1
  1.8 1.0 %copy-done.1 = f32[3,32,8,128]{3,2,1,0:T(8,128)S(1)} copy-done((f32[3,32,8,128]{3,2,1,0:T(8,128)S(1)}, f32[3,32,8,128]{3,2,1,0:T(8,128)}, u32[]{:S(2)}) %copy-start.1) | copy-done | bytes 393240
  2.8 0.0 copy-start.2
  2.8 0.9 %copy-done.2 = f32[32,8,128]{2,1,0:T(8,128)S(1)} copy-done((f32[32,8,128]{2,1,0:T(8,128)S(1)}, f32[32,8,128]{2,1,0:T(8,128)}, u32[]{:S(2)}) %copy-start.2) | copy-done | bytes 131096
  3.7 0.3 load.1
  4.0 0.1 collective-permute-start
  4.1 2.4 %collective-permute-start.1 = (f32[22,32,128]{2,1,0:T(8,128)S(1)}, f32[22,32,128]{2,1,0:T(8,128)S(1)}, u32[]{:S(2)}, u32[]{:S(2)}) collective-permute-start(f32[22,32,128]{2,1,0:T(8,128)S(1)} %get-tuple-element.26), channel_id=1, source_target_pairs={{1,2},{2,1},{3,4},{4,3},{5,6},{6,5},{9,10},{10,9},{11,12},{12,11},... | collective-permute-start | bytes 1081352 | tf_op jit(solution)/shard_map/ppermute | solution.py:357
  6.6 0.0 collective-permute-done.got_a
  6.6 6.3 %collective-permute-done.1.got_b = f32[22,32,128]{2,1,0:T(8,128)S(1)} collective-permute-done((f32[22,32,128]{2,1,0:T(8,128)S(1)}, f32[22,32,128]{2,1,0:T(8,128)S(1)}, u32[]{:S(2)}, u32[]{:S(2)}) %collective-permute-start.1) | collective-permute-done | bytes 360480 | tf_op jit(solution)/shard_map/ppermute | solution.py:357
  12.8 0.0 copy-start.3
  12.8 0.0 copy-start.4
  12.8 0.0 copy-start.5
  12.9 0.0 copy-start.6
  12.9 0.0 copy-start.9
  12.9 0.0 copy-start.10
  12.9 0.0 copy-start.7
  12.9 0.0 copy-start.8
  12.9 0.3 turn_first.1
  13.2 1.6 %collective-permute-start.2 = (f32[35,8,128]{2,1,0:T(8,128)S(1)}, f32[35,8,128]{2,1,0:T(8,128)S(1)}, u32[]{:S(2)}, u32[]{:S(2)}) collective-permute-start(f32[35,8,128]{2,1,0:T(8,128)S(1)} %get-tuple-element.30), channel_id=1, source_target_pairs={{0,8},{8,0},{16,24},{24,16},{1,9},{9,1},{17,25},{25,17},{2,10},{10... | collective-permute-start | bytes 430088 | tf_op jit(solution)/shard_map/ppermute | solution.py:357
  14.8 2.4 %collective-permute-start.3 = (f32[35,8,128]{2,1,0:T(8,128)S(1)}, f32[35,8,128]{2,1,0:T(8,128)S(1)}, u32[]{:S(2)}, u32[]{:S(2)}) collective-permute-start(f32[35,8,128]{2,1,0:T(8,128)S(1)} %get-tuple-element.31), channel_id=1, source_target_pairs={{8,16},{16,8},{9,17},{17,9},{10,18},{18,10},{11,19},{19,11},{12,20... | collective-permute-start | bytes 430088 | tf_op jit(solution)/shard_map/ppermute | solution.py:357
  17.2 0.0 copy-done.3
  17.2 0.0 copy-done.4
  17.2 0.0 copy-done.5
  17.2 0.0 copy-done.6
  17.2 0.0 copy-done.9
  17.2 0.0 copy-done.10
  17.2 1.9 %prepare.1.rock = f32[5,256,128]{2,1,0:T(8,128)S(1)} custom-call(f32[32,8,128]{2,1,0:T(8,128)S(1)} %copy-done.3, f32[32,8,128]{2,1,0:T(8,128)S(1)} %copy-done.4, s32[32,8,128]{2,1,0:T(8,128)S(1)} %copy-done.5, s32[32,8,128]{2,1,0:T(8,128)S(1)} %copy-done.6, f32[8]{0:T(128)S(1)} %copy-done.9, f32[8]{0:T(128)S(1)} %copy-done.10), custom_call_target="tpu_custom_call" | custom-call | flops 1000000 | bytes 1000000 | tf_op jit(solution)/shard_map/prepare/pallas_call | solution.py:337
  19.1 0.3 collective-permute-done.2.got_a
  19.5 4.0 %collective-permute-done.3.got_b = f32[35,8,128]{2,1,0:T(8,128)S(1)} collective-permute-done((f32[35,8,128]{2,1,0:T(8,128)S(1)}, f32[35,8,128]{2,1,0:T(8,128)S(1)}, u32[]{:S(2)}, u32[]{:S(2)}) %collective-permute-start.3) | collective-permute-done | bytes 143392 | tf_op jit(solution)/shard_map/ppermute | solution.py:357
  23.5 0.0 copy-done.7
  23.5 0.0 copy-done.8
  23.5 7.7 %advance.1 = (f32[6,656,128]{2,1,0:T(8,128)S(1)}, f32[3,656,128]{2,1,0:T(8,128)S(1)}, f32[656,128]{1,0:T(8,128)S(1)}, f32[15,32,128]{2,1,0:T(8,128)S(1)}, f32[15,32,128]{2,1,0:T(8,128)S(1)}) custom-call(f32[6,656,128]{2,1,0:T(8,128)S(1)} %get-tuple-element.27.s_in, ...), custom_call_target="tpu_custom_call", output_to_operand_aliasing={{0}: (0, {}), {1}: (1, {}), {2}: (2, {})} | custom-call | flops 10000000 | bytes 1000000 | tf_op jit(solution)/shard_map/advance/pallas_call | solution.py:337
  31.2 0.1 collective-permute-start.4
  31.3 1.9 %collective-permute-start.5 = (f32[15,32,128]{2,1,0:T(8,128)S(1)}, f32[15,32,128]{2,1,0:T(8,128)S(1)}, u32[]{:S(2)}, u32[]{:S(2)}) collective-permute-start(f32[15,32,128]{2,1,0:T(8,128)S(1)} %get-tuple-element.34), channel_id=1, source_target_pairs={{1,2},{2,1},{3,4},{4,3},{5,6},{6,5},{9,10},{10,9},{11,12},{12,11},... | collective-permute-start | bytes 737288 | tf_op jit(solution)/shard_map/ppermute | solution.py:357
  33.2 0.0 collective-permute-done.4.got_a
  33.2 5.6 %collective-permute-done.5.got_b = f32[15,32,128]{2,1,0:T(8,128)S(1)} collective-permute-done((f32[15,32,128]{2,1,0:T(8,128)S(1)}, f32[15,32,128]{2,1,0:T(8,128)S(1)}, u32[]{:S(2)}, u32[]{:S(2)}) %collective-permute-start.5) | collective-permute-done | bytes 245792 | tf_op jit(solution)/shard_map/ppermute | solution.py:357
  38.8 0.2 turn.1
  39.0 0.1 collective-permute-start.6
  39.1 3.4 %collective-permute-start.7 = (f32[28,8,128]{2,1,0:T(8,128)S(1)}, f32[28,8,128]{2,1,0:T(8,128)S(1)}, u32[]{:S(2)}, u32[]{:S(2)}) collective-permute-start(f32[28,8,128]{2,1,0:T(8,128)S(1)} %get-tuple-element.39), channel_id=1, source_target_pairs={{8,16},{16,8},{9,17},{17,9},{10,18},{18,10},{11,19},{19,11},{12,20... | collective-permute-start | bytes 344072 | tf_op jit(solution)/shard_map/ppermute | solution.py:357
  42.5 2.1 %collective-permute-done.6.got_a = f32[28,8,128]{2,1,0:T(8,128)S(1)} collective-permute-done((f32[28,8,128]{2,1,0:T(8,128)S(1)}, f32[28,8,128]{2,1,0:T(8,128)S(1)}, u32[]{:S(2)}, u32[]{:S(2)}) %collective-permute-start.6) | collective-permute-done | bytes 114720 | tf_op jit(solution)/shard_map/ppermute | solution.py:357
  44.6 2.8 %collective-permute-done.7.got_b = f32[28,8,128]{2,1,0:T(8,128)S(1)} collective-permute-done((f32[28,8,128]{2,1,0:T(8,128)S(1)}, f32[28,8,128]{2,1,0:T(8,128)S(1)}, u32[]{:S(2)}, u32[]{:S(2)}) %collective-permute-start.7) | collective-permute-done | bytes 114720 | tf_op jit(solution)/shard_map/ppermute | solution.py:357
  47.4 8.5 %finish.1 = (f32[6,656,128]{2,1,0:T(8,128)S(1)}, f32[3,656,128]{2,1,0:T(8,128)S(1)}, f32[3,32,8,128]{3,2,1,0:T(8,128)}, f32[6,32,8,128]{3,2,1,0:T(8,128)}) custom-call(f32[6,656,128]{2,1,0:T(8,128)S(1)} %get-tuple-element.35.s_in, f32[3,656,128]{2,1,0:T(8,128)S(1)} %get-tuple-element.36.v_in, ...), custom_call_target="tpu_custom_call", output_to_operand_aliasing={{0}: (0, {}), {1}: (1, {})} | custom-call | flops 10000000 | bytes 1000000 | tf_op jit(solution)/shard_map/finish/pallas_call | solution.py:337
Async XLA Ops:
  0.6 1.1 %copy-start = (f32[6,32,8,128]{3,2,1,0:T(8,128)S(1)}, f32[6,32,8,128]{3,2,1,0:T(8,128)}, u32[]{:S(2)}) copy-start(f32[6,32,8,128]{3,2,1,0:T(8,128)} %s_in.1) | copy-start | bytes 2359300
  1.8 1.0 %copy-start.1 = (f32[3,32,8,128]{3,2,1,0:T(8,128)S(1)}, f32[3,32,8,128]{3,2,1,0:T(8,128)}, u32[]{:S(2)}) copy-start(f32[3,32,8,128]{3,2,1,0:T(8,128)} %v_in.1) | copy-start | bytes 1179652
  2.8 0.9 %copy-start.2 = (f32[32,8,128]{2,1,0:T(8,128)S(1)}, f32[32,8,128]{2,1,0:T(8,128)}, u32[]{:S(2)}) copy-start(f32[32,8,128]{2,1,0:T(8,128)} %b_in.1) | copy-start | bytes 393220
  4.0 2.5 %collective-permute-start = (f32[22,32,128]{2,1,0:T(8,128)S(1)}, f32[22,32,128]{2,1,0:T(8,128)S(1)}, u32[]{:S(2)}, u32[]{:S(2)}) collective-permute-start(f32[22,32,128]{2,1,0:T(8,128)S(1)} %get-tuple-element.25), channel_id=1, source_target_pairs={{0,1},{1,0},{2,3},{3,2},{4,5},{5,4},{6,7},{7,6},{8,9},{9,8},{10,11... | collective-permute-start | bytes 1081352 | tf_op jit(solution)/shard_map/ppermute | solution.py:357
  4.1 8.7 %collective-permute-start.1 = (f32[22,32,128]{2,1,0:T(8,128)S(1)}, f32[22,32,128]{2,1,0:T(8,128)S(1)}, u32[]{:S(2)}, u32[]{:S(2)}) collective-permute-start(f32[22,32,128]{2,1,0:T(8,128)S(1)} %get-tuple-element.26), channel_id=1, source_target_pairs={{1,2},{2,1},{3,4},{4,3},{5,6},{6,5},{9,10},{10,9},{11,12},{12,11},... | collective-permute-start | bytes 1081352 | tf_op jit(solution)/shard_map/ppermute | solution.py:357
  12.8 4.3 %copy-start.3 = (f32[32,8,128]{2,1,0:T(8,128)S(1)}, f32[32,8,128]{2,1,0:T(8,128)}, u32[]{:S(2)}) copy-start(f32[32,8,128]{2,1,0:T(8,128)} %lame_in.1) | copy-start | bytes 393220
  12.8 4.4 %copy-start.4 = (f32[32,8,128]{2,1,0:T(8,128)S(1)}, f32[32,8,128]{2,1,0:T(8,128)}, u32[]{:S(2)}) copy-start(f32[32,8,128]{2,1,0:T(8,128)} %shear_in.1) | copy-start | bytes 393220
  12.8 4.4 %copy-start.5 = (s32[32,8,128]{2,1,0:T(8,128)S(1)}, s32[32,8,128]{2,1,0:T(8,128)}, u32[]{:S(2)}) copy-start(s32[32,8,128]{2,1,0:T(8,128)} %zone_in.1) | copy-start | bytes 393220
  12.9 4.4 %copy-start.6 = (s32[32,8,128]{2,1,0:T(8,128)S(1)}, s32[32,8,128]{2,1,0:T(8,128)}, u32[]{:S(2)}) copy-start(s32[32,8,128]{2,1,0:T(8,128)} %eligible_in.1) | copy-start | bytes 393220
  12.9 4.4 %copy-start.9 = (f32[8]{0:T(128)S(1)}, f32[8]{0:T(128)}, u32[]{:S(2)}) copy-start(f32[8]{0:T(128)} %cohesion.1) | copy-start | bytes 100
  12.9 4.4 %copy-start.10 = (f32[8]{0:T(128)S(1)}, f32[8]{0:T(128)}, u32[]{:S(2)}) copy-start(f32[8]{0:T(128)} %friction.1) | copy-start | bytes 100
  12.9 10.6 %copy-start.7 = (f32[6,16]{1,0:T(8,128)S(1)}, f32[6,16]{1,0:T(8,128)}, u32[]{:S(2)}) copy-start(f32[6,16]{1,0:T(8,128)} %moment.3) | copy-start | bytes 1156
  12.9 10.6 %copy-start.8 = (s32[16]{0:T(128)S(1)}, s32[16]{0:T(128)}, u32[]{:S(2)}) copy-start(s32[16]{0:T(128)} %cell.3) | copy-start | bytes 196
  13.2 6.2 %collective-permute-start.2 = (f32[35,8,128]{2,1,0:T(8,128)S(1)}, f32[35,8,128]{2,1,0:T(8,128)S(1)}, u32[]{:S(2)}, u32[]{:S(2)}) collective-permute-start(f32[35,8,128]{2,1,0:T(8,128)S(1)} %get-tuple-element.30), channel_id=1, source_target_pairs={{0,8},{8,0},{16,24},{24,16},{1,9},{9,1},{17,25},{25,17},{2,10},{10... | collective-permute-start | bytes 430088 | tf_op jit(solution)/shard_map/ppermute | solution.py:357
  14.8 8.7 %collective-permute-start.3 = (f32[35,8,128]{2,1,0:T(8,128)S(1)}, f32[35,8,128]{2,1,0:T(8,128)S(1)}, u32[]{:S(2)}, u32[]{:S(2)}) collective-permute-start(f32[35,8,128]{2,1,0:T(8,128)S(1)} %get-tuple-element.31), channel_id=1, source_target_pairs={{8,16},{16,8},{9,17},{17,9},{10,18},{18,10},{11,19},{19,11},{12,20... | collective-permute-start | bytes 430088 | tf_op jit(solution)/shard_map/ppermute | solution.py:357
  31.2 2.0 %collective-permute-start.4 = (f32[15,32,128]{2,1,0:T(8,128)S(1)}, f32[15,32,128]{2,1,0:T(8,128)S(1)}, u32[]{:S(2)}, u32[]{:S(2)}) collective-permute-start(f32[15,32,128]{2,1,0:T(8,128)S(1)} %get-tuple-element.33), channel_id=1, source_target_pairs={{0,1},{1,0},{2,3},{3,2},{4,5},{5,4},{6,7},{7,6},{8,9},{9,8},{10,11... | collective-permute-start | bytes 737288 | tf_op jit(solution)/shard_map/ppermute | solution.py:357
  31.3 7.5 %collective-permute-start.5 = (f32[15,32,128]{2,1,0:T(8,128)S(1)}, f32[15,32,128]{2,1,0:T(8,128)S(1)}, u32[]{:S(2)}, u32[]{:S(2)}) collective-permute-start(f32[15,32,128]{2,1,0:T(8,128)S(1)} %get-tuple-element.34), channel_id=1, source_target_pairs={{1,2},{2,1},{3,4},{4,3},{5,6},{6,5},{9,10},{10,9},{11,12},{12,11},... | collective-permute-start | bytes 737288 | tf_op jit(solution)/shard_map/ppermute | solution.py:357
  39.0 5.6 %collective-permute-start.6 = (f32[28,8,128]{2,1,0:T(8,128)S(1)}, f32[28,8,128]{2,1,0:T(8,128)S(1)}, u32[]{:S(2)}, u32[]{:S(2)}) collective-permute-start(f32[28,8,128]{2,1,0:T(8,128)S(1)} %get-tuple-element.38), channel_id=1, source_target_pairs={{0,8},{8,0},{16,24},{24,16},{1,9},{9,1},{17,25},{25,17},{2,10},{10... | collective-permute-start | bytes 344072 | tf_op jit(solution)/shard_map/ppermute | solution.py:357
  39.1 8.3 %collective-permute-start.7 = (f32[28,8,128]{2,1,0:T(8,128)S(1)}, f32[28,8,128]{2,1,0:T(8,128)S(1)}, u32[]{:S(2)}, u32[]{:S(2)}) collective-permute-start(f32[28,8,128]{2,1,0:T(8,128)S(1)} %get-tuple-element.39), channel_id=1, source_target_pairs={{8,16},{16,8},{9,17},{17,9},{10,18},{18,10},{11,19},{19,11},{12,20... | collective-permute-start | bytes 344072 | tf_op jit(solution)/shard_map/ppermute | solution.py:357

commit v2 on v1

--- a/solution.py
+++ b/solution.py
@@ -223,28 +223,39 @@
     return ref[pl.ds(row, 8), :]
 
 
-def update_velocity(shape, stress, flow, buoyancy):
-    lanes = Lanes(shape.depth)
+def push_velocity(shape, lanes, stress, flow, buoyancy, row, along="xyz"):
     sx, sy = shape.pitch, 1
     xx, yy, zz, xy, xz, yz = (stress.at[c] for c in range(6))
-
-    def layer(i, carry):
-        base = pl.multiple_of(i * shape.pitch, 8)
-        for t in range(0, shape.pitch, 8):
-            row = base + t
-            scale = time_step * tile(buoyancy, row)
-            force_x = forward(xx, row, sx) + backward(xy, row, sy) + lanes.backward(tile(xz, row))
-            flow[0, pl.ds(row, 8), :] += scale * force_x
-            force_y = backward(xy, row, sx) + forward(yy, row, sy) + lanes.backward(tile(yz, row))
-            flow[1, pl.ds(row, 8), :] += scale * force_y
-            force_z = backward(xz, row, sx) + backward(yz, row, sy) + lanes.forward(tile(zz, row))
-            flow[2, pl.ds(row, 8), :] += scale * force_z
+    parts = {
+        "x": lambda: (forward(xx, row, sx), backward(xy, row, sx), backward(xz, row, sx)),
+        "y": lambda: (backward(xy, row, sy), forward(yy, row, sy), backward(yz, row, sy)),
+        "z": lambda: (
+            lanes.backward(tile(xz, row)),
+            lanes.backward(tile(yz, row)),
+            lanes.forward(tile(zz, row)),
+        ),
+    }
+    force = parts[along[0]]()
+    for axis in along[1:]:
+        force = [f + g for f, g in zip(force, parts[axis]())]
+    scale = time_step * tile(buoyancy, row)
+    for c in range(3):
+        flow[c, pl.ds(row, 8), :] += scale * force[c]
+
+
+def layers(first, stop, body, unroll):
+    def run(x, carry):
+        body(x)
         return carry
 
-    lax.fori_loop(PAD_X - 2, PAD_X + shape.rows_x + 2, layer, 0)
-
-
-def inject(shape, stress, source_cell, source_moment):
+    lax.fori_loop(first, stop, run, 0, unroll=unroll)
+
+
+def aligned(shape, x, y):
+    return pl.multiple_of((x + PAD_X) * shape.pitch + RIM + y, 8)
+
+
+def inject(shape, stress, source_cell, source_moment, wanted):
     rows_x, rows_y, depth = shape.rows_x, shape.rows_y, shape.depth
     total_y = rows_y * lax.axis_size("gy")
     start_x = lax.axis_index("gx") * rows_x
@@ -253,71 +264,77 @@
     lane = lax.broadcasted_iota(jnp.int32, (8, depth), 1)
     for s in range(source_cell.shape[0]):
         cell = source_cell[s]
-        x = cell // (total_y * depth) - start_x
-        y = cell // depth % total_y - start_y
-        z = cell % depth
-
-        @pl.when((x >= 0) & (x < rows_x) & (y >= 0) & (y < rows_y))
+        line = lax.div(cell, depth)
+        x = lax.div(line, total_y) - start_x
+        y = lax.rem(line, total_y) - start_y
+        z = lax.rem(cell, depth)
+
+        @pl.when(wanted(x) & (y >= 0) & (y < rows_y))
         def _(x=x, y=y, z=z, s=s):
-            row = pl.multiple_of((x + PAD_X) * shape.pitch + RIM + y // 8 * 8, 8)
-            here = (sub == y % 8) & (lane == z)
+            band = lax.div(y, 8) * 8
+            row = aligned(shape, x, band)
+            here = (sub == y - band) & (lane == z)
             for c in range(6):
                 amount = time_step * source_moment[c, s]
                 stress[c, pl.ds(row, 8), :] += jnp.where(here, amount, 0.0)
 
 
-def update_stress(shape, stress, flow, rock):
-    lanes = Lanes(shape.depth)
+def push_stress(shape, lanes, stress, flow, rock, x):
     sx, sy = shape.pitch, 1
     vx, vy, vz = (flow.at[c] for c in range(3))
 
-    def layer(i, carry):
-        for t in range(0, shape.rows_y, 8):
-            row = pl.multiple_of((i + PAD_X) * shape.pitch + RIM + t, 8)
-            own = pl.multiple_of(i * shape.rows_y + t, 8)
-            first = time_step * rock[0, pl.ds(own, 8), :]
-            shear = time_step * rock[1, pl.ds(own, 8), :]
-            strain_x = backward(vx, row, sx)
-            strain_y = backward(vy, row, sy)
-            here_z = tile(vz, row)
-            strain_z = lanes.backward(here_z)
-            volume = first * (strain_x + strain_y + strain_z)
-            twice = 2.0 * shear
-            xx = tile(stress.at[XX], row) + (volume + twice * strain_x)
-            yy = tile(stress.at[YY], row) + (volume + twice * strain_y)
-            zz = tile(stress.at[ZZ], row) + (volume + twice * strain_z)
-            xy = tile(stress.at[XY], row) + shear * (forward(vx, row, sy) + forward(vy, row, sx))
-            xz = tile(stress.at[XZ], row) + shear * (
-                lanes.forward(tile(vx, row)) + forward(vz, row, sx)
-            )
-            yz = tile(stress.at[YZ], row) + shear * (
-                lanes.forward(tile(vy, row)) + forward(vz, row, sy)
-            )
-            pressure = (xx + yy + zz) * (1.0 / 3.0)
-            dx, dy, dz = xx - pressure, yy - pressure, zz - pressure
-            second = 0.5 * (dx * dx + dy * dy + dz * dz) + xy * xy + xz * xz + yz * yz
-            strength = jnp.maximum(
-                rock[2, pl.ds(own, 8), :] - pressure * rock[3, pl.ds(own, 8), :], 0.0
-            )
-            ratio = strength * lax.rsqrt(jnp.maximum(second, shear_floor * shear_floor))
-            factor = jnp.where(rock[4, pl.ds(own, 8), :] > 0.5, jnp.minimum(ratio, 1.0), 1.0)
-            stress[XX, pl.ds(row, 8), :] = pressure + factor * dx
-            stress[YY, pl.ds(row, 8), :] = pressure + factor * dy
-            stress[ZZ, pl.ds(row, 8), :] = pressure + factor * dz
-            stress[XY, pl.ds(row, 8), :] = factor * xy
-            stress[XZ, pl.ds(row, 8), :] = factor * xz
-            stress[YZ, pl.ds(row, 8), :] = factor * yz
-        return carry
-
-    lax.fori_loop(0, shape.rows_x, layer, 0)
-
-
-def own_cells(shape, ref):
+    for t in range(0, shape.rows_y, 8):
+        row = aligned(shape, x, t)
+        own = pl.multiple_of(x * shape.rows_y + t, 8)
+        first = time_step * rock[0, pl.ds(own, 8), :]
+        shear = time_step * rock[1, pl.ds(own, 8), :]
+        strain_x = backward(vx, row, sx)
+        strain_y = backward(vy, row, sy)
+        here_z = tile(vz, row)
+        strain_z = lanes.backward(here_z)
+        volume = first * (strain_x + strain_y + strain_z)
+        twice = 2.0 * shear
+        xx = tile(stress.at[XX], row) + (volume + twice * strain_x)
+        yy = tile(stress.at[YY], row) + (volume + twice * strain_y)
+        zz = tile(stress.at[ZZ], row) + (volume + twice * strain_z)
+        xy = tile(stress.at[XY], row) + shear * (forward(vx, row, sy) + forward(vy, row, sx))
+        xz = tile(stress.at[XZ], row) + shear * (
+            lanes.forward(tile(vx, row)) + forward(vz, row, sx)
+        )
+        yz = tile(stress.at[YZ], row) + shear * (
+            lanes.forward(tile(vy, row)) + forward(vz, row, sy)
+        )
+        pressure = (xx + yy + zz) * (1.0 / 3.0)
+        dx, dy, dz = xx - pressure, yy - pressure, zz - pressure
+        second = 0.5 * (dx * dx + dy * dy + dz * dz) + xy * xy + xz * xz + yz * yz
+        strength = jnp.maximum(
+            rock[2, pl.ds(own, 8), :] - pressure * rock[3, pl.ds(own, 8), :], 0.0
+        )
+        ratio = strength * lax.rsqrt(jnp.maximum(second, shear_floor * shear_floor))
+        factor = jnp.where(rock[4, pl.ds(own, 8), :] > 0.5, jnp.minimum(ratio, 1.0), 1.0)
+        stress[XX, pl.ds(row, 8), :] = pressure + factor * dx
+        stress[YY, pl.ds(row, 8), :] = pressure + factor * dy
+        stress[ZZ, pl.ds(row, 8), :] = pressure + factor * dz
+        stress[XY, pl.ds(row, 8), :] = factor * xy
+        stress[XZ, pl.ds(row, 8), :] = factor * xz
+        stress[YZ, pl.ds(row, 8), :] = factor * yz
+
+
+def own_cells(shape, ref, first=0, count=None):
     lead = ref.shape[:-2]
     view = ref.reshape(*lead, shape.rows_x + 2 * PAD_X + 1, shape.pitch, shape.depth)
+    count = shape.rows_x - first if count is None else count
     return view.at[
-        (slice(None),) * len(lead) + (pl.ds(PAD_X, shape.rows_x), pl.ds(RIM, shape.rows_y))
+        (slice(None),) * len(lead) + (pl.ds(PAD_X + first, count), pl.ds(RIM, shape.rows_y))
     ]
+
+
+def run_copies(pairs, sems):
+    copies = [pltpu.make_async_copy(a, b, sems.at[i]) for i, (a, b) in enumerate(pairs)]
+    for c in copies:
+        c.start()
+    for c in copies:
+        c.wait()
 
 
 def vmem(shape):
@@ -326,12 +343,13 @@
 
 in_vmem = pl.BlockSpec(memory_space=pltpu.VMEM)
 in_smem = pl.BlockSpec(memory_space=pltpu.SMEM)
-in_hbm = pl.BlockSpec(memory_space=pl.ANY)
+in_hbm = pl.BlockSpec(memory_space=pltpu.HBM)
 
 
 def call(body, ins, in_specs, out_shape, out_specs, name, flops, aliases=None, scratch=()):
+    space = {id(in_vmem): pltpu.VMEM, id(in_hbm): pltpu.HBM}
     ins = [
-        pltpu.with_memory_space_constraint(x, pltpu.VMEM) if s is in_vmem else x
+        pltpu.with_memory_space_constraint(x, space[id(s)]) if id(s) in space else x
         for x, s in zip(ins, in_specs)
     ]
     return pl.pallas_call(
@@ -386,16 +404,13 @@
             return vmem((all_rows if first_round else stress_rows, rows_x, depth))
         return vmem((stress_slots + (flow_slots if first_round else 0), 8, depth))
 
+    inner = (2, rows_x - 2)
+    deep = (4, rows_x - 4)
+    bands = range(0, rows_y, 8)
+
     def load(v_in, s_in, b_in, s, v, b, first, second, sems):
-        copies = [
-            pltpu.make_async_copy(s_in, own_cells(shape, s), sems.at[0]),
-            pltpu.make_async_copy(v_in, own_cells(shape, v), sems.at[1]),
-            pltpu.make_async_copy(b_in, own_cells(shape, b), sems.at[2]),
-        ]
-        for c in copies:
-            c.start()
-        for c in copies:
-            c.wait()
+        own = [own_cells(shape, ref) for ref in (s, v, b)]
+        run_copies(list(zip((s_in, v_in, b_in), own)), sems)
         send_y(shape, s, v, b, first, second)
 
     s, v, b, first, second = call(
@@ -409,23 +424,31 @@
         scratch=[pltpu.SemaphoreType.DMA((3,))],
     )
 
-    def prepare(lame_in, shear_in, zone_in, eligible_in, cohesion, friction, rock, zones, able, sems):
+    def across(s, v, b):
+        lanes = Lanes(depth)
+
+        def layer(x):
+            for t in bands:
+                push_velocity(shape, lanes, s, v, b, aligned(shape, x, t), "xz")
+
+        layers(*inner, layer, 4)
+
+    def prepare(
+        v_in, s, b, lame_in, shear_in, zone_in, able_in, cohesion, friction, v, rock, zones, able, sems
+    ):
         flat = rock.reshape(5, rows_x, rows_y, depth)
-        copies = [
-            pltpu.make_async_copy(zone_in, zones, sems.at[0]),
-            pltpu.make_async_copy(eligible_in, able, sems.at[1]),
-            pltpu.make_async_copy(lame_in, flat.at[0], sems.at[2]),
-            pltpu.make_async_copy(shear_in, flat.at[1], sems.at[3]),
-        ]
+        pairs = ((zone_in, zones), (able_in, able), (lame_in, flat.at[0]), (shear_in, flat.at[1]))
+        copies = [pltpu.make_async_copy(a, c, sems.at[i]) for i, (a, c) in enumerate(pairs)]
         for c in copies:
             c.start()
-        copies[0].wait()
-        copies[1].wait()
-
-        def layer(i, carry):
-            for t in range(0, rows_y, 8):
-                own = pl.multiple_of(i * rows_y + t, 8)
-                which = zones[i, pl.ds(t, 8), :]
+        across(s, v, b)
+        for c in copies:
+            c.wait()
+
+        def layer(x):
+            for t in bands:
+                own = pl.multiple_of(x * rows_y + t, 8)
+                which = zones[x, pl.ds(t, 8), :]
                 hold = jnp.full((8, depth), cohesion[0], jnp.float32)
                 rub = jnp.full((8, depth), friction[0], jnp.float32)
                 for k in range(1, cohesion.shape[0]):
@@ -434,33 +457,69 @@
                     rub = jnp.where(hit, friction[k], rub)
                 rock[2, pl.ds(own, 8), :] = hold * jnp.sqrt(1.0 - rub * rub)
                 rock[3, pl.ds(own, 8), :] = rub
-                rock[4, pl.ds(own, 8), :] = jnp.where(able[i, pl.ds(t, 8), :] == 1, 1.0, 0.0)
-            return carry
-
-        lax.fori_loop(0, rows_x, layer, 0)
-        copies[2].wait()
-        copies[3].wait()
-
-    rock = call(
-        prepare,
-        [lame_first, modulus, zone, eligible, cohesion, friction],
-        [in_hbm] * 4 + [in_smem] * 2,
-        vmem((5, rows_x * rows_y, depth)),
-        in_vmem,
-        "prepare",
-        1000000,
-        scratch=[
-            pltpu.VMEM((rows_x, rows_y, depth), jnp.int32),
-            pltpu.VMEM((rows_x, rows_y, depth), jnp.int32),
-            pltpu.SemaphoreType.DMA((4,)),
-        ],
-    )
-
+                rock[4, pl.ds(own, 8), :] = jnp.where(able[x, pl.ds(t, 8), :] == 1, 1.0, 0.0)
+
+        layers(0, rows_x, layer, 4)
+
+    def plain(v_in, s, b, v):
+        across(s, v, b)
+
+    def middle(s, v, b, rock, cell, moment):
+        lanes = Lanes(depth)
+
+        def layer(x):
+            for t in bands:
+                push_velocity(shape, lanes, s, v, b, aligned(shape, x, t), "y")
+            push_velocity(shape, lanes, s, v, b, aligned(shape, x, -RIM), "xyz")
+
+        for t in bands:
+            push_velocity(shape, lanes, s, v, b, aligned(shape, inner[0], t), "y")
+        layers(inner[0] + 1, inner[1], layer, 4)
+        inject(shape, s, cell, moment, lambda x: (x >= deep[0]) & (x < deep[1]))
+        layers(*deep, lambda x: push_stress(shape, lanes, s, v, rock, x), 4)
+
+    def outer(s, v, b, rock, cell, moment, ready=None):
+        lanes = Lanes(depth)
+        for low in (-2, inner[1]):
+            for x in range(low, low + 4):
+                for t in bands:
+                    push_velocity(shape, lanes, s, v, b, aligned(shape, x, t), "xyz")
+        for low in (0, inner[1]):
+            for x in range(low, low + 3):
+                push_velocity(shape, lanes, s, v, b, aligned(shape, x, -RIM), "xyz")
+        if ready is not None:
+            ready()
+        rows = lambda x: (x >= 0) & (x < rows_x) & ((x < deep[0]) | (x >= deep[1]))
+        inject(shape, s, cell, moment, rows)
+        for low in (0, deep[1]):
+            for x in range(low, low + 4):
+                push_stress(shape, lanes, s, v, rock, x)
+
+    cells = [source_cell, source_moment]
+    out_shapes = [
+        pltpu.HBM(velocity.shape, jnp.float32),
+        pltpu.HBM(stress.shape, jnp.float32),
+    ]
     for step in range(STEPS):
         begin, end = step == 0, step == STEPS - 1
         first, second = swaps("gy", first, second)
 
         if begin:
+            v, rock = call(
+                prepare,
+                [v, s, b, lame_first, modulus, zone, eligible, cohesion, friction],
+                [in_vmem] * 3 + [in_hbm] * 4 + [in_smem] * 2,
+                [whole_v, vmem((5, rows_x * rows_y, depth))],
+                [in_vmem] * 2,
+                "prepare",
+                10000000,
+                aliases={0: 0},
+                scratch=[
+                    pltpu.VMEM((rows_x, rows_y, depth), jnp.int32),
+                    pltpu.VMEM((rows_x, rows_y, depth), jnp.int32),
+                    pltpu.SemaphoreType.DMA((4,)),
+                ],
+            )
 
             def turn(s_in, v_in, b_in, got_a, got_b, s, v, b, out_a, out_b):
                 receive_y(shape, s, v, b, got_a, got_b)
@@ -477,6 +536,7 @@
                 aliases={0: 0, 1: 1, 2: 2},
             )
         else:
+            v = call(plain, [v, s, b], [in_vmem] * 3, whole_v, in_vmem, "plain", 10000000, {0: 0})
 
             def turn(s_in, got_a, got_b, s, out_a, out_b):
                 receive_y(shape, s, None, None, got_a, got_b)
@@ -496,53 +556,88 @@
 
         if not end:
 
-            def advance(s_in, v_in, b_in, rock, got_a, got_b, cell, moment, s, v, b, out_a, out_b):
-                fields = (s, v, b) if begin else (s, None, None)
-                receive_x(shape, *fields, got_a, got_b)
-                update_velocity(shape, s, v, b)
-                inject(shape, s, cell, moment)
-                update_stress(shape, s, v, rock)
+            def interior(s_in, v_in, b, rock, cell, moment, s, v):
+                middle(s, v, b, rock, cell, moment)
+
+            s, v = call(
+                interior,
+                [s, v, b, rock] + cells,
+                [in_vmem] * 4 + [in_smem] * 2,
+                [whole_s, whole_v],
+                [in_vmem] * 2,
+                "interior",
+                10000000,
+                aliases={0: 0, 1: 1},
+            )
+
+            def border(s_in, v_in, b_in, rock, got_a, got_b, cell, moment, s, v, b, out_a, out_b):
+                receive_x(shape, *((s, v, b) if begin else (s, None, None)), got_a, got_b)
+                outer(s, v, b, rock, cell, moment)
                 send_y(shape, s, None, None, out_a, out_b)
 
             s, v, b, first, second = call(
-                advance,
-                [s, v, b, rock, first, second, source_cell, source_moment],
+                border,
+                [s, v, b, rock, first, second] + cells,
                 [in_vmem] * 6 + [in_smem] * 2,
                 [whole_s, whole_v, whole_b, buffers("y", False), buffers("y", False)],
                 [in_vmem] * 5,
-                "advance",
+                "border",
                 10000000,
                 aliases={0: 0, 1: 1, 2: 2},
             )
         else:
 
-            def finish(s_in, v_in, b, rock, got_a, got_b, cell, moment, s, v, v_out, s_out, sems):
-                receive_x(shape, s, None, None, got_a, got_b)
-                update_velocity(shape, s, v, b)
-                out_v = pltpu.make_async_copy(own_cells(shape, v), v_out, sems.at[0])
-                out_v.start()
-                inject(shape, s, cell, moment)
-                update_stress(shape, s, v, rock)
-                out_s = pltpu.make_async_copy(own_cells(shape, s), s_out, sems.at[1])
-                out_s.start()
-                out_v.wait()
-                out_s.wait()
-
-            _, _, velocity, stress = call(
-                finish,
-                [s, v, b, rock, first, second, source_cell, source_moment],
-                [in_vmem] * 6 + [in_smem] * 2,
-                [
-                    whole_s,
-                    whole_v,
-                    jax.ShapeDtypeStruct(velocity.shape, jnp.float32),
-                    jax.ShapeDtypeStruct(stress.shape, jnp.float32),
-                ],
-                [in_vmem, in_vmem, in_hbm, in_hbm],
-                "finish",
+            def interior(s_in, v_in, b, rock, cell, moment, s, v, v_out, s_out, sems):
+                middle(s, v, b, rock, cell, moment)
+                pairs = []
+                for ref, out, (low, high) in ((v, v_out, inner), (s, s_out, deep)):
+                    part = out.at[:, pl.ds(low, high - low)]
+                    pairs.append((own_cells(shape, ref, low, high - low), part))
+                run_copies(pairs, sems)
+
+            s, v, v_out, s_out = call(
+                interior,
+                [s, v, b, rock] + cells,
+                [in_vmem] * 4 + [in_smem] * 2,
+                [whole_s, whole_v] + out_shapes,
+                [in_vmem] * 2 + [in_hbm] * 2,
+                "interior_last",
                 10000000,
                 aliases={0: 0, 1: 1},
                 scratch=[pltpu.SemaphoreType.DMA((2,))],
+            )
+
+            def border(
+                s_in, v_in, b, rock, got_a, got_b, cell, moment, v_old, s_old, s, v, v_out, s_out, sems
+            ):
+                def copies(ref, out, low, high, at):
+                    spans = ((0, low), (high, rows_x - high))
+                    return [
+                        pltpu.make_async_copy(
+                            own_cells(shape, ref, x, n), out.at[:, pl.ds(x, n)], sems.at[at + i]
+                        )
+                        for i, (x, n) in enumerate(spans)
+                    ]
+
+                v_copies = copies(v, v_out, *inner, 0)
+                s_copies = copies(s, s_out, *deep, 2)
+                receive_x(shape, s, None, None, got_a, got_b)
+                outer(s, v, b, rock, cell, moment, lambda: [c.start() for c in v_copies])
+                for c in s_copies:
+                    c.start()
+                for c in v_copies + s_copies:
+                    c.wait()
+
+            _, _, velocity, stress = call(
+                border,
+                [s, v, b, rock, first, second] + cells + [v_out, s_out],
+                [in_vmem] * 6 + [in_smem] * 2 + [in_hbm] * 2,
+                [whole_s, whole_v] + out_shapes,
+                [in_vmem, in_vmem, in_hbm, in_hbm],
+                "border_last",
+                10000000,
+                aliases={0: 0, 1: 1, 8: 2, 9: 3},
+                scratch=[pltpu.SemaphoreType.DMA((4,))],
             )
     return (velocity, stress)
 

time: 56.2 us -> 41.5 us (0.74)
  waiting for transfers between devices: 21.1 us -> 12.9 us
  Pallas kernels: 19 us -> 14.3 us
  local copies, waits for them, and re-layouts: 3.07 us -> 1.31 us
    ppermute x8, waiting for transfers between devices: 21.1 us -> 12.9 us  [swaps(): got.append(lax.ppermute(block, axis, pairs))]
    pallas_call x6 -> x9, Pallas kernels: 19 us -> 14.3 us  [call(): pl.pallas_call(body, in_specs=in_specs, out_shape=out_shape, out_specs=ou...]
    unnamed x22 -> x8, local copies, waits for them, and re-layouts: 3.07 us -> 1.31 us
  transfers between devices with their start and end apart: 8 -> 8, of which waited for: 6 -> 4; matrix products, arithmetic and copies ran while one was open for 0% -> 0% of each run, Pallas kernels for 3% -> 21%
where the time goes in v2:
time: 41.5 us; the launch traced here: 41.2 us
  Pallas kernels  14.3 us (34%)
  waiting for transfers between devices  12.9 us (31%)
  starting transfers between devices  11.9 us (29%)
  local copies, waits for them, and re-layouts  1.31 us (3%)
  between operations  0.81 us (2%)
    pallas_call x9, Pallas kernels, call(): pl.pallas_call(body, in_specs=in_specs, out_shape=out_shape, out_specs=ou...  14.3 us
    ppermute x8, waiting for transfers between devices, swaps(): got.append(lax.ppermute(block, axis, pairs))  12.9 us
    ppermute x8, starting transfers between devices, swaps(): got.append(lax.ppermute(block, axis, pairs))  11.9 us
    unnamed x8, local copies, waits for them, and re-layouts  1.31 us
  transfers between devices with their start and end apart: 8, of which 4 were waited for; matrix products, arithmetic and copies ran while one was open for 0% of the time, Pallas kernels for 21%

profile of v2, /device:TPU:12, one launch (start us, length us, event | category | flops | bytes accessed | tf_op | source)
XLA Modules:
  0.0 41.2 jit_solution(3558184272910506867)
XLA Ops:
  0.6 1.5 %load.1 = (f32[6,656,128]{2,1,0:T(8,128)S(1)}, f32[3,656,128]{2,1,0:T(8,128)S(1)}, f32[656,128]{1,0:T(8,128)S(1)}, f32[22,32,128]{2,1,0:T(8,128)S(1)}, f32[22,32,128]{2,1,0:T(8,128)S(1)}) custom-call(f32[3,32,8,128]{3,2,1,0:T(8,128)} %v_in.1, f32[6,32,8,128]{3,2,1,0:T(8,128)} %s_in.1, f32[32,8,128]{2,1,0:T(8,128)} %b_in.1), custom_call_target="tpu_custom_call" | custom-call | flops 1000000 | bytes 1000000 | tf_op jit(solution)/shard_map/load/pallas_call | solution.py:355
  2.1 0.1 collective-permute-start
  2.2 2.4 %collective-permute-start.1 = (f32[22,32,128]{2,1,0:T(8,128)S(1)}, f32[22,32,128]{2,1,0:T(8,128)S(1)}, u32[]{:S(2)}, u32[]{:S(2)}) collective-permute-start(f32[22,32,128]{2,1,0:T(8,128)S(1)} %get-tuple-element.35), channel_id=1, source_target_pairs={{1,2},{2,1},{3,4},{4,3},{5,6},{6,5},{9,10},{10,9},{11,12},{12,11},... | collective-permute-start | bytes 1081352 | tf_op jit(solution)/shard_map/ppermute | solution.py:375
  4.7 0.0 copy-start.2
  4.7 0.6 %copy-done.2 = f32[8]{0:T(128)S(1)} copy-done((f32[8]{0:T(128)S(1)}, f32[8]{0:T(128)}, u32[]{:S(2)}) %copy-start.2) | copy-done | bytes 56
  5.3 0.0 copy-start.3
  5.3 0.7 %copy-done.3 = f32[8]{0:T(128)S(1)} copy-done((f32[8]{0:T(128)S(1)}, f32[8]{0:T(128)}, u32[]{:S(2)}) %copy-start.3) | copy-done | bytes 56
  6.0 1.9 %prepare.1 = (f32[3,656,128]{2,1,0:T(8,128)S(1)}, f32[5,256,128]{2,1,0:T(8,128)S(1)}) custom-call(f32[3,656,128]{2,1,0:T(8,128)S(1)} %get-tuple-element.31.v_in, f32[6,656,128]{2,1,0:T(8,128)S(1)} %get-tuple-element.30.s.s_in, f32[656,128]{1,0:T(8,128)S(1)} %get-tuple-element.32.b.b_in, f32[32,8,128]{2,1,0:T(8,128)} %lame_in.1, ...), custom_call_target="tpu_custom_call", output_to_operand_aliasing={{0}: (0, {})} | custom-call | flops 10000000 | bytes 1000000 | tf_op jit(solution)/shard_map/prepare/pallas_call | solution.py:355
  7.9 0.0 collective-permute-done.got_a
  7.9 3.1 %collective-permute-done.1.got_b = f32[22,32,128]{2,1,0:T(8,128)S(1)} collective-permute-done((f32[22,32,128]{2,1,0:T(8,128)S(1)}, f32[22,32,128]{2,1,0:T(8,128)S(1)}, u32[]{:S(2)}, u32[]{:S(2)}) %collective-permute-start.1) | collective-permute-done | bytes 360480 | tf_op jit(solution)/shard_map/ppermute | solution.py:375
  11.0 0.0 copy-start
  11.0 0.0 copy-start.1
  11.0 0.3 turn_first.1
  11.3 1.6 %collective-permute-start.2 = (f32[35,8,128]{2,1,0:T(8,128)S(1)}, f32[35,8,128]{2,1,0:T(8,128)S(1)}, u32[]{:S(2)}, u32[]{:S(2)}) collective-permute-start(f32[35,8,128]{2,1,0:T(8,128)S(1)} %get-tuple-element.42), channel_id=1, source_target_pairs={{0,8},{8,0},{16,24},{24,16},{1,9},{9,1},{17,25},{25,17},{2,10},{10... | collective-permute-start | bytes 430088 | tf_op jit(solution)/shard_map/ppermute | solution.py:375
  12.8 2.4 %collective-permute-start.3 = (f32[35,8,128]{2,1,0:T(8,128)S(1)}, f32[35,8,128]{2,1,0:T(8,128)S(1)}, u32[]{:S(2)}, u32[]{:S(2)}) collective-permute-start(f32[35,8,128]{2,1,0:T(8,128)S(1)} %get-tuple-element.43), channel_id=1, source_target_pairs={{8,16},{16,8},{9,17},{17,9},{10,18},{18,10},{11,19},{19,11},{12,20... | collective-permute-start | bytes 430088 | tf_op jit(solution)/shard_map/ppermute | solution.py:375
  15.2 0.0 copy-done
  15.2 0.0 copy-done.1
  15.2 2.6 %interior.1 = (f32[6,656,128]{2,1,0:T(8,128)S(1)}, f32[3,656,128]{2,1,0:T(8,128)S(1)}) custom-call(f32[6,656,128]{2,1,0:T(8,128)S(1)} %get-tuple-element.36.s_in, f32[3,656,128]{2,1,0:T(8,128)S(1)} %get-tuple-element.37.v_in, f32[656,128]{1,0:T(8,128)S(1)} %get-tuple-element.38.b.b_in, ...), custom_call_target="tpu_custom_call", output_to_operand_aliasing={{0}: (0, {}), {1}: (1, {})} | custom-call | flops 10000000 | bytes 1000000 | tf_op jit(solution)/shard_map/interior/pallas_call | solution.py:355
  17.8 0.0 collective-permute-done.2.got_a
  17.8 3.7 %collective-permute-done.3.got_b = f32[35,8,128]{2,1,0:T(8,128)S(1)} collective-permute-done((f32[35,8,128]{2,1,0:T(8,128)S(1)}, f32[35,8,128]{2,1,0:T(8,128)S(1)}, u32[]{:S(2)}, u32[]{:S(2)}) %collective-permute-start.3) | collective-permute-done | bytes 143392 | tf_op jit(solution)/shard_map/ppermute | solution.py:375
  21.5 1.4 %border.1 = (f32[6,656,128]{2,1,0:T(8,128)S(1)}, f32[3,656,128]{2,1,0:T(8,128)S(1)}, f32[656,128]{1,0:T(8,128)S(1)}, f32[15,32,128]{2,1,0:T(8,128)S(1)}, f32[15,32,128]{2,1,0:T(8,128)S(1)}) custom-call(f32[6,656,128]{2,1,0:T(8,128)S(1)} %get-tuple-element.40.s_in, ...), custom_call_target="tpu_custom_call", output_to_operand_aliasing={{0}: (0, {}), {1}: (1, {}), {2}: (2, {})} | custom-call | flops 10000000 | bytes 1000000 | tf_op jit(solution)/shard_map/border/pallas_call | solution.py:355
  22.9 0.1 collective-permute-start.4
  23.0 1.9 %collective-permute-start.5 = (f32[15,32,128]{2,1,0:T(8,128)S(1)}, f32[15,32,128]{2,1,0:T(8,128)S(1)}, u32[]{:S(2)}, u32[]{:S(2)}) collective-permute-start(f32[15,32,128]{2,1,0:T(8,128)S(1)} %get-tuple-element.46), channel_id=1, source_target_pairs={{1,2},{2,1},{3,4},{4,3},{5,6},{6,5},{9,10},{10,9},{11,12},{12,11},... | collective-permute-start | bytes 737288 | tf_op jit(solution)/shard_map/ppermute | solution.py:375
  25.0 0.8 %plain.1.v_in = f32[3,656,128]{2,1,0:T(8,128)S(1)} custom-call(f32[3,656,128]{2,1,0:T(8,128)S(1)} %get-tuple-element.48.v_in, f32[6,656,128]{2,1,0:T(8,128)S(1)} %get-tuple-element.44.s_in.s, f32[656,128]{1,0:T(8,128)S(1)} %get-tuple-element.49.b), custom_call_target="tpu_custom_call", output_to_operand_aliasing={{}: (0, {})} | custom-call | flops 10000000 | bytes 1000000 | tf_op jit(solution)/shard_map/plain/pallas_call | solution.py:355
  25.7 0.0 collective-permute-done.4.got_a
  25.7 4.8 %collective-permute-done.5.got_b = f32[15,32,128]{2,1,0:T(8,128)S(1)} collective-permute-done((f32[15,32,128]{2,1,0:T(8,128)S(1)}, f32[15,32,128]{2,1,0:T(8,128)S(1)}, u32[]{:S(2)}, u32[]{:S(2)}) %collective-permute-start.5) | collective-permute-done | bytes 245792 | tf_op jit(solution)/shard_map/ppermute | solution.py:375
  30.5 0.2 turn.1
  30.8 0.1 collective-permute-start.6
  30.9 3.4 %collective-permute-start.7 = (f32[28,8,128]{2,1,0:T(8,128)S(1)}, f32[28,8,128]{2,1,0:T(8,128)S(1)}, u32[]{:S(2)}, u32[]{:S(2)}) collective-permute-start(f32[28,8,128]{2,1,0:T(8,128)S(1)} %get-tuple-element.53), channel_id=1, source_target_pairs={{8,16},{16,8},{9,17},{17,9},{10,18},{18,10},{11,19},{19,11},{12,20... | collective-permute-start | bytes 344072 | tf_op jit(solution)/shard_map/ppermute | solution.py:375
  34.2 3.5 %interior_last.1 = (f32[6,656,128]{2,1,0:T(8,128)S(1)}, f32[3,656,128]{2,1,0:T(8,128)S(1)}, f32[3,32,8,128]{3,2,1,0:T(8,128)}, f32[6,32,8,128]{3,2,1,0:T(8,128)}) custom-call(f32[6,656,128]{2,1,0:T(8,128)S(1)} %get-tuple-element.47.s_in, f32[3,656,128]{2,1,0:T(8,128)S(1)} %plain.1.v_in, ...), custom_call_target="tpu_custom_call", output_to_operand_aliasing={{0}: (0, {}), {1}: (1, {})} | custom-call | flops 10000000 | bytes 1000000 | tf_op jit(solution)/shard_map/interior_last/pallas_call | solution.py:355
  37.8 0.0 collective-permute-done.6.got_a
  37.8 1.4 %collective-permute-done.7.got_b = f32[28,8,128]{2,1,0:T(8,128)S(1)} collective-permute-done((f32[28,8,128]{2,1,0:T(8,128)S(1)}, f32[28,8,128]{2,1,0:T(8,128)S(1)}, u32[]{:S(2)}, u32[]{:S(2)}) %collective-permute-start.7) | collective-permute-done | bytes 114720 | tf_op jit(solution)/shard_map/ppermute | solution.py:375
  39.2 2.0 %border_last.1 = (f32[6,656,128]{2,1,0:T(8,128)S(1)}, f32[3,656,128]{2,1,0:T(8,128)S(1)}, f32[3,32,8,128]{3,2,1,0:T(8,128)}, f32[6,32,8,128]{3,2,1,0:T(8,128)}) custom-call(f32[6,656,128]{2,1,0:T(8,128)S(1)} %get-tuple-element.50.s_in, ...), custom_call_target="tpu_custom_call", output_to_operand_aliasing={{0}: (0, {}), {1}: (1, {}), {2}: (8, {}), {3}: (9, {})} | custom-call | flops 10000000 | bytes 1000000 | tf_op jit(solution)/shard_map/border_last/pallas_call | solution.py:355
Async XLA Ops:
  2.1 5.7 %collective-permute-start = (f32[22,32,128]{2,1,0:T(8,128)S(1)}, f32[22,32,128]{2,1,0:T(8,128)S(1)}, u32[]{:S(2)}, u32[]{:S(2)}) collective-permute-start(f32[22,32,128]{2,1,0:T(8,128)S(1)} %get-tuple-element.34), channel_id=1, source_target_pairs={{0,1},{1,0},{2,3},{3,2},{4,5},{5,4},{6,7},{7,6},{8,9},{9,8},{10,11... | collective-permute-start | bytes 1081352 | tf_op jit(solution)/shard_map/ppermute | solution.py:375
  2.2 8.7 %collective-permute-start.1 = (f32[22,32,128]{2,1,0:T(8,128)S(1)}, f32[22,32,128]{2,1,0:T(8,128)S(1)}, u32[]{:S(2)}, u32[]{:S(2)}) collective-permute-start(f32[22,32,128]{2,1,0:T(8,128)S(1)} %get-tuple-element.35), channel_id=1, source_target_pairs={{1,2},{2,1},{3,4},{4,3},{5,6},{6,5},{9,10},{10,9},{11,12},{12,11},... | collective-permute-start | bytes 1081352 | tf_op jit(solution)/shard_map/ppermute | solution.py:375
  4.7 0.7 %copy-start.2 = (f32[8]{0:T(128)S(1)}, f32[8]{0:T(128)}, u32[]{:S(2)}) copy-start(f32[8]{0:T(128)} %cohesion.1) | copy-start | bytes 100
  5.3 0.7 %copy-start.3 = (f32[8]{0:T(128)S(1)}, f32[8]{0:T(128)}, u32[]{:S(2)}) copy-start(f32[8]{0:T(128)} %friction.1) | copy-start | bytes 100
  11.0 4.3 %copy-start = (f32[6,16]{1,0:T(8,128)S(1)}, f32[6,16]{1,0:T(8,128)}, u32[]{:S(2)}) copy-start(f32[6,16]{1,0:T(8,128)} %moment.7) | copy-start | bytes 1156
  11.0 4.3 %copy-start.1 = (s32[16]{0:T(128)S(1)}, s32[16]{0:T(128)}, u32[]{:S(2)}) copy-start(s32[16]{0:T(128)} %cell.7) | copy-start | bytes 196
  11.3 6.5 %collective-permute-start.2 = (f32[35,8,128]{2,1,0:T(8,128)S(1)}, f32[35,8,128]{2,1,0:T(8,128)S(1)}, u32[]{:S(2)}, u32[]{:S(2)}) collective-permute-start(f32[35,8,128]{2,1,0:T(8,128)S(1)} %get-tuple-element.42), channel_id=1, source_target_pairs={{0,8},{8,0},{16,24},{24,16},{1,9},{9,1},{17,25},{25,17},{2,10},{10... | collective-permute-start | bytes 430088 | tf_op jit(solution)/shard_map/ppermute | solution.py:375
  12.8 8.6 %collective-permute-start.3 = (f32[35,8,128]{2,1,0:T(8,128)S(1)}, f32[35,8,128]{2,1,0:T(8,128)S(1)}, u32[]{:S(2)}, u32[]{:S(2)}) collective-permute-start(f32[35,8,128]{2,1,0:T(8,128)S(1)} %get-tuple-element.43), channel_id=1, source_target_pairs={{8,16},{16,8},{9,17},{17,9},{10,18},{18,10},{11,19},{19,11},{12,20... | collective-permute-start | bytes 430088 | tf_op jit(solution)/shard_map/ppermute | solution.py:375
  22.9 2.8 %collective-permute-start.4 = (f32[15,32,128]{2,1,0:T(8,128)S(1)}, f32[15,32,128]{2,1,0:T(8,128)S(1)}, u32[]{:S(2)}, u32[]{:S(2)}) collective-permute-start(f32[15,32,128]{2,1,0:T(8,128)S(1)} %get-tuple-element.45), channel_id=1, source_target_pairs={{0,1},{1,0},{2,3},{3,2},{4,5},{5,4},{6,7},{7,6},{8,9},{9,8},{10,11... | collective-permute-start | bytes 737288 | tf_op jit(solution)/shard_map/ppermute | solution.py:375
  23.0 7.5 %collective-permute-start.5 = (f32[15,32,128]{2,1,0:T(8,128)S(1)}, f32[15,32,128]{2,1,0:T(8,128)S(1)}, u32[]{:S(2)}, u32[]{:S(2)}) collective-permute-start(f32[15,32,128]{2,1,0:T(8,128)S(1)} %get-tuple-element.46), channel_id=1, source_target_pairs={{1,2},{2,1},{3,4},{4,3},{5,6},{6,5},{9,10},{10,9},{11,12},{12,11},... | collective-permute-start | bytes 737288 | tf_op jit(solution)/shard_map/ppermute | solution.py:375
  30.8 7.0 %collective-permute-start.6 = (f32[28,8,128]{2,1,0:T(8,128)S(1)}, f32[28,8,128]{2,1,0:T(8,128)S(1)}, u32[]{:S(2)}, u32[]{:S(2)}) collective-permute-start(f32[28,8,128]{2,1,0:T(8,128)S(1)} %get-tuple-element.52), channel_id=1, source_target_pairs={{0,8},{8,0},{16,24},{24,16},{1,9},{9,1},{17,25},{25,17},{2,10},{10... | collective-permute-start | bytes 344072 | tf_op jit(solution)/shard_map/ppermute | solution.py:375
  30.9 8.3 %collective-permute-start.7 = (f32[28,8,128]{2,1,0:T(8,128)S(1)}, f32[28,8,128]{2,1,0:T(8,128)S(1)}, u32[]{:S(2)}, u32[]{:S(2)}) collective-permute-start(f32[28,8,128]{2,1,0:T(8,128)S(1)} %get-tuple-element.53), channel_id=1, source_target_pairs={{8,16},{16,8},{9,17},{17,9},{10,18},{18,10},{11,19},{19,11},{12,20... | collective-permute-start | bytes 344072 | tf_op jit(solution)/shard_map/ppermute | solution.py:375

commit v3 on v2

--- a/solution.py
+++ b/solution.py
@@ -14,14 +14,15 @@
 
 XX, YY, ZZ, XY, XZ, YZ = range(6)
 
-LOW_Y = ((XX, 1), (XY, 3), (XZ, 1), (YY, 3), (YZ, 3), (ZZ, 1))
-HIGH_Y = ((XX, 2), (XY, 3), (XZ, 2), (YY, 3), (YZ, 3), (ZZ, 2))
-LOW_X = ((XX, 3), (XY, 3), (XZ, 3), (YY, 1), (YZ, 1), (ZZ, 1))
-HIGH_X = ((XX, 3), (XY, 3), (XZ, 3), (YY, 2), (YZ, 2), (ZZ, 2))
+LOW_Y = ((XY, 2), (YY, 1), (YZ, 2))
+HIGH_Y = ((XY, 1), (YY, 2), (YZ, 1))
+LOW_X = ((XX, 1), (XY, 2), (XZ, 2))
+HIGH_X = ((XX, 2), (XY, 1), (XZ, 1))
 LOW_FLOW_Y = ((0, 1), (1, 2), (2, 1))
 HIGH_FLOW_Y = ((0, 2), (1, 1), (2, 2))
 LOW_FLOW_X = ((0, 2), (1, 1), (2, 1))
 HIGH_FLOW_X = ((0, 1), (1, 2), (2, 2))
+DRIVES = (XX, XY, XZ)
 
 PAD_X = 4
 RIM = 8
@@ -41,18 +42,6 @@
     return [(c, k) for c, depth in spec for k in range(depth)]
 
 
-def y_rows(low, high, rows_y):
-    up = [(c, rows_y - 1 - k) for c, k in entries(low)]
-    down = [(c, k) for c, k in entries(high)]
-    return up, down
-
-
-def got_y(low, high, rows_y):
-    below = [(c, -1 - k) for c, k in entries(low)]
-    above = [(c, rows_y + k) for c, k in entries(high)]
-    return below, above
-
-
 def pack_y(shape, pairs, out):
     for slot, (ref, y) in enumerate(pairs):
         for x in range(0, shape.rows_x, 8):
@@ -65,125 +54,191 @@
             ref[pl.ds(shape.row(x, y), 8, stride=shape.pitch), :] = got[slot, pl.ds(x, 8), :]
 
 
-def pack_x(shape, whole, inner, out):
-    sub = lax.broadcasted_iota(jnp.int32, (8, shape.depth), 0)
-    slot = 0
-    for ref, x, rim in whole:
-        for t in range(0, shape.rows_y, 8):
-            out[slot] = ref[pl.ds(shape.row(x, t), 8), :]
-            slot += 1
-        if rim:
-            after = ref[pl.ds(shape.row(x + 1, -RIM), 8), :]
-            before = ref[pl.ds(shape.row(x, -RIM), 8), :]
-            out[slot] = jnp.where(sub < 4, after, before)
-            slot += 1
-    return slot
-
-
-def unpack_x(shape, whole, got):
-    slot = 0
-    for ref, x, rim in whole:
-        for t in range(0, shape.rows_y, 8):
-            ref[pl.ds(shape.row(x, t), 8), :] = got[slot]
-            slot += 1
-        if rim:
-            ref[pl.ds(shape.row(x + 1, -RIM), 4), :] = got[slot, 0:4, :]
-            ref[pl.ds(shape.row(x, -4), 4), :] = got[slot, 4:8, :]
-            slot += 1
-
-
-def x_slots(spec, rows_y, rim):
-    count = 0
-    for c, depth in spec:
-        count += depth * (rows_y // 8 + (1 if rim and c != ZZ else 0))
-    return count
-
-
-def x_list(stress, flow, buoyancy, spec, flow_spec, place):
-    whole = [(stress.at[c], place(k), c != ZZ) for c, k in entries(spec)]
-    if flow is not None:
-        whole += [(flow.at[c], place(k), False) for c, k in entries(flow_spec)]
-        whole += [(buoyancy, place(k), False) for k in range(2)]
-    return whole
-
-
-def y_list(stress, flow, buoyancy, rows, flow_rows, rim_rows):
-    pairs = [(stress.at[c], y) for c, y in rows]
-    if flow is not None:
-        pairs += [(flow.at[c], y) for c, y in flow_rows]
-        pairs += [(buoyancy, y) for y in rim_rows]
+def y_list(fields, spec, flow_spec, place):
+    halo, flow, buoyancy = fields
+    pairs = [(halo[c], place(k)) for c, k in entries(spec)]
+    pairs += [(flow.at[c], place(k)) for c, k in entries(flow_spec)]
+    if buoyancy is not None:
+        pairs += [(buoyancy, place(k)) for k in range(2)]
     return pairs
 
 
-def send_y(shape, stress, flow, buoyancy, first, second):
-    rows_y = shape.rows_y
-    up, down = y_rows(LOW_Y, HIGH_Y, rows_y)
-    flow_up, flow_down = y_rows(LOW_FLOW_Y, HIGH_FLOW_Y, rows_y)
-    up = y_list(stress, flow, buoyancy, up, flow_up, (rows_y - 1, rows_y - 2))
-    down = y_list(stress, flow, buoyancy, down, flow_down, (0, 1))
-    odd = lax.axis_index("gy") % 2
+def edge_layers(shape):
+    return (0, 1, shape.rows_x - 2, shape.rows_x - 1)
+
+
+def pack_corner(shape, stress, flow_spec, place, out):
+    for i, x in enumerate(edge_layers(shape)):
+        for j, (c, k) in enumerate(entries(flow_spec)):
+            row = shape.row(x, place(k))
+            out[pl.ds(8 * i + j, 1), :] = stress[DRIVES[c], pl.ds(row, 1), :]
+
+
+def by_parity(axis, body, first, second):
+    odd = lax.axis_index(axis) % 2
 
     @pl.when(odd == 0)
     def _():
-        pack_y(shape, up, first)
-        pack_y(shape, down, second)
+        body(second, first)
 
     @pl.when(odd == 1)
     def _():
-        pack_y(shape, down, first)
-        pack_y(shape, up, second)
-
-
-def receive_y(shape, stress, flow, buoyancy, first, second):
-    rows_y = shape.rows_y
-    below, above = got_y(LOW_Y, HIGH_Y, rows_y)
-    flow_below, flow_above = got_y(LOW_FLOW_Y, HIGH_FLOW_Y, rows_y)
-    below = y_list(stress, flow, buoyancy, below, flow_below, (-1, -2))
-    above = y_list(stress, flow, buoyancy, above, flow_above, (rows_y, rows_y + 1))
-    odd = lax.axis_index("gy") % 2
-
-    @pl.when(odd == 0)
-    def _():
-        unpack_y(shape, above, first)
-        unpack_y(shape, below, second)
-
-    @pl.when(odd == 1)
-    def _():
-        unpack_y(shape, below, first)
-        unpack_y(shape, above, second)
-
-
-def send_x(shape, stress, flow, buoyancy, first, second):
-    last = shape.rows_x - 1
-    up = x_list(stress, flow, buoyancy, LOW_X, LOW_FLOW_X, lambda k: last - k)
-    down = x_list(stress, flow, buoyancy, HIGH_X, HIGH_FLOW_X, lambda k: k)
-    odd = lax.axis_index("gx") % 2
-
-    @pl.when(odd == 0)
-    def _():
-        pack_x(shape, up, None, first)
-        pack_x(shape, down, None, second)
-
-    @pl.when(odd == 1)
-    def _():
-        pack_x(shape, down, None, first)
-        pack_x(shape, up, None, second)
-
-
-def receive_x(shape, stress, flow, buoyancy, first, second):
-    below = x_list(stress, flow, buoyancy, LOW_X, LOW_FLOW_X, lambda k: -1 - k)
-    above = x_list(stress, flow, buoyancy, HIGH_X, HIGH_FLOW_X, lambda k: shape.rows_x + k)
-    odd = lax.axis_index("gx") % 2
-
-    @pl.when(odd == 0)
-    def _():
-        unpack_x(shape, above, first)
-        unpack_x(shape, below, second)
-
-    @pl.when(odd == 1)
-    def _():
-        unpack_x(shape, below, first)
-        unpack_x(shape, above, second)
+        body(first, second)
+
+
+def send_y(shape, stress, flow, buoyancy, first, second):
+    fields = ({c: stress.at[c] for c in range(6)}, flow, buoyancy)
+    top = lambda k: shape.rows_y - 1 - k
+    bottom = lambda k: k
+
+    def body(below, above):
+        last = above.shape[0] - 1
+        pack_y(shape, y_list(fields, LOW_Y, LOW_FLOW_Y, top), above)
+        pack_corner(shape, stress, LOW_FLOW_Y, top, above.at[last])
+        pack_y(shape, y_list(fields, HIGH_Y, HIGH_FLOW_Y, bottom), below)
+        pack_corner(shape, stress, HIGH_FLOW_Y, bottom, below.at[last])
+
+    by_parity("gy", body, first, second)
+
+
+def receive_y(shape, halo, flow, buoyancy, first, second):
+    fields = ({c: halo.at[i] for i, c in enumerate((XY, YY, YZ))}, flow, buoyancy)
+
+    def body(below, above):
+        unpack_y(shape, y_list(fields, LOW_Y, LOW_FLOW_Y, lambda k: -1 - k), below)
+        unpack_y(shape, y_list(fields, HIGH_Y, HIGH_FLOW_Y, lambda k: shape.rows_y + k), above)
+
+    by_parity("gy", body, first, second)
+
+
+def x_count(shape, first_round):
+    bands = shape.rows_y // 8
+    most = max(
+        len(entries(spec)) * (bands + 1) + len(entries(flow_spec)) * bands
+        for spec, flow_spec in ((LOW_X, LOW_FLOW_X), (HIGH_X, HIGH_FLOW_X))
+    )
+    return most + (2 * bands if first_round else 0)
+
+
+def y_count(first_round):
+    most = max(
+        len(entries(spec)) + len(entries(flow_spec))
+        for spec, flow_spec in ((LOW_Y, LOW_FLOW_Y), (HIGH_Y, HIGH_FLOW_Y))
+    )
+    return most + 1 + (2 if first_round else 0)
+
+
+def x_slots(shape, spec, flow_spec, first_round):
+    bands = range(0, shape.rows_y, 8)
+    keys = [("s", c, k, t) for c, k in entries(spec) for t in bands]
+    keys += [("v", c, k, t) for c, k in entries(flow_spec) for t in bands]
+    keys += [("rim", c, k) for c, k in entries(spec)]
+    if first_round:
+        keys += [("b", 0, k, t) for k in range(2) for t in bands]
+    return {key: i for i, key in enumerate(keys)}
+
+
+def send_x(shape, stress, flow, buoyancy, got_first, got_second, first, second):
+    arrays = {"s": stress, "v": flow, "b": buoyancy}
+    layer_at = {x: i for i, x in enumerate(edge_layers(shape))}
+
+    def with_corners(got_below, got_above):
+        def fill(out, spec, flow_spec, place):
+            slots = x_slots(shape, spec, flow_spec, buoyancy is not None)
+            for (kind, c, k, *t), slot in slots.items():
+                if kind == "rim":
+                    for got, rims, at in (
+                        (got_above, HIGH_FLOW_Y, lambda d: d),
+                        (got_below, LOW_FLOW_Y, lambda d: 7 - d),
+                    ):
+                        for j, (which, depth) in enumerate(entries(rims)):
+                            if DRIVES[which] == c:
+                                row = 8 * layer_at[place(k)] + j
+                                corner = got[got.shape[0] - 1, pl.ds(row, 1), :]
+                                out[slot, pl.ds(at(depth), 1), :] = corner
+                else:
+                    ref = arrays[kind] if kind == "b" else arrays[kind].at[c]
+                    out[slot] = tile(ref, shape.row(place(k), t[0]))
+
+        def body(below, above):
+            fill(above, LOW_X, LOW_FLOW_X, lambda k: shape.rows_x - 1 - k)
+            fill(below, HIGH_X, HIGH_FLOW_X, lambda k: k)
+
+        by_parity("gx", body, first, second)
+
+    by_parity("gy", with_corners, got_first, got_second)
+
+
+NEAR, FAR = near_weight, far_weight
+UP = {1: NEAR, 0: -NEAR, 2: -FAR, -1: FAR}
+DOWN = {0: NEAR, -1: -NEAR, 1: -FAR, -2: FAR}
+
+
+def crossing(c, x, sources):
+    total = None
+    for step, weight in (UP if c == 0 else DOWN).items():
+        if x + step in sources:
+            term = weight * sources[x + step]()
+            total = term if total is None else total + term
+    return total
+
+
+def receive_x(shape, stress, flow, buoyancy, first_round, first, second):
+    rows_x = shape.rows_x
+    sub = lax.broadcasted_iota(jnp.int32, (8, shape.depth), 0)
+
+    def body(below, above):
+        sides = (
+            (below, x_slots(shape, LOW_X, LOW_FLOW_X, first_round), lambda k: -1 - k),
+            (above, x_slots(shape, HIGH_X, HIGH_FLOW_X, first_round), lambda k: rows_x + k),
+        )
+        came = {}
+        for got, slots, place in sides:
+            for (kind, c, k, *t), slot in slots.items():
+                if kind == "b":
+                    buoyancy[pl.ds(shape.row(place(k), t[0]), 8), :] = got[slot]
+                else:
+                    came[(kind, c, place(k), *t)] = (got, slot)
+
+        def arrived(kind, c, *t):
+            return {
+                key[2]: (lambda got=got, slot=slot: got[slot])
+                for key, (got, slot) in came.items()
+                if key[:2] == (kind, c) and key[3:] == t
+            }
+
+        for t in range(0, shape.rows_y, 8):
+            for c in range(3):
+                halo = arrived("s", DRIVES[c], t)
+                own = {
+                    x: (lambda x=x: tile(stress.at[DRIVES[c]], shape.row(x, t)))
+                    for x in edge_layers(shape)
+                }
+                rim = arrived("v", c, t)
+                for x in edge_layers(shape):
+                    force = crossing(c, x, halo)
+                    if force is not None:
+                        row = shape.row(x, t)
+                        flow[c, pl.ds(row, 8), :] += time_step * tile(buoyancy, row) * force
+                for x, value in rim.items():
+                    row = shape.row(x, t)
+                    force = crossing(c, x, own)
+                    flow[c, pl.ds(row, 8), :] = value() + time_step * tile(buoyancy, row) * force
+        for c in range(3):
+            halo = arrived("rim", DRIVES[c])
+            forces = {x: crossing(c, x, halo) for x in edge_layers(shape)}
+            for x in sorted({x + d for x in edge_layers(shape) for d in (0, 1)}):
+                high, low = forces.get(x - 1), forces.get(x)
+                if high is None and low is None:
+                    continue
+                zero = jnp.zeros((8, shape.depth), jnp.float32)
+                force = jnp.where(
+                    sub < 4, zero if high is None else high, zero if low is None else low
+                )
+                row = shape.row(x, -RIM)
+                flow[c, pl.ds(row, 8), :] += time_step * tile(buoyancy, row) * force
+
+    by_parity("gx", body, first, second)
 
 
 class Lanes:
@@ -238,6 +293,14 @@
     force = parts[along[0]]()
     for axis in along[1:]:
         force = [f + g for f, g in zip(force, parts[axis]())]
+    scale = time_step * tile(buoyancy, row)
+    for c in range(3):
+        flow[c, pl.ds(row, 8), :] += scale * force[c]
+
+
+def push_across_y(halves, flow, buoyancy, row):
+    xy, yy, yz = halves
+    force = (backward(xy, row, 1), forward(yy, row, 1), backward(yz, row, 1))
     scale = time_step * tile(buoyancy, row)
     for c in range(3):
         flow[c, pl.ds(row, 8), :] += scale * force[c]
@@ -392,58 +455,66 @@
     shape = Shape(*zone.shape)
     rows_x, rows_y, depth = zone.shape
     whole_s, whole_v = vmem((6, shape.rows, depth)), vmem((3, shape.rows, depth))
-    whole_b = vmem((shape.rows, depth))
-    stress_rows = max(len(entries(LOW_Y)), len(entries(HIGH_Y)))
-    all_rows = stress_rows + 5 + 2
-    stress_slots = max(x_slots(LOW_X, rows_y, True), x_slots(HIGH_X, rows_y, True))
-    flow_slots = (max(x_slots(LOW_FLOW_X, rows_y, False), x_slots(HIGH_FLOW_X, rows_y, False))
-                  + 2 * (rows_y // 8))
-
-    def buffers(axis, first_round):
-        if axis == "y":
-            return vmem((all_rows if first_round else stress_rows, rows_x, depth))
-        return vmem((stress_slots + (flow_slots if first_round else 0), 8, depth))
+    whole_b, whole_h = vmem((shape.rows, depth)), vmem((3, shape.rows, depth))
+    y_buffers = {first: vmem((y_count(first), rows_x, depth)) for first in (True, False)}
+    x_buffers = {first: vmem((x_count(shape, first), 8, depth)) for first in (True, False)}
 
     inner = (2, rows_x - 2)
     deep = (4, rows_x - 4)
+    next_inner = (6, rows_x - 6)
     bands = range(0, rows_y, 8)
 
-    def load(v_in, s_in, b_in, s, v, b, first, second, sems):
-        own = [own_cells(shape, ref) for ref in (s, v, b)]
-        run_copies(list(zip((s_in, v_in, b_in), own)), sems)
+    def own_forces(lanes, s, v, b, x):
+        for t in bands:
+            push_velocity(shape, lanes, s, v, b, aligned(shape, x, t))
+
+    def load(v_in, s_in, b_in, s, v, b, h, first, second, sems):
+        groups = []
+        for g, x in enumerate(range(0, rows_x, 8)):
+            group = []
+            for i, (source, ref) in enumerate(((s_in, s), (v_in, v), (b_in, b))):
+                part = source.at[:, pl.ds(x, 8)] if i < 2 else source.at[pl.ds(x, 8)]
+                place = own_cells(shape, ref, x, 8)
+                group.append(pltpu.make_async_copy(part, place, sems.at[g, i]))
+                group[-1].start()
+            groups.append(group)
+        zero = jnp.zeros((8, depth), jnp.float32)
+        for x in range(0, rows_x + 1):
+            for c in (XY, YY, YZ):
+                s[c, pl.ds(shape.row(x, -RIM), 8), :] = zero
+        for x in range(0, rows_x):
+            for t in bands:
+                for c in range(3):
+                    h[c, pl.ds(shape.row(x, t), 8), :] = zero
+        for x in (-2, -1, rows_x, rows_x + 1):
+            for t in bands:
+                for c in range(6):
+                    s[c, pl.ds(shape.row(x, t), 8), :] = zero
+        lanes = Lanes(depth)
+        done = 0
+        for g, group in enumerate(groups):
+            for copy in group:
+                copy.wait()
+            stop = rows_x if g == len(groups) - 1 else 8 * g + 6
+            layers(done, stop, lambda x: own_forces(lanes, s, v, b, x), stop - done)
+            done = stop
         send_y(shape, s, v, b, first, second)
 
-    s, v, b, first, second = call(
+    s, v, b, h, first, second = call(
         load,
         [velocity, stress, buoyancy],
         [in_hbm] * 3,
-        [whole_s, whole_v, whole_b, buffers("y", True), buffers("y", True)],
-        [in_vmem] * 5,
+        [whole_s, whole_v, whole_b, whole_h, y_buffers[True], y_buffers[True]],
+        [in_vmem] * 6,
         "load",
-        1000000,
-        scratch=[pltpu.SemaphoreType.DMA((3,))],
+        10000000,
+        scratch=[pltpu.SemaphoreType.DMA((rows_x // 8, 3))],
     )
 
-    def across(s, v, b):
-        lanes = Lanes(depth)
-
-        def layer(x):
-            for t in bands:
-                push_velocity(shape, lanes, s, v, b, aligned(shape, x, t), "xz")
-
-        layers(*inner, layer, 4)
-
-    def prepare(
-        v_in, s, b, lame_in, shear_in, zone_in, able_in, cohesion, friction, v, rock, zones, able, sems
-    ):
+    def prepare(after, lame_in, shear_in, zone_in, able_in, cohesion, friction, rock, zones, able, sems):
         flat = rock.reshape(5, rows_x, rows_y, depth)
         pairs = ((zone_in, zones), (able_in, able), (lame_in, flat.at[0]), (shear_in, flat.at[1]))
-        copies = [pltpu.make_async_copy(a, c, sems.at[i]) for i, (a, c) in enumerate(pairs)]
-        for c in copies:
-            c.start()
-        across(s, v, b)
-        for c in copies:
-            c.wait()
+        run_copies(pairs, sems)
 
         def layer(x):
             for t in bands:
@@ -461,34 +532,37 @@
 
         layers(0, rows_x, layer, 4)
 
-    def plain(v_in, s, b, v):
-        across(s, v, b)
-
-    def middle(s, v, b, rock, cell, moment):
+    rock = call(
+        prepare,
+        [b, lame_first, modulus, zone, eligible, cohesion, friction],
+        [in_vmem] + [in_hbm] * 4 + [in_smem] * 2,
+        vmem((5, rows_x * rows_y, depth)),
+        in_vmem,
+        "prepare",
+        10000000,
+        scratch=[
+            pltpu.VMEM((rows_x, rows_y, depth), jnp.int32),
+            pltpu.VMEM((rows_x, rows_y, depth), jnp.int32),
+            pltpu.SemaphoreType.DMA((4,)),
+        ],
+    )
+
+    def middle(s, v, b, h, rock, cell, moment):
         lanes = Lanes(depth)
+        halves = [h.at[c] for c in range(3)]
+        own = [s.at[c] for c in (XY, YY, YZ)]
 
         def layer(x):
             for t in bands:
-                push_velocity(shape, lanes, s, v, b, aligned(shape, x, t), "y")
-            push_velocity(shape, lanes, s, v, b, aligned(shape, x, -RIM), "xyz")
-
-        for t in bands:
-            push_velocity(shape, lanes, s, v, b, aligned(shape, inner[0], t), "y")
-        layers(inner[0] + 1, inner[1], layer, 4)
+                push_across_y(halves, v, b, aligned(shape, x, t))
+
+        layers(*inner, layer, 4)
+        layers(0, rows_x + 1, lambda x: push_across_y(own, v, b, aligned(shape, x, -RIM)), 3)
         inject(shape, s, cell, moment, lambda x: (x >= deep[0]) & (x < deep[1]))
         layers(*deep, lambda x: push_stress(shape, lanes, s, v, rock, x), 4)
 
-    def outer(s, v, b, rock, cell, moment, ready=None):
+    def outer(s, v, b, rock, cell, moment):
         lanes = Lanes(depth)
-        for low in (-2, inner[1]):
-            for x in range(low, low + 4):
-                for t in bands:
-                    push_velocity(shape, lanes, s, v, b, aligned(shape, x, t), "xyz")
-        for low in (0, inner[1]):
-            for x in range(low, low + 3):
-                push_velocity(shape, lanes, s, v, b, aligned(shape, x, -RIM), "xyz")
-        if ready is not None:
-            ready()
         rows = lambda x: (x >= 0) & (x < rows_x) & ((x < deep[0]) | (x >= deep[1]))
         inject(shape, s, cell, moment, rows)
         for low in (0, deep[1]):
@@ -505,64 +579,56 @@
         first, second = swaps("gy", first, second)
 
         if begin:
-            v, rock = call(
-                prepare,
-                [v, s, b, lame_first, modulus, zone, eligible, cohesion, friction],
-                [in_vmem] * 3 + [in_hbm] * 4 + [in_smem] * 2,
-                [whole_v, vmem((5, rows_x * rows_y, depth))],
-                [in_vmem] * 2,
-                "prepare",
-                10000000,
-                aliases={0: 0},
-                scratch=[
-                    pltpu.VMEM((rows_x, rows_y, depth), jnp.int32),
-                    pltpu.VMEM((rows_x, rows_y, depth), jnp.int32),
-                    pltpu.SemaphoreType.DMA((4,)),
-                ],
-            )
-
-            def turn(s_in, v_in, b_in, got_a, got_b, s, v, b, out_a, out_b):
-                receive_y(shape, s, v, b, got_a, got_b)
-                send_x(shape, s, v, b, out_a, out_b)
-
-            s, v, b, first, second = call(
+
+            def turn(s, v_in, b_in, h_in, got_a, got_b, v, b, h, out_a, out_b):
+                receive_y(shape, h, v, b, got_a, got_b)
+                for x in edge_layers(shape):
+                    for t in bands:
+                        push_across_y([h.at[c] for c in range(3)], v, b, shape.row(x, t))
+                send_x(shape, s, v, b, got_a, got_b, out_a, out_b)
+
+            v, b, h, first, second = call(
                 turn,
-                [s, v, b, first, second],
-                [in_vmem] * 5,
-                [whole_s, whole_v, whole_b, buffers("x", True), buffers("x", True)],
+                [s, v, b, h, first, second],
+                [in_vmem] * 6,
+                [whole_v, whole_b, whole_h, x_buffers[True], x_buffers[True]],
                 [in_vmem] * 5,
                 "turn_first",
                 1000000,
-                aliases={0: 0, 1: 1, 2: 2},
+                aliases={1: 0, 2: 1, 3: 2},
             )
         else:
-            v = call(plain, [v, s, b], [in_vmem] * 3, whole_v, in_vmem, "plain", 10000000, {0: 0})
-
-            def turn(s_in, got_a, got_b, s, out_a, out_b):
-                receive_y(shape, s, None, None, got_a, got_b)
-                send_x(shape, s, None, None, out_a, out_b)
-
-            s, first, second = call(
+
+            def turn(s, v_in, b, h_in, got_a, got_b, v, h, out_a, out_b):
+                receive_y(shape, h, v, None, got_a, got_b)
+                for x in edge_layers(shape):
+                    for t in bands:
+                        push_across_y([h.at[c] for c in range(3)], v, b, shape.row(x, t))
+                send_x(shape, s, v, None, got_a, got_b, out_a, out_b)
+
+            v, h, first, second = call(
                 turn,
-                [s, first, second],
-                [in_vmem] * 3,
-                [whole_s, buffers("x", False), buffers("x", False)],
-                [in_vmem] * 3,
+                [s, v, b, h, first, second],
+                [in_vmem] * 6,
+                [whole_v, whole_h, x_buffers[False], x_buffers[False]],
+                [in_vmem] * 4,
                 "turn",
                 1000000,
-                aliases={0: 0},
+                aliases={1: 0, 3: 1},
             )
         first, second = swaps("gx", first, second)
 
         if not end:
 
-            def interior(s_in, v_in, b, rock, cell, moment, s, v):
-                middle(s, v, b, rock, cell, moment)
+            def interior(s_in, v_in, b, h, rock, cell, moment, s, v):
+                middle(s, v, b, h, rock, cell, moment)
+                lanes = Lanes(depth)
+                layers(*next_inner, lambda x: own_forces(lanes, s, v, b, x), 4)
 
             s, v = call(
                 interior,
-                [s, v, b, rock] + cells,
-                [in_vmem] * 4 + [in_smem] * 2,
+                [s, v, b, h, rock] + cells,
+                [in_vmem] * 5 + [in_smem] * 2,
                 [whole_s, whole_v],
                 [in_vmem] * 2,
                 "interior",
@@ -571,15 +637,19 @@
             )
 
             def border(s_in, v_in, b_in, rock, got_a, got_b, cell, moment, s, v, b, out_a, out_b):
-                receive_x(shape, *((s, v, b) if begin else (s, None, None)), got_a, got_b)
+                receive_x(shape, s, v, b, begin, got_a, got_b)
                 outer(s, v, b, rock, cell, moment)
-                send_y(shape, s, None, None, out_a, out_b)
+                lanes = Lanes(depth)
+                for low in (0, next_inner[1]):
+                    for x in range(low, low + next_inner[0]):
+                        own_forces(lanes, s, v, b, x)
+                send_y(shape, s, v, None, out_a, out_b)
 
             s, v, b, first, second = call(
                 border,
                 [s, v, b, rock, first, second] + cells,
                 [in_vmem] * 6 + [in_smem] * 2,
-                [whole_s, whole_v, whole_b, buffers("y", False), buffers("y", False)],
+                [whole_s, whole_v, whole_b, y_buffers[False], y_buffers[False]],
                 [in_vmem] * 5,
                 "border",
                 10000000,
@@ -587,8 +657,8 @@
             )
         else:
 
-            def interior(s_in, v_in, b, rock, cell, moment, s, v, v_out, s_out, sems):
-                middle(s, v, b, rock, cell, moment)
+            def interior(s_in, v_in, b, h, rock, cell, moment, s, v, v_out, s_out, sems):
+                middle(s, v, b, h, rock, cell, moment)
                 pairs = []
                 for ref, out, (low, high) in ((v, v_out, inner), (s, s_out, deep)):
                     part = out.at[:, pl.ds(low, high - low)]
@@ -597,8 +667,8 @@
 
             s, v, v_out, s_out = call(
                 interior,
-                [s, v, b, rock] + cells,
-                [in_vmem] * 4 + [in_smem] * 2,
+                [s, v, b, h, rock] + cells,
+                [in_vmem] * 5 + [in_smem] * 2,
                 [whole_s, whole_v] + out_shapes,
                 [in_vmem] * 2 + [in_hbm] * 2,
                 "interior_last",
@@ -621,8 +691,10 @@
 
                 v_copies = copies(v, v_out, *inner, 0)
                 s_copies = copies(s, s_out, *deep, 2)
-                receive_x(shape, s, None, None, got_a, got_b)
-                outer(s, v, b, rock, cell, moment, lambda: [c.start() for c in v_copies])
+                receive_x(shape, s, v, b, begin, got_a, got_b)
+                for c in v_copies:
+                    c.start()
+                outer(s, v, b, rock, cell, moment)
                 for c in s_copies:
                     c.start()
                 for c in v_copies + s_copies:

time: 41.5 us -> 35.9 us (0.87)
  waiting for transfers between devices: 12.9 us -> 9.75 us
  Pallas kernels: 14.3 us -> 12.9 us
  starting transfers between devices: 11.9 us -> 10.9 us
    ppermute x8, waiting for transfers between devices: 12.9 us -> 9.75 us  [swaps(): got.append(lax.ppermute(block, axis, pairs))]
    pallas_call x9 -> x8, Pallas kernels: 14.3 us -> 12.9 us  [call(): pl.pallas_call(body, in_specs=in_specs, out_shape=out_shape, out_specs=ou...]
    ppermute x8, starting transfers between devices: 11.9 us -> 10.9 us  [swaps(): got.append(lax.ppermute(block, axis, pairs))]
where the time goes in v3:
time: 35.9 us; the launch traced here: 35.7 us
  Pallas kernels  12.9 us (36%)
  starting transfers between devices  10.9 us (30%)
  waiting for transfers between devices  9.75 us (27%)
  local copies, waits for them, and re-layouts  1.31 us (4%)
  between operations  0.8 us (2%)
    pallas_call x8, Pallas kernels, call(): pl.pallas_call(body, in_specs=in_specs, out_shape=out_shape, out_specs=ou...  12.9 us
    ppermute x8, starting transfers between devices, swaps(): got.append(lax.ppermute(block, axis, pairs))  10.9 us
    ppermute x8, waiting for transfers between devices, swaps(): got.append(lax.ppermute(block, axis, pairs))  9.75 us
    unnamed x8, local copies, waits for them, and re-layouts  1.31 us
  transfers between devices with their start and end apart: 8, of which 4 were waited for; matrix products, arithmetic and copies ran while one was open for 0% of the time, Pallas kernels for 21%

profile of v3, /device:TPU:12, one launch (start us, length us, event | category | flops | bytes accessed | tf_op | source)
XLA Modules:
  0.0 35.7 jit_solution(14326429822730652572)
XLA Ops:
  0.6 1.9 %load.1 = (f32[6,656,128]{2,1,0:T(8,128)S(1)}, f32[3,656,128]{2,1,0:T(8,128)S(1)}, f32[656,128]{1,0:T(8,128)S(1)}, f32[3,656,128]{2,1,0:T(8,128)S(1)}, f32[12,32...) custom-call(f32[3,32,8,128]{3,2,1,0:T(8,128)} %v_in.1, f32[6,32,8,128]{3,2,1,0:T(8,128)} %s_in.1, f32[32,8,128]{2,1,0:T(8,128)} %b_in.1), custom_call_target="tpu_custom_call" | custom-call | flops 10000000 | bytes 1000000 | tf_op jit(solution)/shard_map/load/pallas_call | solution.py:418
  2.5 0.1 collective-permute-start
  2.6 2.4 %collective-permute-start.1 = (f32[12,32,128]{2,1,0:T(8,128)S(1)}, f32[12,32,128]{2,1,0:T(8,128)S(1)}, u32[]{:S(2)}, u32[]{:S(2)}) collective-permute-start(f32[12,32,128]{2,1,0:T(8,128)S(1)} %get-tuple-element.35), channel_id=1, source_target_pairs={{1,2},{2,1},{3,4},{4,3},{5,6},{6,5},{9,10},{10,9},{11,12},{12,11},... | collective-permute-start | bytes 589832 | tf_op jit(solution)/shard_map/ppermute | solution.py:438
  5.0 0.0 copy-start.2
  5.0 0.6 %copy-done.2 = f32[8]{0:T(128)S(1)} copy-done((f32[8]{0:T(128)S(1)}, f32[8]{0:T(128)}, u32[]{:S(2)}) %copy-start.2) | copy-done | bytes 56
  5.7 0.0 copy-start.3
  5.7 0.7 %copy-done.3 = f32[8]{0:T(128)S(1)} copy-done((f32[8]{0:T(128)S(1)}, f32[8]{0:T(128)}, u32[]{:S(2)}) %copy-start.3) | copy-done | bytes 56
  6.3 1.9 %prepare.1.rock = f32[5,256,128]{2,1,0:T(8,128)S(1)} custom-call(f32[656,128]{1,0:T(8,128)S(1)} %get-tuple-element.32.b_in.after, f32[32,8,128]{2,1,0:T(8,128)} %lame_in.1, f32[32,8,128]{2,1,0:T(8,128)} %shear_in.1, s32[32,8,128]{2,1,0:T(8,128)} %zone_in.1, s32[32,8,128]{2,1,0:T(8,128)} %able_in.1, f32[8]{0:T(128)S(1)} %copy-done.2, f32[8]{0:T(128)S(1)} %copy-done.3), custom_call_target="tpu_custom_call" | custom-call | flops 10000000 | bytes 1000000 | tf_op jit(solution)/shard_map/prepare/pallas_call | solution.py:418
  8.2 0.0 collective-permute-done.got_a
  8.2 1.3 %collective-permute-done.1.got_b = f32[12,32,128]{2,1,0:T(8,128)S(1)} collective-permute-done((f32[12,32,128]{2,1,0:T(8,128)S(1)}, f32[12,32,128]{2,1,0:T(8,128)S(1)}, u32[]{:S(2)}, u32[]{:S(2)}) %collective-permute-start.1) | collective-permute-done | bytes 196640 | tf_op jit(solution)/shard_map/ppermute | solution.py:438
  9.6 0.0 copy-start
  9.6 0.0 copy-start.1
  9.6 0.2 turn_first.1
  9.8 1.6 %collective-permute-start.2 = (f32[16,8,128]{2,1,0:T(8,128)S(1)}, f32[16,8,128]{2,1,0:T(8,128)S(1)}, u32[]{:S(2)}, u32[]{:S(2)}) collective-permute-start(f32[16,8,128]{2,1,0:T(8,128)S(1)} %get-tuple-element.41), channel_id=1, source_target_pairs={{0,8},{8,0},{16,24},{24,16},{1,9},{9,1},{17,25},{25,17},{2,10},{10... | collective-permute-start | bytes 196616 | tf_op jit(solution)/shard_map/ppermute | solution.py:438
  11.3 2.4 %collective-permute-start.3 = (f32[16,8,128]{2,1,0:T(8,128)S(1)}, f32[16,8,128]{2,1,0:T(8,128)S(1)}, u32[]{:S(2)}, u32[]{:S(2)}) collective-permute-start(f32[16,8,128]{2,1,0:T(8,128)S(1)} %get-tuple-element.42), channel_id=1, source_target_pairs={{8,16},{16,8},{9,17},{17,9},{10,18},{18,10},{11,19},{19,11},{12,20... | collective-permute-start | bytes 196616 | tf_op jit(solution)/shard_map/ppermute | solution.py:438
  13.7 0.0 copy-done
  13.7 0.0 copy-done.1
  13.7 2.6 %interior.1 = (f32[6,656,128]{2,1,0:T(8,128)S(1)}, f32[3,656,128]{2,1,0:T(8,128)S(1)}) custom-call(f32[6,656,128]{2,1,0:T(8,128)S(1)} %get-tuple-element.30.s.s_in, f32[3,656,128]{2,1,0:T(8,128)S(1)} %get-tuple-element.36.v_in, f32[656,128]{1,0:T(8,128)S(1)} %get-tuple-element.37.b.b_in, ...), custom_call_target="tpu_custom_call", output_to_operand_aliasing={{0}: (0, {}), {1}: (1, {})} | custom-call | flops 10000000 | bytes 1000000 | tf_op jit(solution)/shard_map/interior/pallas_call | solution.py:418
  16.3 0.0 collective-permute-done.2.got_a
  16.4 2.0 %collective-permute-done.3.got_b = f32[16,8,128]{2,1,0:T(8,128)S(1)} collective-permute-done((f32[16,8,128]{2,1,0:T(8,128)S(1)}, f32[16,8,128]{2,1,0:T(8,128)S(1)}, u32[]{:S(2)}, u32[]{:S(2)}) %collective-permute-start.3) | collective-permute-done | bytes 65568 | tf_op jit(solution)/shard_map/ppermute | solution.py:438
  18.4 1.3 %border.1 = (f32[6,656,128]{2,1,0:T(8,128)S(1)}, f32[3,656,128]{2,1,0:T(8,128)S(1)}, f32[656,128]{1,0:T(8,128)S(1)}, f32[10,32,128]{2,1,0:T(8,128)S(1)}, f32[10,32,128]{2,1,0:T(8,128)S(1)}) custom-call(f32[6,656,128]{2,1,0:T(8,128)S(1)} %get-tuple-element.39.s_in, ...), custom_call_target="tpu_custom_call", output_to_operand_aliasing={{0}: (0, {}), {1}: (1, {}), {2}: (2, {})} | custom-call | flops 10000000 | bytes 1000000 | tf_op jit(solution)/shard_map/border/pallas_call | solution.py:418
  19.7 0.1 collective-permute-start.4
  19.8 1.9 %collective-permute-start.5 = (f32[10,32,128]{2,1,0:T(8,128)S(1)}, f32[10,32,128]{2,1,0:T(8,128)S(1)}, u32[]{:S(2)}, u32[]{:S(2)}) collective-permute-start(f32[10,32,128]{2,1,0:T(8,128)S(1)} %get-tuple-element.47), channel_id=1, source_target_pairs={{1,2},{2,1},{3,4},{4,3},{5,6},{6,5},{9,10},{10,9},{11,12},{12,11},... | collective-permute-start | bytes 491528 | tf_op jit(solution)/shard_map/ppermute | solution.py:438
  21.8 0.0 collective-permute-done.4.got_a
  21.8 4.7 %collective-permute-done.5.got_b = f32[10,32,128]{2,1,0:T(8,128)S(1)} collective-permute-done((f32[10,32,128]{2,1,0:T(8,128)S(1)}, f32[10,32,128]{2,1,0:T(8,128)S(1)}, u32[]{:S(2)}, u32[]{:S(2)}) %collective-permute-start.5) | collective-permute-done | bytes 163872 | tf_op jit(solution)/shard_map/ppermute | solution.py:438
  26.5 0.2 turn.1
  26.7 0.1 collective-permute-start.6
  26.7 2.4 %collective-permute-start.7 = (f32[14,8,128]{2,1,0:T(8,128)S(1)}, f32[14,8,128]{2,1,0:T(8,128)S(1)}, u32[]{:S(2)}, u32[]{:S(2)}) collective-permute-start(f32[14,8,128]{2,1,0:T(8,128)S(1)} %get-tuple-element.53), channel_id=1, source_target_pairs={{8,16},{16,8},{9,17},{17,9},{10,18},{18,10},{11,19},{19,11},{12,20... | collective-permute-start | bytes 172040 | tf_op jit(solution)/shard_map/ppermute | solution.py:438
  29.1 3.0 %interior_last.1 = (f32[6,656,128]{2,1,0:T(8,128)S(1)}, f32[3,656,128]{2,1,0:T(8,128)S(1)}, f32[3,32,8,128]{3,2,1,0:T(8,128)}, f32[6,32,8,128]{3,2,1,0:T(8,128)}) custom-call(f32[6,656,128]{2,1,0:T(8,128)S(1)} %get-tuple-element.43.s.s_in, f32[3,656,128]{2,1,0:T(8,128)S(1)} %get-tuple-element.48.v_in, ...), custom_call_target="tpu_custom_call", output_to_operand_aliasing={{0}: (0, {}), {1}: (1, {})} | custom-call | flops 10000000 | bytes 1000000 | tf_op jit(solution)/shard_map/interior_last/pallas_call | solution.py:418
  32.1 0.0 collective-permute-done.6.got_a
  32.1 1.7 %collective-permute-done.7.got_b = f32[14,8,128]{2,1,0:T(8,128)S(1)} collective-permute-done((f32[14,8,128]{2,1,0:T(8,128)S(1)}, f32[14,8,128]{2,1,0:T(8,128)S(1)}, u32[]{:S(2)}, u32[]{:S(2)}) %collective-permute-start.7) | collective-permute-done | bytes 57376 | tf_op jit(solution)/shard_map/ppermute | solution.py:438
  33.8 1.8 %border_last.1 = (f32[6,656,128]{2,1,0:T(8,128)S(1)}, f32[3,656,128]{2,1,0:T(8,128)S(1)}, f32[3,32,8,128]{3,2,1,0:T(8,128)}, f32[6,32,8,128]{3,2,1,0:T(8,128)}) custom-call(f32[6,656,128]{2,1,0:T(8,128)S(1)} %get-tuple-element.50.s_in, ...), custom_call_target="tpu_custom_call", output_to_operand_aliasing={{0}: (0, {}), {1}: (1, {}), {2}: (8, {}), {3}: (9, {})} | custom-call | flops 10000000 | bytes 1000000 | tf_op jit(solution)/shard_map/border_last/pallas_call | solution.py:418
Async XLA Ops:
  2.5 5.7 %collective-permute-start = (f32[12,32,128]{2,1,0:T(8,128)S(1)}, f32[12,32,128]{2,1,0:T(8,128)S(1)}, u32[]{:S(2)}, u32[]{:S(2)}) collective-permute-start(f32[12,32,128]{2,1,0:T(8,128)S(1)} %get-tuple-element.34), channel_id=1, source_target_pairs={{0,1},{1,0},{2,3},{3,2},{4,5},{5,4},{6,7},{7,6},{8,9},{9,8},{10,11... | collective-permute-start | bytes 589832 | tf_op jit(solution)/shard_map/ppermute | solution.py:438
  2.6 7.0 %collective-permute-start.1 = (f32[12,32,128]{2,1,0:T(8,128)S(1)}, f32[12,32,128]{2,1,0:T(8,128)S(1)}, u32[]{:S(2)}, u32[]{:S(2)}) collective-permute-start(f32[12,32,128]{2,1,0:T(8,128)S(1)} %get-tuple-element.35), channel_id=1, source_target_pairs={{1,2},{2,1},{3,4},{4,3},{5,6},{6,5},{9,10},{10,9},{11,12},{12,11},... | collective-permute-start | bytes 589832 | tf_op jit(solution)/shard_map/ppermute | solution.py:438
  5.0 0.7 %copy-start.2 = (f32[8]{0:T(128)S(1)}, f32[8]{0:T(128)}, u32[]{:S(2)}) copy-start(f32[8]{0:T(128)} %cohesion.1) | copy-start | bytes 100
  5.7 0.7 %copy-start.3 = (f32[8]{0:T(128)S(1)}, f32[8]{0:T(128)}, u32[]{:S(2)}) copy-start(f32[8]{0:T(128)} %friction.1) | copy-start | bytes 100
  9.6 4.2 %copy-start = (f32[6,16]{1,0:T(8,128)S(1)}, f32[6,16]{1,0:T(8,128)}, u32[]{:S(2)}) copy-start(f32[6,16]{1,0:T(8,128)} %moment.7) | copy-start | bytes 1156
  9.6 4.2 %copy-start.1 = (s32[16]{0:T(128)S(1)}, s32[16]{0:T(128)}, u32[]{:S(2)}) copy-start(s32[16]{0:T(128)} %cell.7) | copy-start | bytes 196
  9.8 6.6 %collective-permute-start.2 = (f32[16,8,128]{2,1,0:T(8,128)S(1)}, f32[16,8,128]{2,1,0:T(8,128)S(1)}, u32[]{:S(2)}, u32[]{:S(2)}) collective-permute-start(f32[16,8,128]{2,1,0:T(8,128)S(1)} %get-tuple-element.41), channel_id=1, source_target_pairs={{0,8},{8,0},{16,24},{24,16},{1,9},{9,1},{17,25},{25,17},{2,10},{10... | collective-permute-start | bytes 196616 | tf_op jit(solution)/shard_map/ppermute | solution.py:438
  11.3 7.0 %collective-permute-start.3 = (f32[16,8,128]{2,1,0:T(8,128)S(1)}, f32[16,8,128]{2,1,0:T(8,128)S(1)}, u32[]{:S(2)}, u32[]{:S(2)}) collective-permute-start(f32[16,8,128]{2,1,0:T(8,128)S(1)} %get-tuple-element.42), channel_id=1, source_target_pairs={{8,16},{16,8},{9,17},{17,9},{10,18},{18,10},{11,19},{19,11},{12,20... | collective-permute-start | bytes 196616 | tf_op jit(solution)/shard_map/ppermute | solution.py:438
  19.7 2.0 %collective-permute-start.4 = (f32[10,32,128]{2,1,0:T(8,128)S(1)}, f32[10,32,128]{2,1,0:T(8,128)S(1)}, u32[]{:S(2)}, u32[]{:S(2)}) collective-permute-start(f32[10,32,128]{2,1,0:T(8,128)S(1)} %get-tuple-element.46), channel_id=1, source_target_pairs={{0,1},{1,0},{2,3},{3,2},{4,5},{5,4},{6,7},{7,6},{8,9},{9,8},{10,11... | collective-permute-start | bytes 491528 | tf_op jit(solution)/shard_map/ppermute | solution.py:438
  19.8 6.6 %collective-permute-start.5 = (f32[10,32,128]{2,1,0:T(8,128)S(1)}, f32[10,32,128]{2,1,0:T(8,128)S(1)}, u32[]{:S(2)}, u32[]{:S(2)}) collective-permute-start(f32[10,32,128]{2,1,0:T(8,128)S(1)} %get-tuple-element.47), channel_id=1, source_target_pairs={{1,2},{2,1},{3,4},{4,3},{5,6},{6,5},{9,10},{10,9},{11,12},{12,11},... | collective-permute-start | bytes 491528 | tf_op jit(solution)/shard_map/ppermute | solution.py:438
  26.7 5.5 %collective-permute-start.6 = (f32[14,8,128]{2,1,0:T(8,128)S(1)}, f32[14,8,128]{2,1,0:T(8,128)S(1)}, u32[]{:S(2)}, u32[]{:S(2)}) collective-permute-start(f32[14,8,128]{2,1,0:T(8,128)S(1)} %get-tuple-element.52), channel_id=1, source_target_pairs={{0,8},{8,0},{16,24},{24,16},{1,9},{9,1},{17,25},{25,17},{2,10},{10... | collective-permute-start | bytes 172040 | tf_op jit(solution)/shard_map/ppermute | solution.py:438
  26.7 7.1 %collective-permute-start.7 = (f32[14,8,128]{2,1,0:T(8,128)S(1)}, f32[14,8,128]{2,1,0:T(8,128)S(1)}, u32[]{:S(2)}, u32[]{:S(2)}) collective-permute-start(f32[14,8,128]{2,1,0:T(8,128)S(1)} %get-tuple-element.53), channel_id=1, source_target_pairs={{8,16},{16,8},{9,17},{17,9},{10,18},{18,10},{11,19},{19,11},{12,20... | collective-permute-start | bytes 172040 | tf_op jit(solution)/shard_map/ppermute | solution.py:438

commit v4 on v3

v4 whole, which is shorter than its diff:
```python
import jax
import jax.numpy as jnp
from jax import lax
from jax.experimental import pallas as pl
from jax.experimental.pallas import tpu as pltpu
from jax.sharding import PartitionSpec as P


time_step = 0.1
near_weight = 9.0 / 8.0
far_weight = 1.0 / 24.0
shear_floor = 0.25

XX, YY, ZZ, XY, XZ, YZ = range(6)

LOW_Y = ((XY, 2), (YY, 1), (YZ, 2))
HIGH_Y = ((XY, 1), (YY, 2), (YZ, 1))
LOW_X = ((XX, 1), (XY, 2), (XZ, 2))
HIGH_X = ((XX, 2), (XY, 1), (XZ, 1))
LOW_FLOW_Y = ((0, 1), (1, 2), (2, 1))
HIGH_FLOW_Y = ((0, 2), (1, 1), (2, 2))
BESIDE = 3
LOW_DEEP_X = ((0, 5), (1, 4), (2, 4))
HIGH_DEEP_X = ((0, 4), (1, 5), (2, 5))
DRIVES = (XX, XY, XZ)

PAD_X = 8
RIM = 8


class Shape:
    def __init__(self, rows_x, rows_y, depth):
        self.rows_x, self.rows_y, self.depth = rows_x, rows_y, depth
        self.pitch = rows_y + RIM
        self.rows = (rows_x + 2 * PAD_X + 1) * self.pitch

    def row(self, x, y):
        return (x + PAD_X) * self.pitch + RIM + y


def entries(spec):
    return [(c, k) for c, depth in spec for k in range(depth)]


def pack_y(shape, pairs, out):
    for slot, (ref, y) in enumerate(pairs):
        for x in range(0, shape.rows_x, 8):
            out[slot, pl.ds(x, 8), :] = ref[pl.ds(shape.row(x, y), 8, stride=shape.pitch), :]


def unpack_y(shape, pairs, got):
    for slot, (ref, y) in enumerate(pairs):
        for x in range(0, shape.rows_x, 8):
            ref[pl.ds(shape.row(x, y), 8, stride=shape.pitch), :] = got[slot, pl.ds(x, 8), :]


def y_list(fields, spec, flow_spec, place):
    halo, flow, buoyancy = fields
    pairs = [(halo[c], place(k)) for c, k in entries(spec)]
    pairs += [(flow.at[c], place(k)) for c, k in entries(flow_spec)]
    if buoyancy is not None:
        pairs += [(buoyancy, place(k)) for k in range(2)]
    return pairs


def edge_layers(shape):
    return (0, 1, shape.rows_x - 2, shape.rows_x - 1)


def beside_layers(shape):
    return (-2, -1, shape.rows_x, shape.rows_x + 1)


def pack_singles(shape, stress, layers_x, rows, out):
    for i, x in enumerate(layers_x):
        for j, (c, y) in enumerate(rows):
            out[pl.ds(8 * i + j, 1), :] = stress[c, pl.ds(shape.row(x, y), 1), :]


def by_parity(axis, body, *swapped):
    odd = lax.axis_index(axis) % 2

    @pl.when(odd == 0)
    def _():
        body(*[r for first, second in swapped for r in (second, first)])

    @pl.when(odd == 1)
    def _():
        body(*[r for first, second in swapped for r in (first, second)])


def send_y(shape, stress, flow, buoyancy, first, second):
    fields = ({c: stress.at[c] for c in range(6)}, flow, buoyancy)

    def fill(out, spec, flow_spec, place):
        pack_y(shape, y_list(fields, spec, flow_spec, place), out)
        if buoyancy is None:
            layers_x, rows = beside_layers(shape), [(c, place(k)) for c, k in entries(spec)]
        else:
            layers_x = edge_layers(shape)
            rows = [(DRIVES[c], place(k)) for c, k in entries(flow_spec)]
        pack_singles(shape, stress, layers_x, rows, out.at[out.shape[0] - 1])

    def body(below, above):
        fill(above, LOW_Y, LOW_FLOW_Y, lambda k: shape.rows_y - 1 - k)
        fill(below, HIGH_Y, HIGH_FLOW_Y, lambda k: k)

    by_parity("gy", body, (first, second))


def receive_y(shape, halo, flow, buoyancy, first, second):
    halves = {c: halo.at[i] for i, c in enumerate((XY, YY, YZ))}
    fields = (halves, flow, buoyancy)

    def take(got, spec, flow_spec, place):
        unpack_y(shape, y_list(fields, spec, flow_spec, place), got)
        if buoyancy is None:
            for i, x in enumerate(beside_layers(shape)):
                for j, (c, k) in enumerate(entries(spec)):
                    single = got[got.shape[0] - 1, pl.ds(8 * i + j, 1), :]
                    halves[c][pl.ds(shape.row(x, place(k)), 1), :] = single

    def body(below, above):
        take(below, LOW_Y, LOW_FLOW_Y, lambda k: -1 - k)
        take(above, HIGH_Y, HIGH_FLOW_Y, lambda k: shape.rows_y + k)

    by_parity("gy", body, (first, second))


def y_count(first_round):
    most = max(
        len(entries(spec)) + len(entries(flow_spec))
        for spec, flow_spec in ((LOW_Y, LOW_FLOW_Y), (HIGH_Y, HIGH_FLOW_Y))
    )
    return most + 1 + (2 if first_round else 0)


def x_slots(shape, side):
    spec, flow_spec = ((LOW_X, LOW_DEEP_X), (HIGH_X, HIGH_DEEP_X))[side]
    bands = range(0, shape.rows_y, 8)
    keys = [("v", c, k, t) for c, k in entries(flow_spec) for t in bands]
    keys += [("v", c, k, "rim") for c in range(3) for k in range(BESIDE)]
    keys += [("b", 0, k, "rim") for k in range(2)]
    keys += [("s", c, k, "rim") for c, k in entries(spec)]
    return {key: i for i, key in enumerate(keys)}


def x_count(shape):
    return max(len(x_slots(shape, side)) for side in (0, 1))


def early_slots(shape):
    bands = range(0, shape.rows_y, 8)
    keys = [("s", c, k, t) for c in range(6) for k in range(BESIDE) for t in bands]
    keys += [("r", c, k, t) for c in range(4) for k in range(BESIDE) for t in bands]
    keys += [("b", 0, k, t) for k in range(2) for t in bands]
    return {key: i for i, key in enumerate(keys)}


def send_early(shape, stress, buoyancy, raw, first, second):
    def fill(out, side, place):
        for (kind, c, k, t), slot in early_slots(shape).items():
            x = place(k)
            if kind == "r":
                at = x - (shape.rows_x - BESIDE if side == 0 else 0)
                out[slot] = raw(c, side, at, t)
            else:
                out[slot] = tile(stress.at[c] if kind == "s" else buoyancy, shape.row(x, t))

    def body(below, above):
        fill(above, 0, lambda k: shape.rows_x - 1 - k)
        fill(below, 1, lambda k: k)

    by_parity("gx", body, (first, second))


def receive_early(shape, stress, buoyancy, rock, cohesion, friction, first, second):
    slots = early_slots(shape)

    def take(got, place):
        for (kind, c, k, t), slot in slots.items():
            x = place(k)
            if kind == "s":
                stress[c, pl.ds(shape.row(x, t), 8), :] = got[slot]
            elif kind == "b":
                buoyancy[pl.ds(shape.row(x, t), 8), :] = got[slot]
            elif c == 0:
                raw = [got[slots["r", i, k, t]] for i in range(4)]
                fill_rock(shape, rock, x, t, cohesion, friction, *raw[2:])
                for i in range(2):
                    rock[i, pl.ds((x + BESIDE) * shape.rows_y + t, 8), :] = raw[i]

    def body(below, above):
        take(below, lambda k: -1 - k)
        take(above, lambda k: shape.rows_x + k)

    by_parity("gx", body, (first, second))


def fill_rock(shape, rock, x, t, cohesion, friction, which, able):
    hold = jnp.full((8, shape.depth), cohesion[0], jnp.float32)
    rub = jnp.full((8, shape.depth), friction[0], jnp.float32)
    for k in range(1, cohesion.shape[0]):
        hit = which == k
        hold = jnp.where(hit, cohesion[k], hold)
        rub = jnp.where(hit, friction[k], rub)
    own = pl.multiple_of((x + BESIDE) * shape.rows_y + t, 8)
    rock[2, pl.ds(own, 8), :] = hold * jnp.sqrt(1.0 - rub * rub)
    rock[3, pl.ds(own, 8), :] = rub
    rock[4, pl.ds(own, 8), :] = jnp.where(able == 1, 1.0, 0.0)


def rim_tile(shape, ref, x, sub):
    after, before = tile(ref, shape.row(x + 1, -RIM)), tile(ref, shape.row(x, -RIM))
    return jnp.where(sub < 4, after, before)


def send_x(shape, flow, buoyancy, got_first, got_second, first, second):
    layer_at = {x: i for i, x in enumerate(edge_layers(shape))}
    sub = lax.broadcasted_iota(jnp.int32, (8, shape.depth), 0)

    def fill(out, side, place, got_below, got_above):
        for (kind, c, k, t), slot in x_slots(shape, side).items():
            x = place(k)
            if kind == "s" and t == "rim":
                for got, rims, at in (
                    (got_above, HIGH_FLOW_Y, lambda d: d),
                    (got_below, LOW_FLOW_Y, lambda d: 7 - d),
                ):
                    for j, (which, depth) in enumerate(entries(rims)):
                        if DRIVES[which] == c:
                            single = got[got.shape[0] - 1, pl.ds(8 * layer_at[x] + j, 1), :]
                            out[slot, pl.ds(at(depth), 1), :] = single
            else:
                ref = flow.at[c] if kind == "v" else buoyancy
                if t == "rim":
                    out[slot] = rim_tile(shape, ref, x, sub)
                else:
                    out[slot] = tile(ref, shape.row(x, t))

    def with_corners(got_below, got_above):
        def body(below, above):
            fill(above, 0, lambda k: shape.rows_x - 1 - k, got_below, got_above)
            fill(below, 1, lambda k: k, got_below, got_above)

        by_parity("gx", body, (first, second))

    by_parity("gy", with_corners, (got_first, got_second))


NEAR, FAR = near_weight, far_weight
UP = {1: NEAR, 0: -NEAR, 2: -FAR, -1: FAR}
DOWN = {0: NEAR, -1: -NEAR, 1: -FAR, -2: FAR}


def crossing(c, x, sources):
    total = None
    for step, weight in (UP if c == 0 else DOWN).items():
        if x + step in sources:
            term = weight * sources[x + step]()
            total = term if total is None else total + term
    return total


def receive_x(shape, stress, flow, buoyancy, got, sent):
    rows_x, depth = shape.rows_x, shape.depth
    sub = lax.broadcasted_iota(jnp.int32, (8, depth), 0)
    zero = jnp.zeros((8, depth), jnp.float32)

    def add(c, row, force):
        flow[c, pl.ds(row, 8), :] += time_step * tile(buoyancy, row) * force

    def body(below, above, sent_below, sent_above):
        def read(sides):
            return {
                (kind, c, place(k), t): (ref, slot)
                for ref, side, place in sides
                for (kind, c, k, t), slot in x_slots(shape, side).items()
            }

        came = read(((below, 0, lambda k: -1 - k), (above, 1, lambda k: rows_x + k)))
        went = read(((sent_above, 0, lambda k: rows_x - 1 - k), (sent_below, 1, lambda k: k)))

        def rims(of, c):
            return {
                x: (lambda ref=ref, slot=slot: ref[slot])
                for (kind, which, x, t), (ref, slot) in of.items()
                if (kind, which, t) == ("s", DRIVES[c], "rim")
            }

        for (kind, c, x, t), (ref, slot) in came.items():
            if t != "rim":
                flow[c, pl.ds(shape.row(x, t), 8), :] = ref[slot]
        for t in range(0, shape.rows_y, 8):
            for c in range(3):
                there = {
                    x: (lambda x=x: tile(stress.at[DRIVES[c]], shape.row(x, t)))
                    for x in edge_layers(shape) + beside_layers(shape)
                }
                inside = {x: there[x] for x in edge_layers(shape)}
                outside = {x: there[x] for x in beside_layers(shape)}
                for targets, sources in ((inside, outside), (outside, inside)):
                    for x in targets:
                        force = crossing(c, x, sources)
                        if force is not None:
                            add(c, shape.row(x, t), force)
        for c in range(3):
            halo, own = rims(came, c), rims(went, c)
            forces = {x: crossing(c, x, halo) for x in edge_layers(shape)}
            for x in sorted({x + d for x in edge_layers(shape) for d in (0, 1)}):
                high, low = forces.get(x - 1), forces.get(x)
                if high is None and low is None:
                    continue
                high, low = (zero if f is None else f for f in (high, low))
                add(c, shape.row(x, -RIM), jnp.where(sub < 4, high, low))
            for x in [d for k in range(BESIDE) for d in (-1 - k, rows_x + k)]:
                ref, slot = came["v", c, x, "rim"]
                value = ref[slot]
                force = crossing(c, x, own)
                if force is not None:
                    ref, slot = came["b", 0, x, "rim"]
                    value = value + time_step * ref[slot] * force
                flow[c, pl.ds(shape.row(x + 1, -RIM), 4), :] = value[0:4]
                flow[c, pl.ds(shape.row(x, -4), 4), :] = value[4:8]

    by_parity("gx", body, got, sent)


class Lanes:
    def __init__(self, depth):
        self.depth = depth
        lane = lax.broadcasted_iota(jnp.int32, (8, depth), 1)
        zero = jnp.zeros((8, depth), jnp.float32)
        near = jnp.full((8, depth), near_weight, jnp.float32)
        far = jnp.full((8, depth), far_weight, jnp.float32)
        self.f_up = jnp.where(lane < depth - 1, near, zero)
        self.f_up2 = jnp.where(lane < depth - 2, far, zero)
        self.f_down = jnp.where(lane > 0, far, zero)
        self.b_down = jnp.where(lane > 0, near, zero)
        self.b_down2 = jnp.where(lane > 1, far, zero)
        self.b_up = jnp.where(lane < depth - 1, far, zero)

    def forward(self, f):
        up, up2, down = (pltpu.roll(f, s % self.depth, 1) for s in (-1, -2, 1))
        return (self.f_up * up - near_weight * f) - (self.f_up2 * up2 - self.f_down * down)

    def backward(self, f):
        up, down, down2 = (pltpu.roll(f, s % self.depth, 1) for s in (-1, 1, 2))
        return (near_weight * f - self.b_down * down) - (self.b_up * up - self.b_down2 * down2)


def forward(ref, row, step):
    a, b, c, d = (ref[pl.ds(row + k * step, 8), :] for k in (-1, 0, 1, 2))
    return near_weight * (c - b) - far_weight * (d - a)


def backward(ref, row, step):
    a, b, c, d = (ref[pl.ds(row + k * step, 8), :] for k in (-2, -1, 0, 1))
    return near_weight * (c - b) - far_weight * (d - a)


def tile(ref, row):
    return ref[pl.ds(row, 8), :]


def push_velocity(shape, lanes, stress, flow, buoyancy, row, along="xyz"):
    sx, sy = shape.pitch, 1
    xx, yy, zz, xy, xz, yz = (stress.at[c] for c in range(6))
    parts = {
        "x": lambda: (forward(xx, row, sx), backward(xy, row, sx), backward(xz, row, sx)),
        "y": lambda: (backward(xy, row, sy), forward(yy, row, sy), backward(yz, row, sy)),
        "z": lambda: (
            lanes.backward(tile(xz, row)),
            lanes.backward(tile(yz, row)),
            lanes.forward(tile(zz, row)),
        ),
    }
    force = parts[along[0]]()
    for axis in along[1:]:
        force = [f + g for f, g in zip(force, parts[axis]())]
    scale = time_step * tile(buoyancy, row)
    for c in range(3):
        flow[c, pl.ds(row, 8), :] += scale * force[c]


def push_across_y(halves, flow, buoyancy, row):
    xy, yy, yz = halves
    force = (backward(xy, row, 1), forward(yy, row, 1), backward(yz, row, 1))
    scale = time_step * tile(buoyancy, row)
    for c in range(3):
        flow[c, pl.ds(row, 8), :] += scale * force[c]


def layers(first, stop, body, unroll):
    def run(x, carry):
        body(x)
        return carry

    lax.fori_loop(first, stop, run, 0, unroll=unroll)


def aligned(shape, x, y):
    return pl.multiple_of((x + PAD_X) * shape.pitch + RIM + y, 8)


def inject(shape, stress, source_cell, source_moment, wanted):
    rows_x, rows_y, depth = shape.rows_x, shape.rows_y, shape.depth
    total_y = rows_y * lax.axis_size("gy")
    start_x = lax.axis_index("gx") * rows_x
    start_y = lax.axis_index("gy") * rows_y
    sub = lax.broadcasted_iota(jnp.int32, (8, depth), 0)
    lane = lax.broadcasted_iota(jnp.int32, (8, depth), 1)
    for s in range(source_cell.shape[0]):
        cell = source_cell[s]
        line = lax.div(cell, depth)
        x = lax.div(line, total_y) - start_x
        y = lax.rem(line, total_y) - start_y
        z = lax.rem(cell, depth)

        @pl.when(wanted(x) & (y >= 0) & (y < rows_y))
        def _(x=x, y=y, z=z, s=s):
            band = lax.div(y, 8) * 8
            row = aligned(shape, x, band)
            here = (sub == y - band) & (lane == z)
            for c in range(6):
                amount = time_step * source_moment[c, s]
                stress[c, pl.ds(row, 8), :] += jnp.where(here, amount, 0.0)


def push_stress(shape, lanes, stress, flow, rock, x):
    sx, sy = shape.pitch, 1
    vx, vy, vz = (flow.at[c] for c in range(3))

    for t in range(0, shape.rows_y, 8):
        row = aligned(shape, x, t)
        own = pl.multiple_of((x + BESIDE) * shape.rows_y + t, 8)
        first = time_step * rock[0, pl.ds(own, 8), :]
        shear = time_step * rock[1, pl.ds(own, 8), :]
        strain_x = backward(vx, row, sx)
        strain_y = backward(vy, row, sy)
        here_z = tile(vz, row)
        strain_z = lanes.backward(here_z)
        volume = first * (strain_x + strain_y + strain_z)
        twice = 2.0 * shear
        xx = tile(stress.at[XX], row) + (volume + twice * strain_x)
        yy = tile(stress.at[YY], row) + (volume + twice * strain_y)
        zz = tile(stress.at[ZZ], row) + (volume + twice * strain_z)
        xy = tile(stress.at[XY], row) + shear * (forward(vx, row, sy) + forward(vy, row, sx))
        xz = tile(stress.at[XZ], row) + shear * (
            lanes.forward(tile(vx, row)) + forward(vz, row, sx)
        )
        yz = tile(stress.at[YZ], row) + shear * (
            lanes.forward(tile(vy, row)) + forward(vz, row, sy)
        )
        pressure = (xx + yy + zz) * (1.0 / 3.0)
        dx, dy, dz = xx - pressure, yy - pressure, zz - pressure
        second = 0.5 * (dx * dx + dy * dy + dz * dz) + xy * xy + xz * xz + yz * yz
        strength = jnp.maximum(
            rock[2, pl.ds(own, 8), :] - pressure * rock[3, pl.ds(own, 8), :], 0.0
        )
        ratio = strength * lax.rsqrt(jnp.maximum(second, shear_floor * shear_floor))
        factor = jnp.where(rock[4, pl.ds(own, 8), :] > 0.5, jnp.minimum(ratio, 1.0), 1.0)
        stress[XX, pl.ds(row, 8), :] = pressure + factor * dx
        stress[YY, pl.ds(row, 8), :] = pressure + factor * dy
        stress[ZZ, pl.ds(row, 8), :] = pressure + factor * dz
        stress[XY, pl.ds(row, 8), :] = factor * xy
        stress[XZ, pl.ds(row, 8), :] = factor * xz
        stress[YZ, pl.ds(row, 8), :] = factor * yz


def own_cells(shape, ref, first=0, count=None):
    lead = ref.shape[:-2]
    view = ref.reshape(*lead, shape.rows_x + 2 * PAD_X + 1, shape.pitch, shape.depth)
    count = shape.rows_x - first if count is None else count
    return view.at[
        (slice(None),) * len(lead) + (pl.ds(PAD_X + first, count), pl.ds(RIM, shape.rows_y))
    ]


def run_copies(pairs, sems):
    copies = [pltpu.make_async_copy(a, b, sems.at[i]) for i, (a, b) in enumerate(pairs)]
    for c in copies:
        c.start()
    for c in copies:
        c.wait()


def vmem(shape):
    return pltpu.VMEM(shape, jnp.float32)


in_vmem = pl.BlockSpec(memory_space=pltpu.VMEM)
in_smem = pl.BlockSpec(memory_space=pltpu.SMEM)
in_hbm = pl.BlockSpec(memory_space=pltpu.HBM)


def call(body, ins, in_specs, out_shape, out_specs, flops, aliases=None, scratch=()):
    space = {id(in_vmem): pltpu.VMEM, id(in_hbm): pltpu.HBM}
    ins = [
        pltpu.with_memory_space_constraint(x, space[id(s)]) if id(s) in space else x
        for x, s in zip(ins, in_specs)
    ]
    return pl.pallas_call(
        body,
        in_specs=in_specs,
        out_shape=out_shape,
        out_specs=out_specs,
        input_output_aliases=aliases or {},
        scratch_shapes=scratch,
        cost_estimate=pl.CostEstimate(flops=flops, bytes_accessed=1000000, transcendentals=0),
        compiler_params=pltpu.CompilerParams(vmem_limit_bytes=16 * 1024 * 1024),
    )(*ins)


def swaps(axis, first, second):
    count = lax.axis_size(axis)
    got = []
    for start, block in ((0, first), (1, second)):
        pairs = []
        for low in range(start, count - 1, 2):
            pairs += [(low, low + 1), (low + 1, low)]
        got.append(lax.ppermute(block, axis, pairs))
    return got


def steps(
    velocity,
    stress,
    lame_first,
    modulus,
    buoyancy,
    zone,
    eligible,
    cohesion,
    friction,
    source_cell,
    source_moment,
):
    shape = Shape(*zone.shape)
    rows_x, rows_y, depth = zone.shape
    whole_s, whole_v = vmem((6, shape.rows, depth)), vmem((3, shape.rows, depth))
    whole_b, whole_h = vmem((shape.rows, depth)), vmem((3, shape.rows, depth))
    y_buffers = {first: vmem((y_count(first), rows_x, depth)) for first in (True, False)}
    x_buffer = vmem((x_count(shape), 8, depth))
    early_buffer = vmem((len(early_slots(shape)), 8, depth))
    whole_r = vmem((5, (rows_x + 2 * BESIDE) * rows_y, depth))

    deep = (4, rows_x - 4)
    next_inner = (6, rows_x - 6)
    bands = range(0, rows_y, 8)

    def own_forces(lanes, s, v, b, x):
        for t in bands:
            push_velocity(shape, lanes, s, v, b, aligned(shape, x, t))

    def load(
        v_in, s_in, b_in, lame_in, shear_in, zone_in, able_in,
        s, v, b, h, first, second, x_first, x_second, floats, ints, sems, edge_sems,
    ):
        groups, edges = [], []
        for g, x in enumerate(range(0, rows_x, 8)):
            group = []
            for i, (source, ref) in enumerate(((s_in, s), (v_in, v), (b_in, b))):
                part = source.at[:, pl.ds(x, 8)] if i < 2 else source.at[pl.ds(x, 8)]
                place = own_cells(shape, ref, x, 8)
                group.append(pltpu.make_async_copy(part, place, sems.at[g, i]))
                group[-1].start()
            groups.append(group)
        for i, source in enumerate((lame_in, shear_in, zone_in, able_in)):
            ref = floats.at[i] if i < 2 else ints.at[i - 2]
            for side, x in enumerate((rows_x - BESIDE, 0)):
                part = source.at[pl.ds(x, BESIDE)]
                edges.append(pltpu.make_async_copy(part, ref.at[side], edge_sems.at[i, side]))
                edges[-1].start()

        def raw(c, side, x, t):
            if c < 2:
                return floats[c, side, x, pl.ds(t, 8), :]
            return ints[c - 2, side, x, pl.ds(t, 8), :].astype(jnp.float32)

        zero = jnp.zeros((8, depth), jnp.float32)
        for x in range(-2, rows_x + 3):
            for c in (XY, YY, YZ):
                s[c, pl.ds(shape.row(x, -RIM), 8), :] = zero
        for x in range(-2, rows_x + 2):
            for t in bands:
                for c in range(3):
                    h[c, pl.ds(shape.row(x, t), 8), :] = zero
        for x in (-2, -1, rows_x, rows_x + 1):
            for t in bands:
                for c in range(6):
                    s[c, pl.ds(shape.row(x, t), 8), :] = zero
        lanes = Lanes(depth)
        done = 0
        for g, group in enumerate(groups):
            for copy in group:
                copy.wait()
            stop = rows_x if g == len(groups) - 1 else 8 * g + 6
            layers(done, stop, lambda x: own_forces(lanes, s, v, b, x), stop - done)
            done = stop
        send_y(shape, s, v, b, first, second)
        for copy in edges:
            copy.wait()
        send_early(shape, s, b, raw, x_first, x_second)

    s, v, b, h, first, second, x_first, x_second = call(
        load,
        [velocity, stress, buoyancy, lame_first, modulus, zone, eligible],
        [in_hbm] * 7,
        [whole_s, whole_v, whole_b, whole_h] + [y_buffers[True]] * 2 + [early_buffer] * 2,
        [in_vmem] * 8,
        10000000,
        scratch=[
            pltpu.VMEM((2, 2, BESIDE, rows_y, depth), jnp.float32),
            pltpu.VMEM((2, 2, BESIDE, rows_y, depth), jnp.int32),
            pltpu.SemaphoreType.DMA((rows_x // 8, 3)),
            pltpu.SemaphoreType.DMA((4, 2)),
        ],
    )

    def prepare(after, lame_in, shear_in, zone_in, able_in, cohesion, friction, rock, zones, able, sems):
        flat = rock.reshape(5, rows_x + 2 * BESIDE, rows_y, depth)
        pairs = [(zone_in, zones), (able_in, able)]
        pairs += [(a, flat.at[i, pl.ds(BESIDE, rows_x)]) for i, a in enumerate((lame_in, shear_in))]
        run_copies(pairs, sems)

        def layer(x):
            for t in bands:
                which, able_here = zones[x, pl.ds(t, 8), :], able[x, pl.ds(t, 8), :]
                fill_rock(shape, rock, x, t, cohesion, friction, which, able_here)

        layers(0, rows_x, layer, 4)

    early_rims = tuple(range(BESIDE + 1)), tuple(range(rows_x - BESIDE, rows_x + 1))
    early = tuple(range(5)), tuple(range(rows_x - 5, rows_x))

    def turn(s, v_in, b_in, h_in, got_a, got_b, v, b, h, out_a, out_b):
        receive_y(shape, h, v, b, got_a, got_b)
        halves = [h.at[c] for c in range(3)]
        own = [s.at[c] for c in (XY, YY, YZ)]
        for x in early[0] + early[1]:
            for t in bands:
                push_across_y(halves, v, b, shape.row(x, t))
        for x in early_rims[0] + early_rims[1]:
            push_across_y(own, v, b, shape.row(x, -RIM))
        send_x(shape, v, b, got_a, got_b, out_a, out_b)

    def interior(
        s_in, v_in, b_in, h, rock_in, early_a, early_b, cell, moment, cohesion, friction, s, v, b, rock
    ):
        lanes = Lanes(depth)
        halves = [h.at[c] for c in range(3)]
        own = [s.at[c] for c in (XY, YY, YZ)]

        def layer(x):
            for t in bands:
                push_across_y(halves, v, b, aligned(shape, x, t))

        def rim(x):
            push_across_y(own, v, b, aligned(shape, x, -RIM))

        layers(early[0][-1] + 1, early[1][0], layer, 4)
        layers(early_rims[0][-1] + 1, early_rims[1][0], rim, 4)
        inject(shape, s, cell, moment, lambda x: (x >= deep[0]) & (x < deep[1]))
        layers(*deep, lambda x: push_stress(shape, lanes, s, v, rock, x), 4)
        layers(*next_inner, lambda x: own_forces(lanes, s, v, b, x), 4)
        receive_early(shape, s, b, rock, cohesion, friction, early_a, early_b)

    def border(
        s_in, v_in, b, rock, got_a, got_b, sent_a, sent_b, cell, moment, s, v, out_a, out_b
    ):
        receive_x(shape, s, v, b, (got_a, got_b), (sent_a, sent_b))
        lanes = Lanes(depth)
        low, high = -BESIDE, rows_x + BESIDE
        near = lambda x: (x >= low) & (x < high) & ((x < deep[0]) | (x >= deep[1]))
        inject(shape, s, cell, moment, near)
        for first, stop in ((low, deep[0]), (deep[1], high)):
            for x in range(first, stop):
                push_stress(shape, lanes, s, v, rock, x)
        for first, stop in ((-2, next_inner[0]), (next_inner[1], rows_x + 2)):
            for x in range(first, stop):
                own_forces(lanes, s, v, b, x)
        send_y(shape, s, v, None, out_a, out_b)

    def finish(
        s_in, v_in, b, h_in, rock, got_a, got_b, cell, moment, s, v, h, v_out, s_out, sems
    ):
        receive_y(shape, h, v, None, got_a, got_b)
        lanes = Lanes(depth)
        halves = [h.at[c] for c in range(3)]
        own = [s.at[c] for c in (XY, YY, YZ)]

        def layer(x):
            for t in bands:
                push_across_y(halves, v, b, aligned(shape, x, t))

        layers(-2, rows_x + 2, layer, 4)
        copies = [pltpu.make_async_copy(own_cells(shape, v), v_out, sems.at[0])]
        copies[0].start()
        layers(0, rows_x + 1, lambda x: push_across_y(own, v, b, aligned(shape, x, -RIM)), 3)
        inject(shape, s, cell, moment, lambda x: (x >= 0) & (x < rows_x))
        for i, x in enumerate(range(0, rows_x, 8)):
            layers(x, x + 8, lambda x: push_stress(shape, lanes, s, v, rock, x), 8)
            part = s_out.at[:, pl.ds(x, 8)]
            copies.append(pltpu.make_async_copy(own_cells(shape, s, x, 8), part, sems.at[i + 1]))
            copies[-1].start()
        for c in copies:
            c.wait()

    cells = [source_cell, source_moment]
    first, second = swaps("gy", first, second)
    x_first, x_second = swaps("gx", x_first, x_second)
    v, b, h, sent_a, sent_b = call(
        turn,
        [s, v, b, h, first, second],
        [in_vmem] * 6,
        [whole_v, whole_b, whole_h, x_buffer, x_buffer],
        [in_vmem] * 5,
        1000000,
        aliases={1: 0, 2: 1, 3: 2},
    )
    got_a, got_b = swaps("gx", sent_a, sent_b)
    rock = call(
        prepare,
        [v, lame_first, modulus, zone, eligible, cohesion, friction],
        [in_vmem] + [in_hbm] * 4 + [in_smem] * 2,
        whole_r,
        in_vmem,
        10000000,
        scratch=[
            pltpu.VMEM((rows_x, rows_y, depth), jnp.int32),
            pltpu.VMEM((rows_x, rows_y, depth), jnp.int32),
            pltpu.SemaphoreType.DMA((4,)),
        ],
    )
    s, v, b, rock = call(
        interior,
        [s, v, b, h, rock, x_first, x_second] + cells + [cohesion, friction],
        [in_vmem] * 7 + [in_smem] * 4,
        [whole_s, whole_v, whole_b, whole_r],
        [in_vmem] * 4,
        10000000,
        aliases={0: 0, 1: 1, 2: 2, 4: 3},
    )
    s, v, first, second = call(
        border,
        [s, v, b, rock, got_a, got_b, sent_a, sent_b] + cells,
        [in_vmem] * 8 + [in_smem] * 2,
        [whole_s, whole_v, y_buffers[False], y_buffers[False]],
        [in_vmem] * 4,
        10000000,
        aliases={0: 0, 1: 1},
    )
    first, second = swaps("gy", first, second)
    outs = call(
        finish,
        [s, v, b, h, rock, first, second] + cells,
        [in_vmem] * 7 + [in_smem] * 2,
        [
            whole_s,
            whole_v,
            whole_h,
            pltpu.HBM(velocity.shape, jnp.float32),
            pltpu.HBM(stress.shape, jnp.float32),
        ],
        [in_vmem] * 3 + [in_hbm] * 2,
        10000000,
        aliases={0: 0, 1: 1, 3: 2},
        scratch=[pltpu.SemaphoreType.DMA((rows_x // 8 + 1,))],
    )
    return (outs[3], outs[4])


def solution(mesh):
    placed = (
        P(None, "gx", "gy", None),
        P(None, "gx", "gy", None),
        P("gx", "gy", None),
        P("gx", "gy", None),
        P("gx", "gy", None),
        P("gx", "gy", None),
        P("gx", "gy", None),
        P(),
        P(),
        P(),
        P(),
    )
    return jax.shard_map(
        steps,
        mesh=mesh,
        in_specs=placed,
        out_specs=(P(None, "gx", "gy", None), P(None, "gx", "gy", None)),
        check_vma=False,
    )
```

time: 35.9 us -> 32.9 us (0.916)
  the two profiles are of different devices: /device:TPU:12 before, /device:TPU:13 now
where the time goes in v4:
time: 32.9 us; the launch traced here: 32.7 us
  starting transfers between devices  14.3 us (43%)
  Pallas kernels  11.2 us (34%)
  waiting for transfers between devices  6.4 us (19%)
  between operations  0.79 us (2%)
    ppermute x8, starting transfers between devices, swaps(): got.append(lax.ppermute(block, axis, pairs))  14.3 us
    pallas_call x6, Pallas kernels, call(): pl.pallas_call(body, in_specs=in_specs, out_shape=out_shape, out_specs=ou...  11.2 us
    ppermute x8, waiting for transfers between devices, swaps(): got.append(lax.ppermute(block, axis, pairs))  6.4 us
  transfers between devices with their start and end apart: 8, of which 3 were waited for; matrix products, arithmetic and copies ran while one was open for 0% of the time, Pallas kernels for 14%

profile of v4, /device:TPU:13, one launch (start us, length us, event | category | flops | bytes accessed | tf_op | source)
XLA Modules:
  0.0 32.7 jit_solution(256520889063813530)
XLA Ops:
  0.6 2.0 %shard_map.122 = (f32[6,784,128]{2,1,0:T(8,128)S(1)}, f32[3,784,128]{2,1,0:T(8,128)S(1)}, f32[784,128]{1,0:T(8,128)S(1)}, f32[3,784,128]{2,1,0:T(8,128)S(1)}, f3...) custom-call(f32[3,32,8,128]{3,2,1,0:T(8,128)} %v_in.1, ...), custom_call_target="tpu_custom_call" | custom-call | flops 10000000 | bytes 1000000 | tf_op jit(solution)/shard_map/pallas_call | solution.py:503
  2.6 0.7 %collective-permute-start = (f32[12,32,128]{2,1,0:T(8,128)S(1)}, f32[12,32,128]{2,1,0:T(8,128)S(1)}, u32[]{:S(2)}, u32[]{:S(2)}) collective-permute-start(f32[12,32,128]{2,1,0:T(8,128)S(1)} %get-tuple-element.29), channel_id=1, source_target_pairs={{0,1},{1,0},{2,3},{3,2},{4,5},{5,4},{6,7},{7,6},{8,9},{9,8},{10,11... | collective-permute-start | bytes 589832 | tf_op jit(solution)/shard_map/ppermute | solution.py:522
  3.4 3.1 %collective-permute-start.1 = (f32[12,32,128]{2,1,0:T(8,128)S(1)}, f32[12,32,128]{2,1,0:T(8,128)S(1)}, u32[]{:S(2)}, u32[]{:S(2)}) collective-permute-start(f32[12,32,128]{2,1,0:T(8,128)S(1)} %get-tuple-element.30), channel_id=1, source_target_pairs={{1,2},{2,1},{3,4},{4,3},{5,6},{6,5},{9,10},{10,9},{11,12},{12,11},... | collective-permute-start | bytes 589832 | tf_op jit(solution)/shard_map/ppermute | solution.py:522
  6.5 1.3 %collective-permute-start.2 = (f32[32,8,128]{2,1,0:T(8,128)S(1)}, f32[32,8,128]{2,1,0:T(8,128)S(1)}, u32[]{:S(2)}, u32[]{:S(2)}) collective-permute-start(f32[32,8,128]{2,1,0:T(8,128)S(1)} %get-tuple-element.34), channel_id=1, source_target_pairs={{0,8},{8,0},{16,24},{24,16},{1,9},{9,1},{17,25},{25,17},{2,10},{10... | collective-permute-start | bytes 393224 | tf_op jit(solution)/shard_map/ppermute | solution.py:522
  7.7 2.1 %collective-permute-start.3 = (f32[32,8,128]{2,1,0:T(8,128)S(1)}, f32[32,8,128]{2,1,0:T(8,128)S(1)}, u32[]{:S(2)}, u32[]{:S(2)}) collective-permute-start(f32[32,8,128]{2,1,0:T(8,128)S(1)} %get-tuple-element.35), channel_id=1, source_target_pairs={{8,16},{16,8},{9,17},{17,9},{10,18},{18,10},{11,19},{19,11},{12,20... | collective-permute-start | bytes 393224 | tf_op jit(solution)/shard_map/ppermute | solution.py:522
  9.8 0.0 collective-permute-done.got_a
  9.9 0.8 %collective-permute-done.1.got_b = f32[12,32,128]{2,1,0:T(8,128)S(1)} collective-permute-done((f32[12,32,128]{2,1,0:T(8,128)S(1)}, f32[12,32,128]{2,1,0:T(8,128)S(1)}, u32[]{:S(2)}, u32[]{:S(2)}) %collective-permute-start.1) | collective-permute-done | bytes 196640 | tf_op jit(solution)/shard_map/ppermute | solution.py:522
  10.6 0.0 copy-start.2
  10.6 0.0 copy-start.3
  10.6 0.3 shard_map.123
  10.9 1.3 %collective-permute-start.4 = (f32[29,8,128]{2,1,0:T(8,128)S(1)}, f32[29,8,128]{2,1,0:T(8,128)S(1)}, u32[]{:S(2)}, u32[]{:S(2)}) collective-permute-start(f32[29,8,128]{2,1,0:T(8,128)S(1)} %get-tuple-element.40.sent_a), channel_id=1, source_target_pairs={{0,8},{8,0},{16,24},{24,16},{1,9},{9,1},{17,25},{25,17},{2,10},{10... | collective-permute-start | bytes 356360 | tf_op jit(solution)/shard_map/ppermute | solution.py:522
  12.2 2.2 %collective-permute-start.5 = (f32[29,8,128]{2,1,0:T(8,128)S(1)}, f32[29,8,128]{2,1,0:T(8,128)S(1)}, u32[]{:S(2)}, u32[]{:S(2)}) collective-permute-start(f32[29,8,128]{2,1,0:T(8,128)S(1)} %get-tuple-element.41.sent_b), channel_id=1, source_target_pairs={{8,16},{16,8},{9,17},{17,9},{10,18},{18,10},{11,19},{19,11},{12,20... | collective-permute-start | bytes 356360 | tf_op jit(solution)/shard_map/ppermute | solution.py:522
  14.4 0.0 copy-done.2
  14.4 0.0 copy-done.3
  14.4 0.0 copy-start
  14.4 0.0 copy-start.1
  14.4 1.9 %shard_map.124.rock_in = f32[5,304,128]{2,1,0:T(8,128)S(1)} custom-call(f32[3,784,128]{2,1,0:T(8,128)S(1)} %get-tuple-element.31.after.v_in, f32[32,8,128]{2,1,0:T(8,128)} %lame_in.3, f32[32,8,128]{2,1,0:T(8,128)} %shear_in.3, s32[32,8,128]{2,1,0:T(8,128)} %zone_in.3, s32[32,8,128]{2,1,0:T(8,128)} %able_in.3, f32[8]{0:T(128)S(1)} %copy-done.2, f32[8]{0:T(128)S(1)} %copy-done.3), custom_call_target="tpu_custom_call" | custom-call | flops 10000000 | bytes 1000000 | tf_op jit(solution)/shard_map/pallas_call | solution.py:503
  16.3 0.0 collective-permute-done.2.early_a
  16.3 0.0 collective-permute-done.3.early_b
  16.3 0.0 copy-done
  16.3 0.0 copy-done.1
  16.3 2.6 %shard_map.125 = (f32[6,784,128]{2,1,0:T(8,128)S(1)}, f32[3,784,128]{2,1,0:T(8,128)S(1)}, f32[784,128]{1,0:T(8,128)S(1)}, f32[5,304,128]{2,1,0:T(8,128)S(1)}) custom-call(f32[6,784,128]{2,1,0:T(8,128)S(1)} %get-tuple-element.25.s.s_in, ...), custom_call_target="tpu_custom_call", output_to_operand_aliasing={{0}: (0, {}), {1}: (1, {}), {2}: (2, {}), {3}: (4, {})} | custom-call | flops 10000000 | bytes 1000000 | tf_op jit(solution)/shard_map/pallas_call | solution.py:503
  18.9 0.0 collective-permute-done.4.got_a
  18.9 2.1 %collective-permute-done.5.got_b = f32[29,8,128]{2,1,0:T(8,128)S(1)} collective-permute-done((f32[29,8,128]{2,1,0:T(8,128)S(1)}, f32[29,8,128]{2,1,0:T(8,128)S(1)}, u32[]{:S(2)}, u32[]{:S(2)}) %collective-permute-start.5) | collective-permute-done | bytes 118816 | tf_op jit(solution)/shard_map/ppermute | solution.py:522
  21.0 1.5 %shard_map.126 = (f32[6,784,128]{2,1,0:T(8,128)S(1)}, f32[3,784,128]{2,1,0:T(8,128)S(1)}, f32[10,32,128]{2,1,0:T(8,128)S(1)}, f32[10,32,128]{2,1,0:T(8,128)S(1)}) custom-call(f32[6,784,128]{2,1,0:T(8,128)S(1)} %get-tuple-element.36.s_in, f32[3,784,128]{2,1,0:T(8,128)S(1)} %get-tuple-element.37.v_in, ...), custom_call_target="tpu_custom_call", output_to_operand_aliasing={{0}: (0, {}), {1}: (1, {})} | custom-call | flops 10000000 | bytes 1000000 | tf_op jit(solution)/shard_map/pallas_call | solution.py:503
  22.5 0.6 %collective-permute-start.6 = (f32[10,32,128]{2,1,0:T(8,128)S(1)}, f32[10,32,128]{2,1,0:T(8,128)S(1)}, u32[]{:S(2)}, u32[]{:S(2)}) collective-permute-start(f32[10,32,128]{2,1,0:T(8,128)S(1)} %get-tuple-element.44), channel_id=1, source_target_pairs={{0,1},{1,0},{2,3},{3,2},{4,5},{5,4},{6,7},{7,6},{8,9},{9,8},{10,11... | collective-permute-start | bytes 491528 | tf_op jit(solution)/shard_map/ppermute | solution.py:522
  23.1 3.1 %collective-permute-start.7 = (f32[10,32,128]{2,1,0:T(8,128)S(1)}, f32[10,32,128]{2,1,0:T(8,128)S(1)}, u32[]{:S(2)}, u32[]{:S(2)}) collective-permute-start(f32[10,32,128]{2,1,0:T(8,128)S(1)} %get-tuple-element.45), channel_id=1, source_target_pairs={{1,2},{2,1},{3,4},{4,3},{5,6},{6,5},{9,10},{10,9},{11,12},{12,11},... | collective-permute-start | bytes 491528 | tf_op jit(solution)/shard_map/ppermute | solution.py:522
  26.2 0.0 collective-permute-done.6.got_a
  26.2 3.5 %collective-permute-done.7.got_b = f32[10,32,128]{2,1,0:T(8,128)S(1)} collective-permute-done((f32[10,32,128]{2,1,0:T(8,128)S(1)}, f32[10,32,128]{2,1,0:T(8,128)S(1)}, u32[]{:S(2)}, u32[]{:S(2)}) %collective-permute-start.7) | collective-permute-done | bytes 163872 | tf_op jit(solution)/shard_map/ppermute | solution.py:522
  29.7 3.0 %shard_map.127 = (f32[6,784,128]{2,1,0:T(8,128)S(1)}, f32[3,784,128]{2,1,0:T(8,128)S(1)}, f32[3,784,128]{2,1,0:T(8,128)S(1)}, f32[3,32,8,128]{3,2,1,0:T(8,128)}, f32[6,32,8,128]{3,2,1,0:T(8,128)}) custom-call(f32[6,784,128]{2,1,0:T(8,128)S(1)} %get-tuple-element.42.s_in, ...), custom_call_target="tpu_custom_call", output_to_operand_aliasing={{0}: (0, {}), {1}: (1, {}), {2}: (3, {})} | custom-call | flops 10000000 | bytes 1000000 | tf_op jit(solution)/shard_map/pallas_call | solution.py:503
Async XLA Ops:
  2.6 7.2 %collective-permute-start = (f32[12,32,128]{2,1,0:T(8,128)S(1)}, f32[12,32,128]{2,1,0:T(8,128)S(1)}, u32[]{:S(2)}, u32[]{:S(2)}) collective-permute-start(f32[12,32,128]{2,1,0:T(8,128)S(1)} %get-tuple-element.29), channel_id=1, source_target_pairs={{0,1},{1,0},{2,3},{3,2},{4,5},{5,4},{6,7},{7,6},{8,9},{9,8},{10,11... | collective-permute-start | bytes 589832 | tf_op jit(solution)/shard_map/ppermute | solution.py:522
  3.4 7.3 %collective-permute-start.1 = (f32[12,32,128]{2,1,0:T(8,128)S(1)}, f32[12,32,128]{2,1,0:T(8,128)S(1)}, u32[]{:S(2)}, u32[]{:S(2)}) collective-permute-start(f32[12,32,128]{2,1,0:T(8,128)S(1)} %get-tuple-element.30), channel_id=1, source_target_pairs={{1,2},{2,1},{3,4},{4,3},{5,6},{6,5},{9,10},{10,9},{11,12},{12,11},... | collective-permute-start | bytes 589832 | tf_op jit(solution)/shard_map/ppermute | solution.py:522
  6.5 9.8 %collective-permute-start.2 = (f32[32,8,128]{2,1,0:T(8,128)S(1)}, f32[32,8,128]{2,1,0:T(8,128)S(1)}, u32[]{:S(2)}, u32[]{:S(2)}) collective-permute-start(f32[32,8,128]{2,1,0:T(8,128)S(1)} %get-tuple-element.34), channel_id=1, source_target_pairs={{0,8},{8,0},{16,24},{24,16},{1,9},{9,1},{17,25},{25,17},{2,10},{10... | collective-permute-start | bytes 393224 | tf_op jit(solution)/shard_map/ppermute | solution.py:522
  7.7 8.6 %collective-permute-start.3 = (f32[32,8,128]{2,1,0:T(8,128)S(1)}, f32[32,8,128]{2,1,0:T(8,128)S(1)}, u32[]{:S(2)}, u32[]{:S(2)}) collective-permute-start(f32[32,8,128]{2,1,0:T(8,128)S(1)} %get-tuple-element.35), channel_id=1, source_target_pairs={{8,16},{16,8},{9,17},{17,9},{10,18},{18,10},{11,19},{19,11},{12,20... | collective-permute-start | bytes 393224 | tf_op jit(solution)/shard_map/ppermute | solution.py:522
  10.6 3.7 %copy-start.2 = (f32[8]{0:T(128)S(1)}, f32[8]{0:T(128)}, u32[]{:S(2)}) copy-start(f32[8]{0:T(128)} %cohesion.3) | copy-start | bytes 100
  10.6 3.7 %copy-start.3 = (f32[8]{0:T(128)S(1)}, f32[8]{0:T(128)}, u32[]{:S(2)}) copy-start(f32[8]{0:T(128)} %friction.3) | copy-start | bytes 100
  10.9 8.0 %collective-permute-start.4 = (f32[29,8,128]{2,1,0:T(8,128)S(1)}, f32[29,8,128]{2,1,0:T(8,128)S(1)}, u32[]{:S(2)}, u32[]{:S(2)}) collective-permute-start(f32[29,8,128]{2,1,0:T(8,128)S(1)} %get-tuple-element.40.sent_a), channel_id=1, source_target_pairs={{0,8},{8,0},{16,24},{24,16},{1,9},{9,1},{17,25},{25,17},{2,10},{10... | collective-permute-start | bytes 356360 | tf_op jit(solution)/shard_map/ppermute | solution.py:522
  12.2 8.8 %collective-permute-start.5 = (f32[29,8,128]{2,1,0:T(8,128)S(1)}, f32[29,8,128]{2,1,0:T(8,128)S(1)}, u32[]{:S(2)}, u32[]{:S(2)}) collective-permute-start(f32[29,8,128]{2,1,0:T(8,128)S(1)} %get-tuple-element.41.sent_b), channel_id=1, source_target_pairs={{8,16},{16,8},{9,17},{17,9},{10,18},{18,10},{11,19},{19,11},{12,20... | collective-permute-start | bytes 356360 | tf_op jit(solution)/shard_map/ppermute | solution.py:522
  14.4 1.9 %copy-start = (f32[6,16]{1,0:T(8,128)S(1)}, f32[6,16]{1,0:T(8,128)}, u32[]{:S(2)}) copy-start(f32[6,16]{1,0:T(8,128)} %moment.5) | copy-start | bytes 1156
  14.4 1.9 %copy-start.1 = (s32[16]{0:T(128)S(1)}, s32[16]{0:T(128)}, u32[]{:S(2)}) copy-start(s32[16]{0:T(128)} %cell.5) | copy-start | bytes 196
  22.5 3.7 %collective-permute-start.6 = (f32[10,32,128]{2,1,0:T(8,128)S(1)}, f32[10,32,128]{2,1,0:T(8,128)S(1)}, u32[]{:S(2)}, u32[]{:S(2)}) collective-permute-start(f32[10,32,128]{2,1,0:T(8,128)S(1)} %get-tuple-element.44), channel_id=1, source_target_pairs={{0,1},{1,0},{2,3},{3,2},{4,5},{5,4},{6,7},{7,6},{8,9},{9,8},{10,11... | collective-permute-start | bytes 491528 | tf_op jit(solution)/shard_map/ppermute | solution.py:522
  23.1 6.6 %collective-permute-start.7 = (f32[10,32,128]{2,1,0:T(8,128)S(1)}, f32[10,32,128]{2,1,0:T(8,128)S(1)}, u32[]{:S(2)}, u32[]{:S(2)}) collective-permute-start(f32[10,32,128]{2,1,0:T(8,128)S(1)} %get-tuple-element.45), channel_id=1, source_target_pairs={{1,2},{2,1},{3,4},{4,3},{5,6},{6,5},{9,10},{10,9},{11,12},{12,11},... | collective-permute-start | bytes 491528 | tf_op jit(solution)/shard_map/ppermute | solution.py:522

commit v5 on v4

v5 whole, which is shorter than its diff:
```python
import jax
import jax.numpy as jnp
from jax import lax
from jax.experimental import pallas as pl
from jax.experimental.pallas import tpu as pltpu
from jax.sharding import PartitionSpec as P


time_step = 0.1
near_weight = 9.0 / 8.0
far_weight = 1.0 / 24.0
shear_floor = 0.25

XX, YY, ZZ, XY, XZ, YZ = range(6)

LOW_X = ((XX, 1), (XY, 2), (XZ, 2))
HIGH_X = ((XX, 2), (XY, 1), (XZ, 1))
LOW_FLOW_Y = ((0, 1), (1, 2), (2, 1))
HIGH_FLOW_Y = ((0, 2), (1, 1), (2, 2))
BESIDE = 3
LOW_DEEP_X = ((0, 5), (1, 4), (2, 4))
HIGH_DEEP_X = ((0, 4), (1, 5), (2, 5))
DRIVES_X = (XX, XY, XZ)
DRIVES_Y = (XY, YY, YZ)
LOW_PUSH = ((0, 2), (1, 1), (2, 2))
HIGH_PUSH = ((0, 1), (1, 2), (2, 1))

NEAR, FAR = near_weight, far_weight
UP = {1: NEAR, 0: -NEAR, 2: -FAR, -1: FAR}
DOWN = {0: NEAR, -1: -NEAR, 1: -FAR, -2: FAR}


def crossing(table, at, sources):
    total = None
    for step, weight in table.items():
        if at + step in sources:
            term = weight * sources[at + step]()
            total = term if total is None else total + term
    return total


def crossing_x(c, x, sources):
    return crossing(UP if c == 0 else DOWN, x, sources)


def crossing_y(c, y, sources):
    return crossing(UP if c == 1 else DOWN, y, sources)


PAD_X = 8
RIM = 8


class Shape:
    def __init__(self, rows_x, rows_y, depth):
        self.rows_x, self.rows_y, self.depth = rows_x, rows_y, depth
        self.pitch = rows_y + RIM
        self.rows = (rows_x + 2 * PAD_X + 1) * self.pitch

    def row(self, x, y):
        return (x + PAD_X) * self.pitch + RIM + y


def entries(spec):
    return [(c, k) for c, depth in spec for k in range(depth)]


def edge_layers(shape):
    return (0, 1, shape.rows_x - 2, shape.rows_x - 1)


def beside_layers(shape):
    return (-2, -1, shape.rows_x, shape.rows_x + 1)


def by_parity(axis, body, *swapped):
    odd = lax.axis_index(axis) % 2

    @pl.when(odd == 0)
    def _():
        body(*[r for first, second in swapped for r in (second, first)])

    @pl.when(odd == 1)
    def _():
        body(*[r for first, second in swapped for r in (first, second)])


def y_faces(shape):
    rows = shape.rows_y
    above = (LOW_PUSH, LOW_FLOW_Y, lambda y: y - rows, lambda y: y + rows)
    below = (HIGH_PUSH, HIGH_FLOW_Y, lambda y: y + rows, lambda y: y - rows)
    return above, below


def pushed(spec, shape):
    low = spec is LOW_PUSH
    return [(c, k if low else shape.rows_y - 1 - k) for c, k in entries(spec)]


def rim_rows(spec, shape):
    low = spec is LOW_FLOW_Y
    return [(c, -1 - k if low else shape.rows_y + k) for c, k in entries(spec)]


def side_rows(spec, shape):
    return [-1, -2] if spec is LOW_FLOW_Y else [shape.rows_y, shape.rows_y + 1]


def send_y(shape, stress, flow, buoyancy, first, second, groups, singles=True):
    rows_y = shape.rows_y

    def fill(out, push, flow_spec, to_other, to_own):
        face = [y for y in (0, 1, rows_y - 2, rows_y - 1) if to_other(y) in (-2, -1, rows_y, rows_y + 1)]

        def force(c, y, read):
            sources = {to_other(o): (lambda o=o: read(DRIVES_Y[c], o)) for o in face}
            return crossing_y(c, y, sources)

        for x in groups:

            def read(c, y):
                return stress[c, pl.ds(shape.row(x, y), 8, stride=shape.pitch), :]

            slot = 0
            for c, y in pushed(push, shape):
                out[slot, pl.ds(x, 8), :] = force(c, y, read)
                slot += 1
            whole = [(flow.at[c], to_own(y)) for c, y in rim_rows(flow_spec, shape)]
            if buoyancy is not None:
                whole += [(buoyancy, to_own(y)) for y in side_rows(flow_spec, shape)]
            for ref, y in whole:
                out[slot, pl.ds(x, 8), :] = ref[pl.ds(shape.row(x, y), 8, stride=shape.pitch), :]
                slot += 1
        if not singles:
            return
        last = out.at[out.shape[0] - 1]
        for i, x in enumerate(edge_layers(shape) if buoyancy is not None else beside_layers(shape)):

            def single(c, y):
                return stress[c, pl.ds(shape.row(x, y), 1), :]

            if buoyancy is not None:
                rows = [single(DRIVES_X[c], to_own(y)) for c, y in rim_rows(flow_spec, shape)]
            else:
                rows = [force(c, y, single) for c, y in pushed(push, shape)]
            for j, row in enumerate(rows):
                last[pl.ds(8 * i + j, 1), :] = row

    def body(below, above):
        for out, face in zip((above, below), y_faces(shape)):
            fill(out, *face)

    by_parity("gy", body, (first, second))


def receive_y(shape, force, flow, buoyancy, first, second, begun=False):
    def take(got, push, flow_spec):
        slot = 0
        whole = [(force.at[c], y, False) for c, y in pushed(push, shape)]
        whole += [(flow.at[c], y, begun) for c, y in rim_rows(flow_spec, shape)]
        if buoyancy is not None:
            whole += [(buoyancy, y, False) for y in side_rows(flow_spec, shape)]
        for slot, (ref, y, add) in enumerate(whole):
            for x in range(0, shape.rows_x, 8):
                place = pl.ds(shape.row(x, y), 8, stride=shape.pitch)
                value = got[slot, pl.ds(x, 8), :]
                ref[place, :] = ref[place, :] + value if add else value
        if buoyancy is None:
            for i, x in enumerate(beside_layers(shape)):
                for j, (c, y) in enumerate(pushed(push, shape)):
                    single = got[got.shape[0] - 1, pl.ds(8 * i + j, 1), :]
                    force[c, pl.ds(shape.row(x, y), 1), :] = single

    def body(below, above):
        take(below, LOW_PUSH, LOW_FLOW_Y)
        take(above, HIGH_PUSH, HIGH_FLOW_Y)

    by_parity("gy", body, (first, second))


def y_count(first_round):
    most = max(
        len(entries(push)) + len(entries(flow_spec))
        for push, flow_spec in ((LOW_PUSH, LOW_FLOW_Y), (HIGH_PUSH, HIGH_FLOW_Y))
    )
    return most + 1 + (2 if first_round else 0)


def early_slots(shape, side):
    bands = range(0, shape.rows_y, 8)
    deep = (LOW_DEEP_X, HIGH_DEEP_X)[side]
    keys = [("s", c, k, t) for c in range(6) for k in range(BESIDE) for t in bands]
    keys += [("r", c, k, t) for c in range(4) for k in range(BESIDE) for t in bands]
    keys += [("b", 0, k, t) for k in range(2) for t in bands]
    keys += [("v", c, k, t) for c, k in entries(deep) for t in bands]
    return {key: i for i, key in enumerate(keys)}


def early_count(shape):
    return max(len(early_slots(shape, side)) for side in (0, 1))


def send_early(shape, stress, flow, buoyancy, raw, first, second):
    def fill(out, side, place):
        for (kind, c, k, t), slot in early_slots(shape, side).items():
            x = place(k)
            if kind == "r":
                at = x - (shape.rows_x - BESIDE if side == 0 else 0)
                out[slot] = raw(c, side, at, t)
            else:
                ref = buoyancy if kind == "b" else (stress if kind == "s" else flow).at[c]
                out[slot] = tile(ref, shape.row(x, t))

    def body(below, above):
        fill(above, 0, lambda k: shape.rows_x - 1 - k)
        fill(below, 1, lambda k: k)

    by_parity("gx", body, (first, second))


def receive_early(shape, stress, flow, buoyancy, rock, cohesion, friction, first, second):
    def take(got, side, place):
        slots = early_slots(shape, side)
        for (kind, c, k, t), slot in slots.items():
            x = place(k)
            if kind == "s":
                stress[c, pl.ds(shape.row(x, t), 8), :] = got[slot]
            elif kind == "b":
                buoyancy[pl.ds(shape.row(x, t), 8), :] = got[slot]
            elif kind == "v":
                flow[c, pl.ds(shape.row(x, t), 8), :] = got[slot]
            elif c == 0:
                raw = [got[slots["r", i, k, t]] for i in range(4)]
                fill_rock(shape, rock, x, t, cohesion, friction, *raw)

    def body(below, above):
        take(below, 0, lambda k: -1 - k)
        take(above, 1, lambda k: shape.rows_x + k)

    by_parity("gx", body, (first, second))
    for t in range(0, shape.rows_y, 8):
        for c in range(3):
            there = {
                x: (lambda x=x: tile(stress.at[DRIVES_X[c]], shape.row(x, t)))
                for x in edge_layers(shape) + beside_layers(shape)
            }
            inside = {x: there[x] for x in edge_layers(shape)}
            outside = {x: there[x] for x in beside_layers(shape)}
            for targets, sources in ((inside, outside), (outside, inside)):
                for x in targets:
                    force = crossing_x(c, x, sources)
                    if force is not None:
                        row = shape.row(x, t)
                        flow[c, pl.ds(row, 8), :] += time_step * tile(buoyancy, row) * force


def fill_rock(shape, rock, x, t, cohesion, friction, first, shear, which, able):
    hold = jnp.full((8, shape.depth), cohesion[0], jnp.float32)
    rub = jnp.full((8, shape.depth), friction[0], jnp.float32)
    for k in range(1, cohesion.shape[0]):
        hit = which == k
        hold = jnp.where(hit, cohesion[k], hold)
        rub = jnp.where(hit, friction[k], rub)
    own = pl.multiple_of((x + BESIDE) * shape.rows_y + t, 8)
    rock[0, pl.ds(own, 8), :] = first
    rock[1, pl.ds(own, 8), :] = shear
    rock[2, pl.ds(own, 8), :] = hold * jnp.sqrt(1.0 - rub * rub)
    rock[3, pl.ds(own, 8), :] = rub
    rock[4, pl.ds(own, 8), :] = jnp.where(able == 1, 1.0, 0.0)


def late_rows(shape, side):
    spec, deep = ((LOW_X, LOW_DEEP_X), (HIGH_X, HIGH_DEEP_X))[side]
    reached = pushed(LOW_PUSH, shape) + pushed(HIGH_PUSH, shape)
    rims = rim_rows(LOW_FLOW_Y, shape) + rim_rows(HIGH_FLOW_Y, shape)
    keys = [("d", c, k, y) for c, k in entries(deep) for which, y in reached if which == c]
    keys += [("v", c, k, y) for k in range(BESIDE) for c, y in rims]
    sides = side_rows(LOW_FLOW_Y, shape) + side_rows(HIGH_FLOW_Y, shape)
    keys += [("b", 0, k, y) for k in range(2) for y in sides]
    depths = dict(spec)
    keys += [("s", c, k, y) for c, y in rims for k in range(depths[DRIVES_X[c]])]
    return {key: i for i, key in enumerate(keys)}


def late_count(shape):
    return -(-max(len(late_rows(shape, side)) for side in (0, 1)) // 8) * 8


def send_late(shape, force, flow, buoyancy, got_first, got_second, first, second):
    layer_at = {x: i for i, x in enumerate(edge_layers(shape))}

    def fill(out, side, place, got_below, got_above):
        singles = {}
        for got, spec in ((got_below, LOW_FLOW_Y), (got_above, HIGH_FLOW_Y)):
            for j, key in enumerate(rim_rows(spec, shape)):
                singles[key] = (got, j)
        for (kind, c, k, y), at in late_rows(shape, side).items():
            x = place(k)
            if kind == "s":
                got, j = singles[c, y]
                row = got[got.shape[0] - 1, pl.ds(8 * layer_at[x] + j, 1), :]
            else:
                ref = {"d": force, "v": flow}[kind].at[c] if kind != "b" else buoyancy
                row = ref[pl.ds(shape.row(x, y), 1), :]
            out[pl.ds(at, 1), :] = row

    def with_singles(got_below, got_above):
        def body(below, above):
            fill(above, 0, lambda k: shape.rows_x - 1 - k, got_below, got_above)
            fill(below, 1, lambda k: k, got_below, got_above)

        by_parity("gx", body, (first, second))

    by_parity("gy", with_singles, (got_first, got_second))


def receive_late(shape, flow, buoyancy, got, sent):
    rows_x = shape.rows_x

    def add(c, x, y, value):
        flow[c, pl.ds(shape.row(x, y), 1), :] += value

    def body(below, above, sent_below, sent_above):
        def read(sides):
            return {
                (kind, c, place(k), y): (lambda ref=ref, at=at: ref[pl.ds(at, 1), :])
                for ref, side, place in sides
                for (kind, c, k, y), at in late_rows(shape, side).items()
            }

        came = read(((below, 0, lambda k: -1 - k), (above, 1, lambda k: rows_x + k)))
        went = read(((sent_above, 0, lambda k: rows_x - 1 - k), (sent_below, 1, lambda k: k)))

        def rims(of, c, y):
            return {x: f for (kind, which, x, at), f in of.items() if (kind, which, at) == ("s", c, y)}

        for (kind, c, x, y), value in came.items():
            if kind == "d":
                add(c, x, y, value())
        for c, y in rim_rows(LOW_FLOW_Y, shape) + rim_rows(HIGH_FLOW_Y, shape):
            halo, own = rims(came, c, y), rims(went, c, y)
            for x in edge_layers(shape):
                force = crossing_x(c, x, halo)
                if force is not None:
                    scale = time_step * buoyancy[pl.ds(shape.row(x, y), 1), :]
                    add(c, x, y, scale * force)
            for x in [d for k in range(BESIDE) for d in (-1 - k, rows_x + k)]:
                value = came["v", c, x, y]()
                force = crossing_x(c, x, own)
                if force is not None:
                    value = value + time_step * came["b", 0, x, y]() * force
                flow[c, pl.ds(shape.row(x, y), 1), :] = value

    by_parity("gx", body, got, sent)


class Lanes:
    def __init__(self, depth):
        self.depth = depth
        lane = lax.broadcasted_iota(jnp.int32, (8, depth), 1)
        zero = jnp.zeros((8, depth), jnp.float32)
        near = jnp.full((8, depth), near_weight, jnp.float32)
        far = jnp.full((8, depth), far_weight, jnp.float32)
        self.f_up = jnp.where(lane < depth - 1, near, zero)
        self.f_up2 = jnp.where(lane < depth - 2, far, zero)
        self.f_down = jnp.where(lane > 0, far, zero)
        self.b_down = jnp.where(lane > 0, near, zero)
        self.b_down2 = jnp.where(lane > 1, far, zero)
        self.b_up = jnp.where(lane < depth - 1, far, zero)

    def forward(self, f):
        up, up2, down = (pltpu.roll(f, s % self.depth, 1) for s in (-1, -2, 1))
        return (self.f_up * up - near_weight * f) - (self.f_up2 * up2 - self.f_down * down)

    def backward(self, f):
        up, down, down2 = (pltpu.roll(f, s % self.depth, 1) for s in (-1, 1, 2))
        return (near_weight * f - self.b_down * down) - (self.b_up * up - self.b_down2 * down2)


def forward(ref, row, step):
    a, b, c, d = (ref[pl.ds(row + k * step, 8), :] for k in (-1, 0, 1, 2))
    return near_weight * (c - b) - far_weight * (d - a)


def backward(ref, row, step):
    a, b, c, d = (ref[pl.ds(row + k * step, 8), :] for k in (-2, -1, 0, 1))
    return near_weight * (c - b) - far_weight * (d - a)


def tile(ref, row):
    return ref[pl.ds(row, 8), :]


def push_velocity(shape, lanes, stress, flow, buoyancy, row, along="xyz"):
    sx, sy = shape.pitch, 1
    xx, yy, zz, xy, xz, yz = (stress.at[c] for c in range(6))
    parts = {
        "x": lambda: (forward(xx, row, sx), backward(xy, row, sx), backward(xz, row, sx)),
        "y": lambda: (backward(xy, row, sy), forward(yy, row, sy), backward(yz, row, sy)),
        "z": lambda: (
            lanes.backward(tile(xz, row)),
            lanes.backward(tile(yz, row)),
            lanes.forward(tile(zz, row)),
        ),
    }
    force = parts[along[0]]()
    for axis in along[1:]:
        force = [f + g for f, g in zip(force, parts[axis]())]
    scale = time_step * tile(buoyancy, row)
    for c in range(3):
        flow[c, pl.ds(row, 8), :] += scale * force[c]


def across_y(stress, buoyancy, row):
    xy, yy, yz = (stress.at[c] for c in DRIVES_Y)
    scale = time_step * tile(buoyancy, row)
    forces = (backward(xy, row, 1), forward(yy, row, 1), backward(yz, row, 1))
    return [scale * f for f in forces]


def layers(first, stop, body, unroll):
    def run(x, carry):
        body(x)
        return carry

    lax.fori_loop(first, stop, run, 0, unroll=unroll)


def aligned(shape, x, y):
    return pl.multiple_of((x + PAD_X) * shape.pitch + RIM + y, 8)


def inject(shape, stress, source_cell, source_moment, wanted):
    rows_x, rows_y, depth = shape.rows_x, shape.rows_y, shape.depth
    total_y = rows_y * lax.axis_size("gy")
    start_x = lax.axis_index("gx") * rows_x
    start_y = lax.axis_index("gy") * rows_y
    sub = lax.broadcasted_iota(jnp.int32, (8, depth), 0)
    lane = lax.broadcasted_iota(jnp.int32, (8, depth), 1)
    for s in range(source_cell.shape[0]):
        cell = source_cell[s]
        line = lax.div(cell, depth)
        x = lax.div(line, total_y) - start_x
        y = lax.rem(line, total_y) - start_y
        z = lax.rem(cell, depth)

        @pl.when(wanted(x) & (y >= 0) & (y < rows_y))
        def _(x=x, y=y, z=z, s=s):
            band = lax.div(y, 8) * 8
            row = aligned(shape, x, band)
            here = (sub == y - band) & (lane == z)
            for c in range(6):
                amount = time_step * source_moment[c, s]
                stress[c, pl.ds(row, 8), :] += jnp.where(here, amount, 0.0)


def push_stress(shape, lanes, stress, flow, rock, x):
    sx, sy = shape.pitch, 1
    vx, vy, vz = (flow.at[c] for c in range(3))

    for t in range(0, shape.rows_y, 8):
        row = aligned(shape, x, t)
        own = pl.multiple_of((x + BESIDE) * shape.rows_y + t, 8)
        first = time_step * rock[0, pl.ds(own, 8), :]
        shear = time_step * rock[1, pl.ds(own, 8), :]
        strain_x = backward(vx, row, sx)
        strain_y = backward(vy, row, sy)
        here_z = tile(vz, row)
        strain_z = lanes.backward(here_z)
        volume = first * (strain_x + strain_y + strain_z)
        twice = 2.0 * shear
        xx = tile(stress.at[XX], row) + (volume + twice * strain_x)
        yy = tile(stress.at[YY], row) + (volume + twice * strain_y)
        zz = tile(stress.at[ZZ], row) + (volume + twice * strain_z)
        xy = tile(stress.at[XY], row) + shear * (forward(vx, row, sy) + forward(vy, row, sx))
        xz = tile(stress.at[XZ], row) + shear * (
            lanes.forward(tile(vx, row)) + forward(vz, row, sx)
        )
        yz = tile(stress.at[YZ], row) + shear * (
            lanes.forward(tile(vy, row)) + forward(vz, row, sy)
        )
        pressure = (xx + yy + zz) * (1.0 / 3.0)
        dx, dy, dz = xx - pressure, yy - pressure, zz - pressure
        second = 0.5 * (dx * dx + dy * dy + dz * dz) + xy * xy + xz * xz + yz * yz
        strength = jnp.maximum(
            rock[2, pl.ds(own, 8), :] - pressure * rock[3, pl.ds(own, 8), :], 0.0
        )
        ratio = strength * lax.rsqrt(jnp.maximum(second, shear_floor * shear_floor))
        factor = jnp.where(rock[4, pl.ds(own, 8), :] > 0.5, jnp.minimum(ratio, 1.0), 1.0)
        stress[XX, pl.ds(row, 8), :] = pressure + factor * dx
        stress[YY, pl.ds(row, 8), :] = pressure + factor * dy
        stress[ZZ, pl.ds(row, 8), :] = pressure + factor * dz
        stress[XY, pl.ds(row, 8), :] = factor * xy
        stress[XZ, pl.ds(row, 8), :] = factor * xz
        stress[YZ, pl.ds(row, 8), :] = factor * yz


def own_cells(shape, ref, first=0, count=None):
    lead = ref.shape[:-2]
    view = ref.reshape(*lead, shape.rows_x + 2 * PAD_X + 1, shape.pitch, shape.depth)
    count = shape.rows_x - first if count is None else count
    return view.at[
        (slice(None),) * len(lead) + (pl.ds(PAD_X + first, count), pl.ds(RIM, shape.rows_y))
    ]


def vmem(shape):
    return pltpu.VMEM(shape, jnp.float32)


in_vmem = pl.BlockSpec(memory_space=pltpu.VMEM)
in_smem = pl.BlockSpec(memory_space=pltpu.SMEM)
in_hbm = pl.BlockSpec(memory_space=pltpu.HBM)


def call(body, ins, in_specs, out_shape, out_specs, flops, aliases=None, scratch=()):
    space = {id(in_vmem): pltpu.VMEM, id(in_hbm): pltpu.HBM}
    ins = [
        pltpu.with_memory_space_constraint(x, space[id(s)]) if id(s) in space else x
        for x, s in zip(ins, in_specs)
    ]
    return pl.pallas_call(
        body,
        in_specs=in_specs,
        out_shape=out_shape,
        out_specs=out_specs,
        input_output_aliases=aliases or {},
        scratch_shapes=scratch,
        cost_estimate=pl.CostEstimate(flops=flops, bytes_accessed=1000000, transcendentals=0),
        compiler_params=pltpu.CompilerParams(vmem_limit_bytes=16 * 1024 * 1024),
    )(*ins)


def swaps(axis, first, second):
    count = lax.axis_size(axis)
    got = []
    for start, block in ((0, first), (1, second)):
        pairs = []
        for low in range(start, count - 1, 2):
            pairs += [(low, low + 1), (low + 1, low)]
        got.append(lax.ppermute(block, axis, pairs))
    return got


def steps(
    velocity,
    stress,
    lame_first,
    modulus,
    buoyancy,
    zone,
    eligible,
    cohesion,
    friction,
    source_cell,
    source_moment,
):
    shape = Shape(*zone.shape)
    rows_x, rows_y, depth = zone.shape
    whole_s, whole_v = vmem((6, shape.rows, depth)), vmem((3, shape.rows, depth))
    whole_b, whole_h = vmem((shape.rows, depth)), vmem((3, shape.rows, depth))
    y_buffers = {first: vmem((y_count(first), rows_x, depth)) for first in (True, False)}
    late_buffer = vmem((late_count(shape), depth))
    early_buffer = vmem((early_count(shape), 8, depth))
    whole_r = vmem((5, (rows_x + 2 * BESIDE) * rows_y, depth))

    inner = (2, rows_x - 2)
    next_inner = (4, rows_x - 4)
    bands = range(0, rows_y, 8)

    def own_forces(lanes, s, v, b, x):
        for t in bands:
            push_velocity(shape, lanes, s, v, b, aligned(shape, x, t))

    def load(
        v_in, s_in, b_in, lame_in, shear_in, zone_in, able_in,
        s, v, b, h, first, second, x_first, x_second, floats, ints, sems, edge_sems,
    ):
        groups, edges = [], []
        marks = list(range(0, rows_x - 8, 8)) + [rows_x - 8, rows_x - 4, rows_x]
        for g, (x, stop) in enumerate(zip(marks, marks[1:])):
            group = []
            for i, (source, ref) in enumerate(((s_in, s), (v_in, v), (b_in, b))):
                span = pl.ds(x, stop - x)
                part = source.at[:, span] if i < 2 else source.at[span]
                place = own_cells(shape, ref, x, stop - x)
                group.append(pltpu.make_async_copy(part, place, sems.at[g, i]))
                group[-1].start()
            groups.append(group)
        for i, source in enumerate((lame_in, shear_in, zone_in, able_in)):
            ref = floats.at[i] if i < 2 else ints.at[i - 2]
            for side, x in enumerate((rows_x - BESIDE, 0)):
                part = source.at[pl.ds(x, BESIDE)]
                edges.append(pltpu.make_async_copy(part, ref.at[side], edge_sems.at[i, side]))
                edges[-1].start()

        def raw(c, side, x, t):
            if c < 2:
                return floats[c, side, x, pl.ds(t, 8), :]
            return ints[c - 2, side, x, pl.ds(t, 8), :].astype(jnp.float32)

        zero = jnp.zeros((8, depth), jnp.float32)
        for x in range(-2, rows_x + 3):
            for c in (XY, YY, YZ):
                s[c, pl.ds(shape.row(x, -RIM), 8), :] = zero
        for x in range(-2, rows_x + 2):
            for t in bands:
                for c in range(3):
                    h[c, pl.ds(shape.row(x, t), 8), :] = zero
        for x in (-2, -1, rows_x, rows_x + 1):
            for t in bands:
                for c in range(6):
                    s[c, pl.ds(shape.row(x, t), 8), :] = zero
        lanes = Lanes(depth)
        done = packed = 0
        for stop, group in zip(marks[1:], groups):
            for copy in group:
                copy.wait()
            stop = stop if stop == rows_x else stop - 2
            layers(done, stop, lambda x: own_forces(lanes, s, v, b, x), stop - done)
            done = stop
            ready = range(packed, done - 7, 8)
            if len(ready) > 0:
                send_y(shape, s, v, b, first, second, ready, done == rows_x)
                packed = ready[-1] + 8
        for copy in edges:
            copy.wait()
        send_early(shape, s, v, b, raw, x_first, x_second)

    s, v, b, h, first, second, x_first, x_second = call(
        load,
        [velocity, stress, buoyancy, lame_first, modulus, zone, eligible],
        [in_hbm] * 7,
        [whole_s, whole_v, whole_b, whole_h] + [y_buffers[True]] * 2 + [early_buffer] * 2,
        [in_vmem] * 8,
        10000000,
        scratch=[
            pltpu.VMEM((2, 2, BESIDE, rows_y, depth), jnp.float32),
            pltpu.VMEM((2, 2, BESIDE, rows_y, depth), jnp.int32),
            pltpu.SemaphoreType.DMA((rows_x // 8 + 1, 3)),
            pltpu.SemaphoreType.DMA((4, 2)),
        ],
    )

    def prepare(after, lame_in, shear_in, zone_in, able_in, cohesion, friction, rock):
        def layer(x):
            for t in bands:
                raw = [r[x, pl.ds(t, 8), :] for r in (lame_in, shear_in, zone_in, able_in)]
                fill_rock(shape, rock, x, t, cohesion, friction, *raw)

        layers(0, rows_x, layer, 8)

    early_rims = tuple(range(BESIDE + 1)), tuple(range(rows_x - BESIDE, rows_x + 1))
    early = tuple(range(5)), tuple(range(rows_x - 5, rows_x))

    def push_rim(s, v, b, x):
        for c, value in enumerate(across_y(s, b, aligned(shape, x, -RIM))):
            v[c, pl.ds(aligned(shape, x, -RIM), 8), :] += value

    def push_rows(v, b, h, x, keep=False):
        for t in bands:
            row = aligned(shape, x, t)
            scale = time_step * tile(b, row)
            for c in range(3):
                gain = scale * tile(h.at[c], row)
                v[c, pl.ds(row, 8), :] += gain
                if keep:
                    h[c, pl.ds(row, 8), :] = gain

    def turn(s, v_in, b_in, h_in, got_a, got_b, v, b, h, out_a, out_b):
        receive_y(shape, h, v, b, got_a, got_b)
        for x in early[0] + early[1]:
            push_rows(v, b, h, x, keep=True)
        for x in early_rims[0] + early_rims[1]:
            push_rim(s, v, b, x)
        send_late(shape, h, v, b, got_a, got_b, out_a, out_b)

    def interior(
        s_in, v_in, b_in, h, rock_in, early_a, early_b, cell, moment, cohesion, friction, s, v, b, rock
    ):
        lanes = Lanes(depth)
        layers(early[0][-1] + 1, early[1][0], lambda x: push_rows(v, b, h, x), 4)
        layers(early_rims[0][-1] + 1, early_rims[1][0], lambda x: push_rim(s, v, b, x), 4)
        receive_early(shape, s, v, b, rock, cohesion, friction, early_a, early_b)
        inject(shape, s, cell, moment, lambda x: (x >= -BESIDE) & (x < rows_x + BESIDE))
        layers(*inner, lambda x: push_stress(shape, lanes, s, v, rock, x), 4)
        layers(*next_inner, lambda x: own_forces(lanes, s, v, b, x), 4)

    def border(s_in, v_in, b, rock, got_a, got_b, sent_a, sent_b, s, v, out_a, out_b):
        receive_late(shape, v, b, (got_a, got_b), (sent_a, sent_b))
        lanes = Lanes(depth)
        for first, stop in ((-BESIDE, inner[0]), (inner[1], rows_x + BESIDE)):
            for x in range(first, stop):
                push_stress(shape, lanes, s, v, rock, x)
        for first, stop in ((-2, next_inner[0]), (next_inner[1], rows_x + 2)):
            for x in range(first, stop):
                own_forces(lanes, s, v, b, x)
        send_y(shape, s, v, None, out_a, out_b, range(0, rows_x, 8))

    def between(s_in, v_in, b, cell, moment, s, v):
        def rim(x):
            for c, value in enumerate(across_y(s, b, aligned(shape, x, -RIM))):
                v[c, pl.ds(aligned(shape, x, -RIM), 8), :] = value

        layers(0, rows_x + 1, rim, 3)
        inject(shape, s, cell, moment, lambda x: (x >= 0) & (x < rows_x))

    def finish(s_in, v_in, b, h_in, rock, got_a, got_b, s, v, h, v_out, s_out, sems):
        receive_y(shape, h, v, None, got_a, got_b, begun=True)
        lanes = Lanes(depth)
        layers(-2, rows_x + 2, lambda x: push_rows(v, b, h, x), 4)
        copies = [pltpu.make_async_copy(own_cells(shape, v), v_out, sems.at[0])]
        copies[0].start()
        for i, x in enumerate(range(0, rows_x, 8)):
            layers(x, x + 8, lambda x: push_stress(shape, lanes, s, v, rock, x), 8)
            part = s_out.at[:, pl.ds(x, 8)]
            copies.append(pltpu.make_async_copy(own_cells(shape, s, x, 8), part, sems.at[i + 1]))
            copies[-1].start()
        for c in copies:
            c.wait()

    cells = [source_cell, source_moment]
    first, second = swaps("gy", first, second)
    x_first, x_second = swaps("gx", x_first, x_second)
    v, b, h, sent_a, sent_b = call(
        turn,
        [s, v, b, h, first, second],
        [in_vmem] * 6,
        [whole_v, whole_b, whole_h, late_buffer, late_buffer],
        [in_vmem] * 5,
        1000000,
        aliases={1: 0, 2: 1, 3: 2},
    )
    got_a, got_b = swaps("gx", sent_a, sent_b)
    rock = call(
        prepare,
        [v, lame_first, modulus, zone, eligible, cohesion, friction],
        [in_vmem] * 5 + [in_smem] * 2,
        whole_r,
        in_vmem,
        10000000,
    )
    s, v, b, rock = call(
        interior,
        [s, v, b, h, rock, x_first, x_second] + cells + [cohesion, friction],
        [in_vmem] * 7 + [in_smem] * 4,
        [whole_s, whole_v, whole_b, whole_r],
        [in_vmem] * 4,
        10000000,
        aliases={0: 0, 1: 1, 2: 2, 4: 3},
    )
    s, v, first, second = call(
        border,
        [s, v, b, rock, got_a, got_b, sent_a, sent_b],
        [in_vmem] * 8,
        [whole_s, whole_v, y_buffers[False], y_buffers[False]],
        [in_vmem] * 4,
        10000000,
        aliases={0: 0, 1: 1},
    )
    first, second = swaps("gy", first, second)
    s, v = call(
        between,
        [s, v, b] + cells,
        [in_vmem] * 3 + [in_smem] * 2,
        [whole_s, whole_v],
        [in_vmem] * 2,
        10000000,
        aliases={0: 0, 1: 1},
    )
    outs = call(
        finish,
        [s, v, b, h, rock, first, second],
        [in_vmem] * 7,
        [
            whole_s,
            whole_v,
            whole_h,
            pltpu.HBM(velocity.shape, jnp.float32),
            pltpu.HBM(stress.shape, jnp.float32),
        ],
        [in_vmem] * 3 + [in_hbm] * 2,
        10000000,
        aliases={0: 0, 1: 1, 3: 2},
        scratch=[pltpu.SemaphoreType.DMA((rows_x // 8 + 1,))],
    )
    return (outs[3], outs[4])


def solution(mesh):
    placed = (
        P(None, "gx", "gy", None),
        P(None, "gx", "gy", None),
        P("gx", "gy", None),
        P("gx", "gy", None),
        P("gx", "gy", None),
        P("gx", "gy", None),
        P("gx", "gy", None),
        P(),
        P(),
        P(),
        P(),
    )
    return jax.shard_map(
        steps,
        mesh=mesh,
        in_specs=placed,
        out_specs=(P(None, "gx", "gy", None), P(None, "gx", "gy", None)),
        check_vma=False,
    )
```

time: 32.9 us -> 30.3 us (0.921)
  the two profiles are of different devices: /device:TPU:13 before, /device:TPU:19 now
where the time goes in v5:
time: 30.3 us; the launch traced here: 30.1 us
  starting transfers between devices  14.8 us (49%)
  Pallas kernels  9.26 us (31%)
  waiting for transfers between devices  5.16 us (17%)
  between operations  0.88 us (3%)
    ppermute x8, starting transfers between devices, swaps(): got.append(lax.ppermute(block, axis, pairs))  14.8 us
    pallas_call x7, Pallas kernels, call(): pl.pallas_call(body, in_specs=in_specs, out_shape=out_shape, out_specs=ou...  9.26 us
    ppermute x8, waiting for transfers between devices, swaps(): got.append(lax.ppermute(block, axis, pairs))  5.16 us
  transfers between devices with their start and end apart: 8, of which 2 were waited for; matrix products, arithmetic and copies ran while one was open for 0% of the time, Pallas kernels for 16%

profile of v5, /device:TPU:19, one launch (start us, length us, event | category | flops | bytes accessed | tf_op | source)
XLA Modules:
  0.0 30.1 jit_solution(14287449499690238143)
XLA Ops:
  0.6 2.1 %shard_map.122 = (f32[6,784,128]{2,1,0:T(8,128)S(1)}, f32[3,784,128]{2,1,0:T(8,128)S(1)}, f32[784,128]{1,0:T(8,128)S(1)}, f32[3,784,128]{2,1,0:T(8,128)S(1)}, f3...) custom-call(f32[3,32,8,128]{3,2,1,0:T(8,128)} %v_in.1, ...), custom_call_target="tpu_custom_call" | custom-call | flops 10000000 | bytes 1000000 | tf_op jit(solution)/shard_map/pallas_call | solution.py:522
  2.7 0.7 %collective-permute-start = (f32[12,32,128]{2,1,0:T(8,128)S(1)}, f32[12,32,128]{2,1,0:T(8,128)S(1)}, u32[]{:S(2)}, u32[]{:S(2)}) collective-permute-start(f32[12,32,128]{2,1,0:T(8,128)S(1)} %get-tuple-element.31), channel_id=1, source_target_pairs={{0,1},{1,0},{2,3},{3,2},{4,5},{5,4},{6,7},{7,6},{8,9},{9,8},{10,11... | collective-permute-start | bytes 589832 | tf_op jit(solution)/shard_map/ppermute | solution.py:541
  3.4 3.1 %collective-permute-start.1 = (f32[12,32,128]{2,1,0:T(8,128)S(1)}, f32[12,32,128]{2,1,0:T(8,128)S(1)}, u32[]{:S(2)}, u32[]{:S(2)}) collective-permute-start(f32[12,32,128]{2,1,0:T(8,128)S(1)} %get-tuple-element.32), channel_id=1, source_target_pairs={{1,2},{2,1},{3,4},{4,3},{5,6},{6,5},{9,10},{10,9},{11,12},{12,11},... | collective-permute-start | bytes 589832 | tf_op jit(solution)/shard_map/ppermute | solution.py:541
  6.6 0.3 %collective-permute-start.2 = (f32[46,8,128]{2,1,0:T(8,128)S(1)}, f32[46,8,128]{2,1,0:T(8,128)S(1)}, u32[]{:S(2)}, u32[]{:S(2)}) collective-permute-start(f32[46,8,128]{2,1,0:T(8,128)S(1)} %get-tuple-element.36), channel_id=1, source_target_pairs={{0,8},{8,0},{16,24},{24,16},{1,9},{9,1},{17,25},{25,17},{2,10},{10... | collective-permute-start | bytes 565256 | tf_op jit(solution)/shard_map/ppermute | solution.py:541
  6.9 4.1 %collective-permute-start.3 = (f32[46,8,128]{2,1,0:T(8,128)S(1)}, f32[46,8,128]{2,1,0:T(8,128)S(1)}, u32[]{:S(2)}, u32[]{:S(2)}) collective-permute-start(f32[46,8,128]{2,1,0:T(8,128)S(1)} %get-tuple-element.37), channel_id=1, source_target_pairs={{8,16},{16,8},{9,17},{17,9},{10,18},{18,10},{11,19},{19,11},{12,20... | collective-permute-start | bytes 565256 | tf_op jit(solution)/shard_map/ppermute | solution.py:541
  10.9 0.0 collective-permute-done.got_a
  11.0 0.0 collective-permute-done.1.got_b
  11.0 0.0 copy-start
  11.0 0.0 copy-start.1
  11.0 0.0 copy-start.2
  11.0 0.0 copy-start.3
  11.0 0.0 copy-start.5
  11.0 0.0 copy-start.6
  11.0 0.3 %shard_map.123 = (f32[3,784,128]{2,1,0:T(8,128)S(1)}, f32[784,128]{1,0:T(8,128)S(1)}, f32[3,784,128]{2,1,0:T(8,128)S(1)}, f32[96,128]{1,0:T(8,128)S(1)}, f32[96,128]{1,0:T(8,128)S(1)}) custom-call(f32[6,784,128]{2,1,0:T(8,128)S(1)} %get-tuple-element.27.s.s_in, ...), custom_call_target="tpu_custom_call", output_to_operand_aliasing={{0}: (1, {}), {1}: (2, {}), {2}: (3, {})} | custom-call | flops 1000000 | bytes 1000000 | tf_op jit(solution)/shard_map/pallas_call | solution.py:522
  11.4 0.1 collective-permute-start.4
  11.4 4.0 %collective-permute-start.5 = (f32[96,128]{1,0:T(8,128)S(1)}, f32[96,128]{1,0:T(8,128)S(1)}, u32[]{:S(2)}, u32[]{:S(2)}) collective-permute-start(f32[96,128]{1,0:T(8,128)S(1)} %get-tuple-element.43.sent_b), channel_id=1, source_target_pairs={{8,16},{16,8},{9,17},{17,9},{10,18},{18,10},{11,19},{19,11},{12,20... | collective-permute-start | bytes 147464 | tf_op jit(solution)/shard_map/ppermute | solution.py:541
  15.5 0.0 copy-done
  15.5 0.0 copy-done.1
  15.5 0.0 copy-done.2
  15.5 0.0 copy-done.3
  15.5 0.0 copy-done.5
  15.5 0.0 copy-done.6
  15.5 0.0 copy-start.4
  15.5 0.0 copy-start.7
  15.5 0.7 %shard_map.124.rock_in = f32[5,304,128]{2,1,0:T(8,128)S(1)} custom-call(f32[3,784,128]{2,1,0:T(8,128)S(1)} %get-tuple-element.33.after.v_in, f32[32,8,128]{2,1,0:T(8,128)S(1)} %copy-done, f32[32,8,128]{2,1,0:T(8,128)S(1)} %copy-done.1, s32[32,8,128]{2,1,0:T(8,128)S(1)} %copy-done.2, s32[32,8,128]{2,1,0:T(8,128)S(1)} %copy-done.3, f32[8]{0:T(128)S(1)} %copy-done.5, ...), custom_call_target="tpu_custom_call" | custom-call | flops 10000000 | bytes 1000000 | tf_op jit(solution)/shard_map/pallas_call | solution.py:522
  16.3 0.0 collective-permute-done.2.early_a
  16.3 1.8 %collective-permute-done.3.early_b = f32[46,8,128]{2,1,0:T(8,128)S(1)} collective-permute-done((f32[46,8,128]{2,1,0:T(8,128)S(1)}, f32[46,8,128]{2,1,0:T(8,128)S(1)}, u32[]{:S(2)}, u32[]{:S(2)}) %collective-permute-start.3) | collective-permute-done | bytes 188448 | tf_op jit(solution)/shard_map/ppermute | solution.py:541
  18.1 0.0 copy-done.4
  18.1 0.0 copy-done.7
  18.1 2.7 %shard_map.125 = (f32[6,784,128]{2,1,0:T(8,128)S(1)}, f32[3,784,128]{2,1,0:T(8,128)S(1)}, f32[784,128]{1,0:T(8,128)S(1)}, f32[5,304,128]{2,1,0:T(8,128)S(1)}) custom-call(f32[6,784,128]{2,1,0:T(8,128)S(1)} %get-tuple-element.27.s.s_in, ...), custom_call_target="tpu_custom_call", output_to_operand_aliasing={{0}: (0, {}), {1}: (1, {}), {2}: (2, {}), {3}: (4, {})} | custom-call | flops 10000000 | bytes 1000000 | tf_op jit(solution)/shard_map/pallas_call | solution.py:522
  20.8 0.0 collective-permute-done.4.got_a
  20.8 0.0 collective-permute-done.5.got_b
  20.8 0.6 %shard_map.126 = (f32[6,784,128]{2,1,0:T(8,128)S(1)}, f32[3,784,128]{2,1,0:T(8,128)S(1)}, f32[10,32,128]{2,1,0:T(8,128)S(1)}, f32[10,32,128]{2,1,0:T(8,128)S(1)}) custom-call(f32[6,784,128]{2,1,0:T(8,128)S(1)} %get-tuple-element.38.s_in, f32[3,784,128]{2,1,0:T(8,128)S(1)} %get-tuple-element.39.v_in, ...), custom_call_target="tpu_custom_call", output_to_operand_aliasing={{0}: (0, {}), {1}: (1, {})} | custom-call | flops 10000000 | bytes 1000000 | tf_op jit(solution)/shard_map/pallas_call | solution.py:522
  21.4 0.4 %collective-permute-start.6 = (f32[10,32,128]{2,1,0:T(8,128)S(1)}, f32[10,32,128]{2,1,0:T(8,128)S(1)}, u32[]{:S(2)}, u32[]{:S(2)}) collective-permute-start(f32[10,32,128]{2,1,0:T(8,128)S(1)} %get-tuple-element.48), channel_id=1, source_target_pairs={{0,1},{1,0},{2,3},{3,2},{4,5},{5,4},{6,7},{7,6},{8,9},{9,8},{10,11... | collective-permute-start | bytes 491528 | tf_op jit(solution)/shard_map/ppermute | solution.py:541
  21.8 2.1 %collective-permute-start.7 = (f32[10,32,128]{2,1,0:T(8,128)S(1)}, f32[10,32,128]{2,1,0:T(8,128)S(1)}, u32[]{:S(2)}, u32[]{:S(2)}) collective-permute-start(f32[10,32,128]{2,1,0:T(8,128)S(1)} %get-tuple-element.49), channel_id=1, source_target_pairs={{1,2},{2,1},{3,4},{4,3},{5,6},{6,5},{9,10},{10,9},{11,12},{12,11},... | collective-permute-start | bytes 491528 | tf_op jit(solution)/shard_map/ppermute | solution.py:541
  23.9 1.1 %shard_map.127 = (f32[6,784,128]{2,1,0:T(8,128)S(1)}, f32[3,784,128]{2,1,0:T(8,128)S(1)}) custom-call(f32[6,784,128]{2,1,0:T(8,128)S(1)} %get-tuple-element.44.s_in, f32[3,784,128]{2,1,0:T(8,128)S(1)} %get-tuple-element.45.v_in, f32[784,128]{1,0:T(8,128)S(1)} %get-tuple-element.40.b, s32[16]{0:T(128)S(1)} %copy-done.7, ...), custom_call_target="tpu_custom_call", output_to_operand_aliasing={{0}: (0, {}), {1}: (1, {})} | custom-call | flops 10000000 | bytes 1000000 | tf_op jit(solution)/shard_map/pallas_call | solution.py:522
  25.0 0.0 collective-permute-done.6.got_a
  25.1 3.4 %collective-permute-done.7.got_b = f32[10,32,128]{2,1,0:T(8,128)S(1)} collective-permute-done((f32[10,32,128]{2,1,0:T(8,128)S(1)}, f32[10,32,128]{2,1,0:T(8,128)S(1)}, u32[]{:S(2)}, u32[]{:S(2)}) %collective-permute-start.7) | collective-permute-done | bytes 163872 | tf_op jit(solution)/shard_map/ppermute | solution.py:541
  28.4 1.7 %shard_map.128 = (f32[6,784,128]{2,1,0:T(8,128)S(1)}, f32[3,784,128]{2,1,0:T(8,128)S(1)}, f32[3,784,128]{2,1,0:T(8,128)S(1)}, f32[3,32,8,128]{3,2,1,0:T(8,128)}, f32[6,32,8,128]{3,2,1,0:T(8,128)}) custom-call(f32[6,784,128]{2,1,0:T(8,128)S(1)} %get-tuple-element.46.s_in, ...), custom_call_target="tpu_custom_call", output_to_operand_aliasing={{0}: (0, {}), {1}: (1, {}), {2}: (3, {})} | custom-call | flops 10000000 | bytes 1000000 | tf_op jit(solution)/shard_map/pallas_call | solution.py:522
Async XLA Ops:
  2.7 8.2 %collective-permute-start = (f32[12,32,128]{2,1,0:T(8,128)S(1)}, f32[12,32,128]{2,1,0:T(8,128)S(1)}, u32[]{:S(2)}, u32[]{:S(2)}) collective-permute-start(f32[12,32,128]{2,1,0:T(8,128)S(1)} %get-tuple-element.31), channel_id=1, source_target_pairs={{0,1},{1,0},{2,3},{3,2},{4,5},{5,4},{6,7},{7,6},{8,9},{9,8},{10,11... | collective-permute-start | bytes 589832 | tf_op jit(solution)/shard_map/ppermute | solution.py:541
  3.4 7.5 %collective-permute-start.1 = (f32[12,32,128]{2,1,0:T(8,128)S(1)}, f32[12,32,128]{2,1,0:T(8,128)S(1)}, u32[]{:S(2)}, u32[]{:S(2)}) collective-permute-start(f32[12,32,128]{2,1,0:T(8,128)S(1)} %get-tuple-element.32), channel_id=1, source_target_pairs={{1,2},{2,1},{3,4},{4,3},{5,6},{6,5},{9,10},{10,9},{11,12},{12,11},... | collective-permute-start | bytes 589832 | tf_op jit(solution)/shard_map/ppermute | solution.py:541
  6.6 9.7 %collective-permute-start.2 = (f32[46,8,128]{2,1,0:T(8,128)S(1)}, f32[46,8,128]{2,1,0:T(8,128)S(1)}, u32[]{:S(2)}, u32[]{:S(2)}) collective-permute-start(f32[46,8,128]{2,1,0:T(8,128)S(1)} %get-tuple-element.36), channel_id=1, source_target_pairs={{0,8},{8,0},{16,24},{24,16},{1,9},{9,1},{17,25},{25,17},{2,10},{10... | collective-permute-start | bytes 565256 | tf_op jit(solution)/shard_map/ppermute | solution.py:541
  6.9 11.2 %collective-permute-start.3 = (f32[46,8,128]{2,1,0:T(8,128)S(1)}, f32[46,8,128]{2,1,0:T(8,128)S(1)}, u32[]{:S(2)}, u32[]{:S(2)}) collective-permute-start(f32[46,8,128]{2,1,0:T(8,128)S(1)} %get-tuple-element.37), channel_id=1, source_target_pairs={{8,16},{16,8},{9,17},{17,9},{10,18},{18,10},{11,19},{19,11},{12,20... | collective-permute-start | bytes 565256 | tf_op jit(solution)/shard_map/ppermute | solution.py:541
  11.0 4.5 %copy-start = (f32[32,8,128]{2,1,0:T(8,128)S(1)}, f32[32,8,128]{2,1,0:T(8,128)}, u32[]{:S(2)}) copy-start(f32[32,8,128]{2,1,0:T(8,128)} %lame_in.3) | copy-start | bytes 393220
  11.0 4.5 %copy-start.1 = (f32[32,8,128]{2,1,0:T(8,128)S(1)}, f32[32,8,128]{2,1,0:T(8,128)}, u32[]{:S(2)}) copy-start(f32[32,8,128]{2,1,0:T(8,128)} %shear_in.3) | copy-start | bytes 393220
  11.0 4.5 %copy-start.2 = (s32[32,8,128]{2,1,0:T(8,128)S(1)}, s32[32,8,128]{2,1,0:T(8,128)}, u32[]{:S(2)}) copy-start(s32[32,8,128]{2,1,0:T(8,128)} %zone_in.3) | copy-start | bytes 393220
  11.0 4.5 %copy-start.3 = (s32[32,8,128]{2,1,0:T(8,128)S(1)}, s32[32,8,128]{2,1,0:T(8,128)}, u32[]{:S(2)}) copy-start(s32[32,8,128]{2,1,0:T(8,128)} %able_in.3) | copy-start | bytes 393220
  11.0 4.5 %copy-start.5 = (f32[8]{0:T(128)S(1)}, f32[8]{0:T(128)}, u32[]{:S(2)}) copy-start(f32[8]{0:T(128)} %cohesion.3) | copy-start | bytes 100
  11.0 4.5 %copy-start.6 = (f32[8]{0:T(128)S(1)}, f32[8]{0:T(128)}, u32[]{:S(2)}) copy-start(f32[8]{0:T(128)} %friction.3) | copy-start | bytes 100
  11.4 9.5 %collective-permute-start.4 = (f32[96,128]{1,0:T(8,128)S(1)}, f32[96,128]{1,0:T(8,128)S(1)}, u32[]{:S(2)}, u32[]{:S(2)}) collective-permute-start(f32[96,128]{1,0:T(8,128)S(1)} %get-tuple-element.42.sent_a), channel_id=1, source_target_pairs={{0,8},{8,0},{16,24},{24,16},{1,9},{9,1},{17,25},{25,17},{2,10},{10... | collective-permute-start | bytes 147464 | tf_op jit(solution)/shard_map/ppermute | solution.py:541
  11.4 9.4 %collective-permute-start.5 = (f32[96,128]{1,0:T(8,128)S(1)}, f32[96,128]{1,0:T(8,128)S(1)}, u32[]{:S(2)}, u32[]{:S(2)}) collective-permute-start(f32[96,128]{1,0:T(8,128)S(1)} %get-tuple-element.43.sent_b), channel_id=1, source_target_pairs={{8,16},{16,8},{9,17},{17,9},{10,18},{18,10},{11,19},{19,11},{12,20... | collective-permute-start | bytes 147464 | tf_op jit(solution)/shard_map/ppermute | solution.py:541
  15.5 2.5 %copy-start.4 = (f32[6,16]{1,0:T(8,128)S(1)}, f32[6,16]{1,0:T(8,128)}, u32[]{:S(2)}) copy-start(f32[6,16]{1,0:T(8,128)} %moment.3) | copy-start | bytes 1156
  15.5 2.5 %copy-start.7 = (s32[16]{0:T(128)S(1)}, s32[16]{0:T(128)}, u32[]{:S(2)}) copy-start(s32[16]{0:T(128)} %cell.3) | copy-start | bytes 196
  21.4 3.6 %collective-permute-start.6 = (f32[10,32,128]{2,1,0:T(8,128)S(1)}, f32[10,32,128]{2,1,0:T(8,128)S(1)}, u32[]{:S(2)}, u32[]{:S(2)}) collective-permute-start(f32[10,32,128]{2,1,0:T(8,128)S(1)} %get-tuple-element.48), channel_id=1, source_target_pairs={{0,1},{1,0},{2,3},{3,2},{4,5},{5,4},{6,7},{7,6},{8,9},{9,8},{10,11... | collective-permute-start | bytes 491528 | tf_op jit(solution)/shard_map/ppermute | solution.py:541
  21.8 6.6 %collective-permute-start.7 = (f32[10,32,128]{2,1,0:T(8,128)S(1)}, f32[10,32,128]{2,1,0:T(8,128)S(1)}, u32[]{:S(2)}, u32[]{:S(2)}) collective-permute-start(f32[10,32,128]{2,1,0:T(8,128)S(1)} %get-tuple-element.49), channel_id=1, source_target_pairs={{1,2},{2,1},{3,4},{4,3},{5,6},{6,5},{9,10},{10,9},{11,12},{12,11},... | collective-permute-start | bytes 491528 | tf_op jit(solution)/shard_map/ppermute | solution.py:541

commit v6 on v5

--- a/solution.py
+++ b/solution.py
@@ -186,29 +186,23 @@
     return most + 1 + (2 if first_round else 0)
 
 
-def early_slots(shape, side):
+def early_slots(shape):
     bands = range(0, shape.rows_y, 8)
-    deep = (LOW_DEEP_X, HIGH_DEEP_X)[side]
     keys = [("s", c, k, t) for c in range(6) for k in range(BESIDE) for t in bands]
     keys += [("r", c, k, t) for c in range(4) for k in range(BESIDE) for t in bands]
     keys += [("b", 0, k, t) for k in range(2) for t in bands]
-    keys += [("v", c, k, t) for c, k in entries(deep) for t in bands]
     return {key: i for i, key in enumerate(keys)}
 
 
-def early_count(shape):
-    return max(len(early_slots(shape, side)) for side in (0, 1))
-
-
-def send_early(shape, stress, flow, buoyancy, raw, first, second):
+def send_early(shape, stress, buoyancy, raw, first, second):
     def fill(out, side, place):
-        for (kind, c, k, t), slot in early_slots(shape, side).items():
+        for (kind, c, k, t), slot in early_slots(shape).items():
             x = place(k)
             if kind == "r":
                 at = x - (shape.rows_x - BESIDE if side == 0 else 0)
                 out[slot] = raw(c, side, at, t)
             else:
-                ref = buoyancy if kind == "b" else (stress if kind == "s" else flow).at[c]
+                ref = buoyancy if kind == "b" else stress.at[c]
                 out[slot] = tile(ref, shape.row(x, t))
 
     def body(below, above):
@@ -218,24 +212,24 @@
     by_parity("gx", body, (first, second))
 
 
-def receive_early(shape, stress, flow, buoyancy, rock, cohesion, friction, first, second):
-    def take(got, side, place):
-        slots = early_slots(shape, side)
+def receive_early(shape, stress, flow, buoyancy, rock, table, first, second):
+    zones = [(table[0, k], table[1, k]) for k in range(table.shape[1])]
+
+    def take(got, place):
+        slots = early_slots(shape)
         for (kind, c, k, t), slot in slots.items():
             x = place(k)
             if kind == "s":
                 stress[c, pl.ds(shape.row(x, t), 8), :] = got[slot]
             elif kind == "b":
                 buoyancy[pl.ds(shape.row(x, t), 8), :] = got[slot]
-            elif kind == "v":
-                flow[c, pl.ds(shape.row(x, t), 8), :] = got[slot]
             elif c == 0:
                 raw = [got[slots["r", i, k, t]] for i in range(4)]
-                fill_rock(shape, rock, x, t, cohesion, friction, *raw)
+                fill_rock(shape, rock, x, t, zones, *raw)
 
     def body(below, above):
-        take(below, 0, lambda k: -1 - k)
-        take(above, 1, lambda k: shape.rows_x + k)
+        take(below, lambda k: -1 - k)
+        take(above, lambda k: shape.rows_x + k)
 
     by_parity("gx", body, (first, second))
     for t in range(0, shape.rows_y, 8):
@@ -249,21 +243,23 @@
             for targets, sources in ((inside, outside), (outside, inside)):
                 for x in targets:
                     force = crossing_x(c, x, sources)
+                    row = shape.row(x, t)
                     if force is not None:
-                        row = shape.row(x, t)
-                        flow[c, pl.ds(row, 8), :] += time_step * tile(buoyancy, row) * force
-
-
-def fill_rock(shape, rock, x, t, cohesion, friction, first, shear, which, able):
-    hold = jnp.full((8, shape.depth), cohesion[0], jnp.float32)
-    rub = jnp.full((8, shape.depth), friction[0], jnp.float32)
-    for k in range(1, cohesion.shape[0]):
+                        force = time_step * tile(buoyancy, row) * force
+                        if x in inside:
+                            force = flow[c, pl.ds(row, 8), :] + force
+                        flow[c, pl.ds(row, 8), :] = force
+
+
+def fill_rock(shape, rock, x, t, zones, first, shear, which, able):
+    hold, rub = zones[0]
+    for k, (cohesion, friction) in enumerate(zones):
         hit = which == k
-        hold = jnp.where(hit, cohesion[k], hold)
-        rub = jnp.where(hit, friction[k], rub)
+        hold = jnp.where(hit, cohesion, hold)
+        rub = jnp.where(hit, friction, rub)
     own = pl.multiple_of((x + BESIDE) * shape.rows_y + t, 8)
-    rock[0, pl.ds(own, 8), :] = first
-    rock[1, pl.ds(own, 8), :] = shear
+    rock[0, pl.ds(own, 8), :] = time_step * first
+    rock[1, pl.ds(own, 8), :] = time_step * shear
     rock[2, pl.ds(own, 8), :] = hold * jnp.sqrt(1.0 - rub * rub)
     rock[3, pl.ds(own, 8), :] = rub
     rock[4, pl.ds(own, 8), :] = jnp.where(able == 1, 1.0, 0.0)
@@ -271,9 +267,8 @@
 
 def late_rows(shape, side):
     spec, deep = ((LOW_X, LOW_DEEP_X), (HIGH_X, HIGH_DEEP_X))[side]
-    reached = pushed(LOW_PUSH, shape) + pushed(HIGH_PUSH, shape)
     rims = rim_rows(LOW_FLOW_Y, shape) + rim_rows(HIGH_FLOW_Y, shape)
-    keys = [("d", c, k, y) for c, k in entries(deep) for which, y in reached if which == c]
+    keys = [("d", c, k, y) for c, k in entries(deep) for y in range(shape.rows_y)]
     keys += [("v", c, k, y) for k in range(BESIDE) for c, y in rims]
     sides = side_rows(LOW_FLOW_Y, shape) + side_rows(HIGH_FLOW_Y, shape)
     keys += [("b", 0, k, y) for k in range(2) for y in sides]
@@ -286,7 +281,7 @@
     return -(-max(len(late_rows(shape, side)) for side in (0, 1)) // 8) * 8
 
 
-def send_late(shape, force, flow, buoyancy, got_first, got_second, first, second):
+def send_late(shape, flow, buoyancy, got_first, got_second, first, second):
     layer_at = {x: i for i, x in enumerate(edge_layers(shape))}
 
     def fill(out, side, place, got_below, got_above):
@@ -296,11 +291,15 @@
                 singles[key] = (got, j)
         for (kind, c, k, y), at in late_rows(shape, side).items():
             x = place(k)
+            if kind == "d":
+                if y % 8 == 0:
+                    out[pl.ds(at, 8), :] = tile(flow.at[c], shape.row(x, y))
+                continue
             if kind == "s":
                 got, j = singles[c, y]
                 row = got[got.shape[0] - 1, pl.ds(8 * layer_at[x] + j, 1), :]
             else:
-                ref = {"d": force, "v": flow}[kind].at[c] if kind != "b" else buoyancy
+                ref = flow.at[c] if kind == "v" else buoyancy
                 row = ref[pl.ds(shape.row(x, y), 1), :]
             out[pl.ds(at, 1), :] = row
 
@@ -323,7 +322,9 @@
     def body(below, above, sent_below, sent_above):
         def read(sides):
             return {
-                (kind, c, place(k), y): (lambda ref=ref, at=at: ref[pl.ds(at, 1), :])
+                (kind, c, place(k), y): (
+                    lambda ref=ref, at=at, n=8 if kind == "d" else 1: ref[pl.ds(at, n), :]
+                )
                 for ref, side, place in sides
                 for (kind, c, k, y), at in late_rows(shape, side).items()
             }
@@ -334,9 +335,16 @@
         def rims(of, c, y):
             return {x: f for (kind, which, x, at), f in of.items() if (kind, which, at) == ("s", c, y)}
 
+        met = {
+            (c, x)
+            for c in range(3)
+            for x in beside_layers(shape)
+            if crossing_x(c, x, {e: lambda: 0.0 for e in edge_layers(shape)}) is not None
+        }
         for (kind, c, x, y), value in came.items():
-            if kind == "d":
-                add(c, x, y, value())
+            if kind == "d" and y % 8 == 0:
+                place = pl.ds(shape.row(x, y), 8)
+                flow[c, place, :] = flow[c, place, :] + value() if (c, x) in met else value()
         for c, y in rim_rows(LOW_FLOW_Y, shape) + rim_rows(HIGH_FLOW_Y, shape):
             halo, own = rims(came, c, y), rims(went, c, y)
             for x in edge_layers(shape):
@@ -430,28 +438,30 @@
     return pl.multiple_of((x + PAD_X) * shape.pitch + RIM + y, 8)
 
 
-def inject(shape, stress, source_cell, source_moment, wanted):
+INJECTION = 5
+
+
+def inject(shape, rock, source_cell, source_moment):
     rows_x, rows_y, depth = shape.rows_x, shape.rows_y, shape.depth
     total_y = rows_y * lax.axis_size("gy")
-    start_x = lax.axis_index("gx") * rows_x
+    start_x = lax.axis_index("gx") * rows_x - BESIDE
     start_y = lax.axis_index("gy") * rows_y
     sub = lax.broadcasted_iota(jnp.int32, (8, depth), 0)
     lane = lax.broadcasted_iota(jnp.int32, (8, depth), 1)
+    unread = (rows_x + 2 * BESIDE) * rows_y
     for s in range(source_cell.shape[0]):
         cell = source_cell[s]
         line = lax.div(cell, depth)
         x = lax.div(line, total_y) - start_x
         y = lax.rem(line, total_y) - start_y
         z = lax.rem(cell, depth)
-
-        @pl.when(wanted(x) & (y >= 0) & (y < rows_y))
-        def _(x=x, y=y, z=z, s=s):
-            band = lax.div(y, 8) * 8
-            row = aligned(shape, x, band)
-            here = (sub == y - band) & (lane == z)
-            for c in range(6):
-                amount = time_step * source_moment[c, s]
-                stress[c, pl.ds(row, 8), :] += jnp.where(here, amount, 0.0)
+        here = (x >= 0) & (x < rows_x + 2 * BESIDE) & (y >= 0) & (y < rows_y)
+        band = lax.div(jnp.where(here, y, 0), 8) * 8
+        row = pl.multiple_of(jnp.where(here, x * rows_y + band, unread), 8)
+        spot = (sub == y - band) & (lane == z)
+        for c in range(6):
+            amount = time_step * source_moment[c, s]
+            rock[INJECTION + c, pl.ds(row, 8), :] += jnp.where(spot, amount, 0.0)
 
 
 def push_stress(shape, lanes, stress, flow, rock, x):
@@ -461,22 +471,25 @@
     for t in range(0, shape.rows_y, 8):
         row = aligned(shape, x, t)
         own = pl.multiple_of((x + BESIDE) * shape.rows_y + t, 8)
-        first = time_step * rock[0, pl.ds(own, 8), :]
-        shear = time_step * rock[1, pl.ds(own, 8), :]
+        first = rock[0, pl.ds(own, 8), :]
+        shear = rock[1, pl.ds(own, 8), :]
+        base = [
+            tile(stress.at[c], row) + rock[INJECTION + c, pl.ds(own, 8), :] for c in range(6)
+        ]
         strain_x = backward(vx, row, sx)
         strain_y = backward(vy, row, sy)
         here_z = tile(vz, row)
         strain_z = lanes.backward(here_z)
         volume = first * (strain_x + strain_y + strain_z)
         twice = 2.0 * shear
-        xx = tile(stress.at[XX], row) + (volume + twice * strain_x)
-        yy = tile(stress.at[YY], row) + (volume + twice * strain_y)
-        zz = tile(stress.at[ZZ], row) + (volume + twice * strain_z)
-        xy = tile(stress.at[XY], row) + shear * (forward(vx, row, sy) + forward(vy, row, sx))
-        xz = tile(stress.at[XZ], row) + shear * (
+        xx = base[XX] + (volume + twice * strain_x)
+        yy = base[YY] + (volume + twice * strain_y)
+        zz = base[ZZ] + (volume + twice * strain_z)
+        xy = base[XY] + shear * (forward(vx, row, sy) + forward(vy, row, sx))
+        xz = base[XZ] + shear * (
             lanes.forward(tile(vx, row)) + forward(vz, row, sx)
         )
-        yz = tile(stress.at[YZ], row) + shear * (
+        yz = base[YZ] + shear * (
             lanes.forward(tile(vy, row)) + forward(vz, row, sy)
         )
         pressure = (xx + yy + zz) * (1.0 / 3.0)
@@ -561,11 +574,11 @@
     whole_b, whole_h = vmem((shape.rows, depth)), vmem((3, shape.rows, depth))
     y_buffers = {first: vmem((y_count(first), rows_x, depth)) for first in (True, False)}
     late_buffer = vmem((late_count(shape), depth))
-    early_buffer = vmem((early_count(shape), 8, depth))
-    whole_r = vmem((5, (rows_x + 2 * BESIDE) * rows_y, depth))
-
-    inner = (2, rows_x - 2)
-    next_inner = (4, rows_x - 4)
+    early_buffer = vmem((len(early_slots(shape)), 8, depth))
+    whole_r = vmem((INJECTION + 6, (rows_x + 2 * BESIDE) * rows_y + 8, depth))
+
+    inner = (4, rows_x - 4)
+    next_inner = (6, rows_x - 6)
     bands = range(0, rows_y, 8)
 
     def own_forces(lanes, s, v, b, x):
@@ -574,7 +587,7 @@
 
     def load(
         v_in, s_in, b_in, lame_in, shear_in, zone_in, able_in,
-        s, v, b, h, first, second, x_first, x_second, floats, ints, sems, edge_sems,
+        s, v, b, h, first, second, floats, ints, sems, edge_sems,
     ):
         groups, edges = [], []
         marks = list(range(0, rows_x - 8, 8)) + [rows_x - 8, rows_x - 4, rows_x]
@@ -593,11 +606,6 @@
                 part = source.at[pl.ds(x, BESIDE)]
                 edges.append(pltpu.make_async_copy(part, ref.at[side], edge_sems.at[i, side]))
                 edges[-1].start()
-
-        def raw(c, side, x, t):
-            if c < 2:
-                return floats[c, side, x, pl.ds(t, 8), :]
-            return ints[c - 2, side, x, pl.ds(t, 8), :].astype(jnp.float32)
 
         zero = jnp.zeros((8, depth), jnp.float32)
         for x in range(-2, rows_x + 3):
@@ -625,30 +633,56 @@
                 packed = ready[-1] + 8
         for copy in edges:
             copy.wait()
-        send_early(shape, s, v, b, raw, x_first, x_second)
-
-    s, v, b, h, first, second, x_first, x_second = call(
+
+    edge = (2, 2, BESIDE, rows_y, depth)
+    s, v, b, h, first, second, floats, ints = call(
         load,
         [velocity, stress, buoyancy, lame_first, modulus, zone, eligible],
         [in_hbm] * 7,
-        [whole_s, whole_v, whole_b, whole_h] + [y_buffers[True]] * 2 + [early_buffer] * 2,
+        [whole_s, whole_v, whole_b, whole_h, y_buffers[True], y_buffers[True], vmem(edge)]
+        + [pltpu.VMEM(edge, jnp.int32)],
         [in_vmem] * 8,
         10000000,
         scratch=[
-            pltpu.VMEM((2, 2, BESIDE, rows_y, depth), jnp.float32),
-            pltpu.VMEM((2, 2, BESIDE, rows_y, depth), jnp.int32),
             pltpu.SemaphoreType.DMA((rows_x // 8 + 1, 3)),
             pltpu.SemaphoreType.DMA((4, 2)),
         ],
     )
 
-    def prepare(after, lame_in, shear_in, zone_in, able_in, cohesion, friction, rock):
+    def pack(s, b, floats, ints, x_first, x_second):
+        def raw(c, side, x, t):
+            if c < 2:
+                return floats[c, side, x, pl.ds(t, 8), :]
+            return ints[c - 2, side, x, pl.ds(t, 8), :].astype(jnp.float32)
+
+        send_early(shape, s, b, raw, x_first, x_second)
+
+    x_first, x_second = call(
+        pack, [s, b, floats, ints], [in_vmem] * 4, [early_buffer] * 2, [in_vmem] * 2, 1000000
+    )
+
+    def prepare(
+        after, lame_in, shear_in, zone_in, able_in, cohesion, friction, cell, moment, rock, table
+    ):
+        zones = [
+            [jnp.full((8, depth), r[k], jnp.float32) for r in (cohesion, friction)]
+            for k in range(cohesion.shape[0])
+        ]
+        for k, both in enumerate(zones):
+            for i, value in enumerate(both):
+                table[i, k] = value
+        zero = jnp.zeros((8, depth), jnp.float32)
+        for c in range(INJECTION, INJECTION + 6):
+            for row in range(0, rock.shape[1], 8):
+                rock[c, pl.ds(row, 8), :] = zero
+
         def layer(x):
             for t in bands:
                 raw = [r[x, pl.ds(t, 8), :] for r in (lame_in, shear_in, zone_in, able_in)]
-                fill_rock(shape, rock, x, t, cohesion, friction, *raw)
+                fill_rock(shape, rock, x, t, zones, *raw)
 
         layers(0, rows_x, layer, 8)
+        inject(shape, rock, cell, moment)
 
     early_rims = tuple(range(BESIDE + 1)), tuple(range(rows_x - BESIDE, rows_x + 1))
     early = tuple(range(5)), tuple(range(rows_x - 5, rows_x))
@@ -657,34 +691,30 @@
         for c, value in enumerate(across_y(s, b, aligned(shape, x, -RIM))):
             v[c, pl.ds(aligned(shape, x, -RIM), 8), :] += value
 
-    def push_rows(v, b, h, x, keep=False):
+    def push_rows(v, b, h, x):
         for t in bands:
             row = aligned(shape, x, t)
             scale = time_step * tile(b, row)
             for c in range(3):
-                gain = scale * tile(h.at[c], row)
-                v[c, pl.ds(row, 8), :] += gain
-                if keep:
-                    h[c, pl.ds(row, 8), :] = gain
+                v[c, pl.ds(row, 8), :] += scale * tile(h.at[c], row)
 
     def turn(s, v_in, b_in, h_in, got_a, got_b, v, b, h, out_a, out_b):
         receive_y(shape, h, v, b, got_a, got_b)
         for x in early[0] + early[1]:
-            push_rows(v, b, h, x, keep=True)
+            push_rows(v, b, h, x)
         for x in early_rims[0] + early_rims[1]:
             push_rim(s, v, b, x)
-        send_late(shape, h, v, b, got_a, got_b, out_a, out_b)
-
-    def interior(
-        s_in, v_in, b_in, h, rock_in, early_a, early_b, cell, moment, cohesion, friction, s, v, b, rock
-    ):
+        send_late(shape, v, b, got_a, got_b, out_a, out_b)
+
+    def interior(s_in, v_in, b, h, rock, s, v):
         lanes = Lanes(depth)
         layers(early[0][-1] + 1, early[1][0], lambda x: push_rows(v, b, h, x), 4)
         layers(early_rims[0][-1] + 1, early_rims[1][0], lambda x: push_rim(s, v, b, x), 4)
-        receive_early(shape, s, v, b, rock, cohesion, friction, early_a, early_b)
-        inject(shape, s, cell, moment, lambda x: (x >= -BESIDE) & (x < rows_x + BESIDE))
         layers(*inner, lambda x: push_stress(shape, lanes, s, v, rock, x), 4)
         layers(*next_inner, lambda x: own_forces(lanes, s, v, b, x), 4)
+
+    def beside(s_in, v_in, b_in, rock_in, table, early_a, early_b, s, v, b, rock):
+        receive_early(shape, s, v, b, rock, table, early_a, early_b)
 
     def border(s_in, v_in, b, rock, got_a, got_b, sent_a, sent_b, s, v, out_a, out_b):
         receive_late(shape, v, b, (got_a, got_b), (sent_a, sent_b))
@@ -697,13 +727,12 @@
                 own_forces(lanes, s, v, b, x)
         send_y(shape, s, v, None, out_a, out_b, range(0, rows_x, 8))
 
-    def between(s_in, v_in, b, cell, moment, s, v):
+    def between(s, v_in, b, v):
         def rim(x):
             for c, value in enumerate(across_y(s, b, aligned(shape, x, -RIM))):
                 v[c, pl.ds(aligned(shape, x, -RIM), 8), :] = value
 
         layers(0, rows_x + 1, rim, 3)
-        inject(shape, s, cell, moment, lambda x: (x >= 0) & (x < rows_x))
 
     def finish(s_in, v_in, b, h_in, rock, got_a, got_b, s, v, h, v_out, s_out, sems):
         receive_y(shape, h, v, None, got_a, got_b, begun=True)
@@ -719,7 +748,6 @@
         for c in copies:
             c.wait()
 
-    cells = [source_cell, source_moment]
     first, second = swaps("gy", first, second)
     x_first, x_second = swaps("gx", x_first, x_second)
     v, b, h, sent_a, sent_b = call(
@@ -732,22 +760,32 @@
         aliases={1: 0, 2: 1, 3: 2},
     )
     got_a, got_b = swaps("gx", sent_a, sent_b)
-    rock = call(
+    rock, table = call(
         prepare,
-        [v, lame_first, modulus, zone, eligible, cohesion, friction],
-        [in_vmem] * 5 + [in_smem] * 2,
-        whole_r,
-        in_vmem,
+        [b, lame_first, modulus, zone, eligible]
+        + [cohesion, friction, source_cell, source_moment],
+        [in_vmem] * 5 + [in_smem] * 4,
+        [whole_r, vmem((2, cohesion.shape[0], 8, depth))],
+        [in_vmem] * 2,
         10000000,
     )
+    s, v = call(
+        interior,
+        [s, v, b, h, rock],
+        [in_vmem] * 5,
+        [whole_s, whole_v],
+        [in_vmem] * 2,
+        10000000,
+        aliases={0: 0, 1: 1},
+    )
     s, v, b, rock = call(
-        interior,
-        [s, v, b, h, rock, x_first, x_second] + cells + [cohesion, friction],
-        [in_vmem] * 7 + [in_smem] * 4,
+        beside,
+        [s, v, b, rock, table, x_first, x_second],
+        [in_vmem] * 7,
         [whole_s, whole_v, whole_b, whole_r],
         [in_vmem] * 4,
         10000000,
-        aliases={0: 0, 1: 1, 2: 2, 4: 3},
+        aliases={0: 0, 1: 1, 2: 2, 3: 3},
     )
     s, v, first, second = call(
         border,
@@ -759,15 +797,7 @@
         aliases={0: 0, 1: 1},
     )
     first, second = swaps("gy", first, second)
-    s, v = call(
-        between,
-        [s, v, b] + cells,
-        [in_vmem] * 3 + [in_smem] * 2,
-        [whole_s, whole_v],
-        [in_vmem] * 2,
-        10000000,
-        aliases={0: 0, 1: 1},
-    )
+    v = call(between, [s, v, b], [in_vmem] * 3, whole_v, in_vmem, 10000000, aliases={1: 0})
     outs = call(
         finish,
         [s, v, b, h, rock, first, second],

time: 30.3 us -> 29.4 us (0.970)
  the two profiles are of different devices: /device:TPU:19 before, /device:TPU:13 now
where the time goes in v6:
time: 29.4 us; the launch traced here: 29.2 us
  starting transfers between devices  14.6 us (50%)
  Pallas kernels  7.83 us (27%)
  waiting for transfers between devices  5.88 us (20%)
  between operations  0.87 us (3%)
    ppermute x8, starting transfers between devices, swaps(): got.append(lax.ppermute(block, axis, pairs))  14.6 us
    pallas_call x9, Pallas kernels, call(): pl.pallas_call(body, in_specs=in_specs, out_shape=out_shape, out_specs=ou...  7.83 us
    ppermute x8, waiting for transfers between devices, swaps(): got.append(lax.ppermute(block, axis, pairs))  5.88 us
  transfers between devices with their start and end apart: 8, of which 3 were waited for; matrix products, arithmetic and copies ran while one was open for 0% of the time, Pallas kernels for 11%

profile of v6, /device:TPU:13, one launch (start us, length us, event | category | flops | bytes accessed | tf_op | source)
XLA Modules:
  0.0 29.2 jit_solution(3091926455968227210)
XLA Ops:
  0.6 2.1 %shard_map.122 = (f32[6,784,128]{2,1,0:T(8,128)S(1)}, f32[3,784,128]{2,1,0:T(8,128)S(1)}, f32[784,128]{1,0:T(8,128)S(1)}, f32[3,784,128]{2,1,0:T(8,128)S(1)}, f3...) custom-call(f32[3,32,8,128]{3,2,1,0:T(8,128)} %v_in.1, ...), custom_call_target="tpu_custom_call" | custom-call | flops 10000000 | bytes 1000000 | tf_op jit(solution)/shard_map/pallas_call | solution.py:535
  2.7 0.7 %collective-permute-start = (f32[12,32,128]{2,1,0:T(8,128)S(1)}, f32[12,32,128]{2,1,0:T(8,128)S(1)}, u32[]{:S(2)}, u32[]{:S(2)}) collective-permute-start(f32[12,32,128]{2,1,0:T(8,128)S(1)} %get-tuple-element.35), channel_id=1, source_target_pairs={{0,1},{1,0},{2,3},{3,2},{4,5},{5,4},{6,7},{7,6},{8,9},{9,8},{10,11... | collective-permute-start | bytes 589832 | tf_op jit(solution)/shard_map/ppermute | solution.py:554
  3.4 3.1 %collective-permute-start.1 = (f32[12,32,128]{2,1,0:T(8,128)S(1)}, f32[12,32,128]{2,1,0:T(8,128)S(1)}, u32[]{:S(2)}, u32[]{:S(2)}) collective-permute-start(f32[12,32,128]{2,1,0:T(8,128)S(1)} %get-tuple-element.36), channel_id=1, source_target_pairs={{1,2},{2,1},{3,4},{4,3},{5,6},{6,5},{9,10},{10,9},{11,12},{12,11},... | collective-permute-start | bytes 589832 | tf_op jit(solution)/shard_map/ppermute | solution.py:554
  6.6 1.3 %collective-permute-start.2 = (f32[32,8,128]{2,1,0:T(8,128)S(1)}, f32[32,8,128]{2,1,0:T(8,128)S(1)}, u32[]{:S(2)}, u32[]{:S(2)}) collective-permute-start(f32[32,8,128]{2,1,0:T(8,128)S(1)} %get-tuple-element.46), channel_id=1, source_target_pairs={{0,8},{8,0},{16,24},{24,16},{1,9},{9,1},{17,25},{25,17},{2,10},{10... | collective-permute-start | bytes 393224 | tf_op jit(solution)/shard_map/ppermute | solution.py:554
  7.8 2.1 %collective-permute-start.3 = (f32[32,8,128]{2,1,0:T(8,128)S(1)}, f32[32,8,128]{2,1,0:T(8,128)S(1)}, u32[]{:S(2)}, u32[]{:S(2)}) collective-permute-start(f32[32,8,128]{2,1,0:T(8,128)S(1)} %get-tuple-element.47), channel_id=1, source_target_pairs={{8,16},{16,8},{9,17},{17,9},{10,18},{18,10},{11,19},{19,11},{12,20... | collective-permute-start | bytes 393224 | tf_op jit(solution)/shard_map/ppermute | solution.py:554
  9.9 0.0 collective-permute-done.got_a
  10.0 0.7 %collective-permute-done.1.got_b = f32[12,32,128]{2,1,0:T(8,128)S(1)} collective-permute-done((f32[12,32,128]{2,1,0:T(8,128)S(1)}, f32[12,32,128]{2,1,0:T(8,128)S(1)}, u32[]{:S(2)}, u32[]{:S(2)}) %collective-permute-start.1) | collective-permute-done | bytes 196640 | tf_op jit(solution)/shard_map/ppermute | solution.py:554
  10.7 0.0 copy-start
  10.7 0.0 copy-start.1
  10.7 0.0 copy-start.2
  10.7 0.0 copy-start.3
  10.7 0.0 copy-start.4
  10.7 0.0 copy-start.5
  10.7 0.0 copy-start.6
  10.7 0.0 copy-start.7
  10.7 0.3 shard_map.123
  11.0 1.3 %collective-permute-start.4 = (f32[160,128]{1,0:T(8,128)S(1)}, f32[160,128]{1,0:T(8,128)S(1)}, u32[]{:S(2)}, u32[]{:S(2)}) collective-permute-start(f32[160,128]{1,0:T(8,128)S(1)} %get-tuple-element.52.sent_a), channel_id=1, source_target_pairs={{0,8},{8,0},{16,24},{24,16},{1,9},{9,1},{17,25},{25,17},{2,10},{10... | collective-permute-start | bytes 245768 | tf_op jit(solution)/shard_map/ppermute | solution.py:554
  12.3 2.2 %collective-permute-start.5 = (f32[160,128]{1,0:T(8,128)S(1)}, f32[160,128]{1,0:T(8,128)S(1)}, u32[]{:S(2)}, u32[]{:S(2)}) collective-permute-start(f32[160,128]{1,0:T(8,128)S(1)} %get-tuple-element.53.sent_b), channel_id=1, source_target_pairs={{8,16},{16,8},{9,17},{17,9},{10,18},{18,10},{11,19},{19,11},{12,20... | collective-permute-start | bytes 245768 | tf_op jit(solution)/shard_map/ppermute | solution.py:554
  14.5 0.0 copy-done
  14.5 0.0 copy-done.1
  14.5 0.0 copy-done.2
  14.5 0.0 copy-done.3
  14.6 0.0 copy-done.4
  14.6 0.0 copy-done.5
  14.6 0.0 copy-done.6
  14.6 0.0 copy-done.7
  14.6 1.1 %shard_map.124 = (f32[11,312,128]{2,1,0:T(8,128)S(1)}, f32[2,8,8,128]{3,2,1,0:T(8,128)S(1)}) custom-call(f32[784,128]{1,0:T(8,128)S(1)} %get-tuple-element.38.after.b.b_in, f32[32,8,128]{2,1,0:T(8,128)S(1)} %copy-done, f32[32,8,128]{2,1,0:T(8,128)S(1)} %copy-done.1, s32[32,8,128]{2,1,0:T(8,128)S(1)} %copy-done.2, s32[32,8,128]{2,1,0:T(8,128)S(1)} %copy-done.3, ...), custom_call_target="tpu_custom_call" | custom-call | flops 10000000 | bytes 1000000 | tf_op jit(solution)/shard_map/pallas_call | solution.py:535
  15.7 1.6 %shard_map.125 = (f32[6,784,128]{2,1,0:T(8,128)S(1)}, f32[3,784,128]{2,1,0:T(8,128)S(1)}) custom-call(f32[6,784,128]{2,1,0:T(8,128)S(1)} %get-tuple-element.31.s.s_in, f32[3,784,128]{2,1,0:T(8,128)S(1)} %get-tuple-element.37.v_in, f32[784,128]{1,0:T(8,128)S(1)} %get-tuple-element.38.after.b.b_in, ...), custom_call_target="tpu_custom_call", output_to_operand_aliasing={{0}: (0, {}), {1}: (1, {})} | custom-call | flops 10000000 | bytes 1000000 | tf_op jit(solution)/shard_map/pallas_call | solution.py:535
  17.3 0.0 collective-permute-done.2.early_a
  17.3 0.0 collective-permute-done.3.early_b
  17.3 0.1 shard_map.127
  17.4 0.0 collective-permute-done.4.got_a
  17.4 1.9 %collective-permute-done.5.got_b = f32[160,128]{1,0:T(8,128)S(1)} collective-permute-done((f32[160,128]{1,0:T(8,128)S(1)}, f32[160,128]{1,0:T(8,128)S(1)}, u32[]{:S(2)}, u32[]{:S(2)}) %collective-permute-start.5) | collective-permute-done | bytes 81952 | tf_op jit(solution)/shard_map/ppermute | solution.py:554
  19.3 0.7 %shard_map.128 = (f32[6,784,128]{2,1,0:T(8,128)S(1)}, f32[3,784,128]{2,1,0:T(8,128)S(1)}, f32[10,32,128]{2,1,0:T(8,128)S(1)}, f32[10,32,128]{2,1,0:T(8,128)S(1)}) custom-call(f32[6,784,128]{2,1,0:T(8,128)S(1)} %get-tuple-element.48.s_in, f32[3,784,128]{2,1,0:T(8,128)S(1)} %get-tuple-element.49.v_in, ...), custom_call_target="tpu_custom_call", output_to_operand_aliasing={{0}: (0, {}), {1}: (1, {})} | custom-call | flops 10000000 | bytes 1000000 | tf_op jit(solution)/shard_map/pallas_call | solution.py:535
  19.9 0.8 %collective-permute-start.6 = (f32[10,32,128]{2,1,0:T(8,128)S(1)}, f32[10,32,128]{2,1,0:T(8,128)S(1)}, u32[]{:S(2)}, u32[]{:S(2)}) collective-permute-start(f32[10,32,128]{2,1,0:T(8,128)S(1)} %get-tuple-element.56), channel_id=1, source_target_pairs={{0,1},{1,0},{2,3},{3,2},{4,5},{5,4},{6,7},{7,6},{8,9},{9,8},{10,11... | collective-permute-start | bytes 491528 | tf_op jit(solution)/shard_map/ppermute | solution.py:554
  20.8 3.1 %collective-permute-start.7 = (f32[10,32,128]{2,1,0:T(8,128)S(1)}, f32[10,32,128]{2,1,0:T(8,128)S(1)}, u32[]{:S(2)}, u32[]{:S(2)}) collective-permute-start(f32[10,32,128]{2,1,0:T(8,128)S(1)} %get-tuple-element.57), channel_id=1, source_target_pairs={{1,2},{2,1},{3,4},{4,3},{5,6},{6,5},{9,10},{10,9},{11,12},{12,11},... | collective-permute-start | bytes 491528 | tf_op jit(solution)/shard_map/ppermute | solution.py:554
  23.9 0.2 shard_map.129.v_in
  24.1 0.0 collective-permute-done.6.got_a
  24.1 3.3 %collective-permute-done.7.got_b = f32[10,32,128]{2,1,0:T(8,128)S(1)} collective-permute-done((f32[10,32,128]{2,1,0:T(8,128)S(1)}, f32[10,32,128]{2,1,0:T(8,128)S(1)}, u32[]{:S(2)}, u32[]{:S(2)}) %collective-permute-start.7) | collective-permute-done | bytes 163872 | tf_op jit(solution)/shard_map/ppermute | solution.py:554
  27.4 1.8 %shard_map.130 = (f32[6,784,128]{2,1,0:T(8,128)S(1)}, f32[3,784,128]{2,1,0:T(8,128)S(1)}, f32[3,784,128]{2,1,0:T(8,128)S(1)}, f32[3,32,8,128]{3,2,1,0:T(8,128)}, f32[6,32,8,128]{3,2,1,0:T(8,128)}) custom-call(f32[6,784,128]{2,1,0:T(8,128)S(1)} %get-tuple-element.54.s.s_in, ...), custom_call_target="tpu_custom_call", output_to_operand_aliasing={{0}: (0, {}), {1}: (1, {}), {2}: (3, {})} | custom-call | flops 10000000 | bytes 1000000 | tf_op jit(solution)/shard_map/pallas_call | solution.py:535
  (1 shorter events, 0.0 us)
Async XLA Ops:
  2.7 7.2 %collective-permute-start = (f32[12,32,128]{2,1,0:T(8,128)S(1)}, f32[12,32,128]{2,1,0:T(8,128)S(1)}, u32[]{:S(2)}, u32[]{:S(2)}) collective-permute-start(f32[12,32,128]{2,1,0:T(8,128)S(1)} %get-tuple-element.35), channel_id=1, source_target_pairs={{0,1},{1,0},{2,3},{3,2},{4,5},{5,4},{6,7},{7,6},{8,9},{9,8},{10,11... | collective-permute-start | bytes 589832 | tf_op jit(solution)/shard_map/ppermute | solution.py:554
  3.4 7.3 %collective-permute-start.1 = (f32[12,32,128]{2,1,0:T(8,128)S(1)}, f32[12,32,128]{2,1,0:T(8,128)S(1)}, u32[]{:S(2)}, u32[]{:S(2)}) collective-permute-start(f32[12,32,128]{2,1,0:T(8,128)S(1)} %get-tuple-element.36), channel_id=1, source_target_pairs={{1,2},{2,1},{3,4},{4,3},{5,6},{6,5},{9,10},{10,9},{11,12},{12,11},... | collective-permute-start | bytes 589832 | tf_op jit(solution)/shard_map/ppermute | solution.py:554
  6.6 10.7 %collective-permute-start.2 = (f32[32,8,128]{2,1,0:T(8,128)S(1)}, f32[32,8,128]{2,1,0:T(8,128)S(1)}, u32[]{:S(2)}, u32[]{:S(2)}) collective-permute-start(f32[32,8,128]{2,1,0:T(8,128)S(1)} %get-tuple-element.46), channel_id=1, source_target_pairs={{0,8},{8,0},{16,24},{24,16},{1,9},{9,1},{17,25},{25,17},{2,10},{10... | collective-permute-start | bytes 393224 | tf_op jit(solution)/shard_map/ppermute | solution.py:554
  7.8 9.5 %collective-permute-start.3 = (f32[32,8,128]{2,1,0:T(8,128)S(1)}, f32[32,8,128]{2,1,0:T(8,128)S(1)}, u32[]{:S(2)}, u32[]{:S(2)}) collective-permute-start(f32[32,8,128]{2,1,0:T(8,128)S(1)} %get-tuple-element.47), channel_id=1, source_target_pairs={{8,16},{16,8},{9,17},{17,9},{10,18},{18,10},{11,19},{19,11},{12,20... | collective-permute-start | bytes 393224 | tf_op jit(solution)/shard_map/ppermute | solution.py:554
  10.7 3.8 %copy-start = (f32[32,8,128]{2,1,0:T(8,128)S(1)}, f32[32,8,128]{2,1,0:T(8,128)}, u32[]{:S(2)}) copy-start(f32[32,8,128]{2,1,0:T(8,128)} %lame_in.3) | copy-start | bytes 393220
  10.7 3.8 %copy-start.1 = (f32[32,8,128]{2,1,0:T(8,128)S(1)}, f32[32,8,128]{2,1,0:T(8,128)}, u32[]{:S(2)}) copy-start(f32[32,8,128]{2,1,0:T(8,128)} %shear_in.3) | copy-start | bytes 393220
  10.7 3.9 %copy-start.2 = (s32[32,8,128]{2,1,0:T(8,128)S(1)}, s32[32,8,128]{2,1,0:T(8,128)}, u32[]{:S(2)}) copy-start(s32[32,8,128]{2,1,0:T(8,128)} %zone_in.3) | copy-start | bytes 393220
  10.7 3.9 %copy-start.3 = (s32[32,8,128]{2,1,0:T(8,128)S(1)}, s32[32,8,128]{2,1,0:T(8,128)}, u32[]{:S(2)}) copy-start(s32[32,8,128]{2,1,0:T(8,128)} %able_in.3) | copy-start | bytes 393220
  10.7 3.9 %copy-start.4 = (f32[6,16]{1,0:T(8,128)S(1)}, f32[6,16]{1,0:T(8,128)}, u32[]{:S(2)}) copy-start(f32[6,16]{1,0:T(8,128)} %moment.1) | copy-start | bytes 1156
  10.7 3.9 %copy-start.5 = (f32[8]{0:T(128)S(1)}, f32[8]{0:T(128)}, u32[]{:S(2)}) copy-start(f32[8]{0:T(128)} %cohesion.1) | copy-start | bytes 100
  10.7 3.9 %copy-start.6 = (f32[8]{0:T(128)S(1)}, f32[8]{0:T(128)}, u32[]{:S(2)}) copy-start(f32[8]{0:T(128)} %friction.1) | copy-start | bytes 100
  10.7 3.9 %copy-start.7 = (s32[16]{0:T(128)S(1)}, s32[16]{0:T(128)}, u32[]{:S(2)}) copy-start(s32[16]{0:T(128)} %cell.1) | copy-start | bytes 196
  11.0 6.4 %collective-permute-start.4 = (f32[160,128]{1,0:T(8,128)S(1)}, f32[160,128]{1,0:T(8,128)S(1)}, u32[]{:S(2)}, u32[]{:S(2)}) collective-permute-start(f32[160,128]{1,0:T(8,128)S(1)} %get-tuple-element.52.sent_a), channel_id=1, source_target_pairs={{0,8},{8,0},{16,24},{24,16},{1,9},{9,1},{17,25},{25,17},{2,10},{10... | collective-permute-start | bytes 245768 | tf_op jit(solution)/shard_map/ppermute | solution.py:554
  12.3 7.0 %collective-permute-start.5 = (f32[160,128]{1,0:T(8,128)S(1)}, f32[160,128]{1,0:T(8,128)S(1)}, u32[]{:S(2)}, u32[]{:S(2)}) collective-permute-start(f32[160,128]{1,0:T(8,128)S(1)} %get-tuple-element.53.sent_b), channel_id=1, source_target_pairs={{8,16},{16,8},{9,17},{17,9},{10,18},{18,10},{11,19},{19,11},{12,20... | collective-permute-start | bytes 245768 | tf_op jit(solution)/shard_map/ppermute | solution.py:554
  19.9 4.2 %collective-permute-start.6 = (f32[10,32,128]{2,1,0:T(8,128)S(1)}, f32[10,32,128]{2,1,0:T(8,128)S(1)}, u32[]{:S(2)}, u32[]{:S(2)}) collective-permute-start(f32[10,32,128]{2,1,0:T(8,128)S(1)} %get-tuple-element.56), channel_id=1, source_target_pairs={{0,1},{1,0},{2,3},{3,2},{4,5},{5,4},{6,7},{7,6},{8,9},{9,8},{10,11... | collective-permute-start | bytes 491528 | tf_op jit(solution)/shard_map/ppermute | solution.py:554
  20.8 6.6 %collective-permute-start.7 = (f32[10,32,128]{2,1,0:T(8,128)S(1)}, f32[10,32,128]{2,1,0:T(8,128)S(1)}, u32[]{:S(2)}, u32[]{:S(2)}) collective-permute-start(f32[10,32,128]{2,1,0:T(8,128)S(1)} %get-tuple-element.57), channel_id=1, source_target_pairs={{1,2},{2,1},{3,4},{4,3},{5,6},{6,5},{9,10},{10,9},{11,12},{12,11},... | collective-permute-start | bytes 491528 | tf_op jit(solution)/shard_map/ppermute | solution.py:554

commit v7 on v6

--- a/solution.py
+++ b/solution.py
@@ -740,10 +740,12 @@
         layers(-2, rows_x + 2, lambda x: push_rows(v, b, h, x), 4)
         copies = [pltpu.make_async_copy(own_cells(shape, v), v_out, sems.at[0])]
         copies[0].start()
-        for i, x in enumerate(range(0, rows_x, 8)):
-            layers(x, x + 8, lambda x: push_stress(shape, lanes, s, v, rock, x), 8)
-            part = s_out.at[:, pl.ds(x, 8)]
-            copies.append(pltpu.make_async_copy(own_cells(shape, s, x, 8), part, sems.at[i + 1]))
+        marks = list(range(0, rows_x - 8, 8)) + [rows_x - 8, rows_x - 4, rows_x]
+        for i, (x, stop) in enumerate(zip(marks, marks[1:])):
+            n = stop - x
+            layers(x, stop, lambda x: push_stress(shape, lanes, s, v, rock, x), n)
+            part = s_out.at[:, pl.ds(x, n)]
+            copies.append(pltpu.make_async_copy(own_cells(shape, s, x, n), part, sems.at[i + 1]))
             copies[-1].start()
         for c in copies:
             c.wait()
@@ -812,7 +814,7 @@
         [in_vmem] * 3 + [in_hbm] * 2,
         10000000,
         aliases={0: 0, 1: 1, 3: 2},
-        scratch=[pltpu.SemaphoreType.DMA((rows_x // 8 + 1,))],
+        scratch=[pltpu.SemaphoreType.DMA((rows_x // 8 + 2,))],
     )
     return (outs[3], outs[4])
 

time: 29.4 us -> 29.5 us (level)
  no operation moved by 1% of the time
where the time goes in v7:
time: 29.5 us; the launch traced here: 29.2 us
  starting transfers between devices  14.6 us (49%)
  Pallas kernels  7.88 us (27%)
  waiting for transfers between devices  5.88 us (20%)
  between operations  0.87 us (3%)
    ppermute x8, starting transfers between devices, swaps(): got.append(lax.ppermute(block, axis, pairs))  14.6 us
    pallas_call x9, Pallas kernels, call(): pl.pallas_call(body, in_specs=in_specs, out_shape=out_shape, out_specs=ou...  7.88 us
    ppermute x8, waiting for transfers between devices, swaps(): got.append(lax.ppermute(block, axis, pairs))  5.88 us
  transfers between devices with their start and end apart: 8, of which 3 were waited for; matrix products, arithmetic and copies ran while one was open for 0% of the time, Pallas kernels for 11%

profile of v7, /device:TPU:13, one launch (start us, length us, event | category | flops | bytes accessed | tf_op | source)
XLA Modules:
  0.0 29.2 jit_solution(1381112962834897858)
XLA Ops:
  0.6 2.1 %shard_map.122 = (f32[6,784,128]{2,1,0:T(8,128)S(1)}, f32[3,784,128]{2,1,0:T(8,128)S(1)}, f32[784,128]{1,0:T(8,128)S(1)}, f32[3,784,128]{2,1,0:T(8,128)S(1)}, f3...) custom-call(f32[3,32,8,128]{3,2,1,0:T(8,128)} %v_in.1, ...), custom_call_target="tpu_custom_call" | custom-call | flops 10000000 | bytes 1000000 | tf_op jit(solution)/shard_map/pallas_call | solution.py:535
  2.7 0.7 %collective-permute-start = (f32[12,32,128]{2,1,0:T(8,128)S(1)}, f32[12,32,128]{2,1,0:T(8,128)S(1)}, u32[]{:S(2)}, u32[]{:S(2)}) collective-permute-start(f32[12,32,128]{2,1,0:T(8,128)S(1)} %get-tuple-element.35), channel_id=1, source_target_pairs={{0,1},{1,0},{2,3},{3,2},{4,5},{5,4},{6,7},{7,6},{8,9},{9,8},{10,11... | collective-permute-start | bytes 589832 | tf_op jit(solution)/shard_map/ppermute | solution.py:554
  3.4 3.1 %collective-permute-start.1 = (f32[12,32,128]{2,1,0:T(8,128)S(1)}, f32[12,32,128]{2,1,0:T(8,128)S(1)}, u32[]{:S(2)}, u32[]{:S(2)}) collective-permute-start(f32[12,32,128]{2,1,0:T(8,128)S(1)} %get-tuple-element.36), channel_id=1, source_target_pairs={{1,2},{2,1},{3,4},{4,3},{5,6},{6,5},{9,10},{10,9},{11,12},{12,11},... | collective-permute-start | bytes 589832 | tf_op jit(solution)/shard_map/ppermute | solution.py:554
  6.6 1.3 %collective-permute-start.2 = (f32[32,8,128]{2,1,0:T(8,128)S(1)}, f32[32,8,128]{2,1,0:T(8,128)S(1)}, u32[]{:S(2)}, u32[]{:S(2)}) collective-permute-start(f32[32,8,128]{2,1,0:T(8,128)S(1)} %get-tuple-element.46), channel_id=1, source_target_pairs={{0,8},{8,0},{16,24},{24,16},{1,9},{9,1},{17,25},{25,17},{2,10},{10... | collective-permute-start | bytes 393224 | tf_op jit(solution)/shard_map/ppermute | solution.py:554
  7.8 2.1 %collective-permute-start.3 = (f32[32,8,128]{2,1,0:T(8,128)S(1)}, f32[32,8,128]{2,1,0:T(8,128)S(1)}, u32[]{:S(2)}, u32[]{:S(2)}) collective-permute-start(f32[32,8,128]{2,1,0:T(8,128)S(1)} %get-tuple-element.47), channel_id=1, source_target_pairs={{8,16},{16,8},{9,17},{17,9},{10,18},{18,10},{11,19},{19,11},{12,20... | collective-permute-start | bytes 393224 | tf_op jit(solution)/shard_map/ppermute | solution.py:554
  9.9 0.0 collective-permute-done.got_a
  10.0 0.7 %collective-permute-done.1.got_b = f32[12,32,128]{2,1,0:T(8,128)S(1)} collective-permute-done((f32[12,32,128]{2,1,0:T(8,128)S(1)}, f32[12,32,128]{2,1,0:T(8,128)S(1)}, u32[]{:S(2)}, u32[]{:S(2)}) %collective-permute-start.1) | collective-permute-done | bytes 196640 | tf_op jit(solution)/shard_map/ppermute | solution.py:554
  10.7 0.0 copy-start
  10.7 0.0 copy-start.1
  10.7 0.0 copy-start.2
  10.7 0.0 copy-start.3
  10.7 0.0 copy-start.4
  10.7 0.0 copy-start.5
  10.7 0.0 copy-start.6
  10.7 0.0 copy-start.7
  10.7 0.3 shard_map.123
  11.0 1.3 %collective-permute-start.4 = (f32[160,128]{1,0:T(8,128)S(1)}, f32[160,128]{1,0:T(8,128)S(1)}, u32[]{:S(2)}, u32[]{:S(2)}) collective-permute-start(f32[160,128]{1,0:T(8,128)S(1)} %get-tuple-element.52.sent_a), channel_id=1, source_target_pairs={{0,8},{8,0},{16,24},{24,16},{1,9},{9,1},{17,25},{25,17},{2,10},{10... | collective-permute-start | bytes 245768 | tf_op jit(solution)/shard_map/ppermute | solution.py:554
  12.3 2.2 %collective-permute-start.5 = (f32[160,128]{1,0:T(8,128)S(1)}, f32[160,128]{1,0:T(8,128)S(1)}, u32[]{:S(2)}, u32[]{:S(2)}) collective-permute-start(f32[160,128]{1,0:T(8,128)S(1)} %get-tuple-element.53.sent_b), channel_id=1, source_target_pairs={{8,16},{16,8},{9,17},{17,9},{10,18},{18,10},{11,19},{19,11},{12,20... | collective-permute-start | bytes 245768 | tf_op jit(solution)/shard_map/ppermute | solution.py:554
  14.5 0.0 copy-done
  14.5 0.0 copy-done.1
  14.5 0.0 copy-done.2
  14.5 0.0 copy-done.3
  14.6 0.0 copy-done.4
  14.6 0.0 copy-done.5
  14.6 0.0 copy-done.6
  14.6 0.0 copy-done.7
  14.6 1.1 %shard_map.124 = (f32[11,312,128]{2,1,0:T(8,128)S(1)}, f32[2,8,8,128]{3,2,1,0:T(8,128)S(1)}) custom-call(f32[784,128]{1,0:T(8,128)S(1)} %get-tuple-element.38.after.b.b_in, f32[32,8,128]{2,1,0:T(8,128)S(1)} %copy-done, f32[32,8,128]{2,1,0:T(8,128)S(1)} %copy-done.1, s32[32,8,128]{2,1,0:T(8,128)S(1)} %copy-done.2, s32[32,8,128]{2,1,0:T(8,128)S(1)} %copy-done.3, ...), custom_call_target="tpu_custom_call" | custom-call | flops 10000000 | bytes 1000000 | tf_op jit(solution)/shard_map/pallas_call | solution.py:535
  15.7 1.6 %shard_map.125 = (f32[6,784,128]{2,1,0:T(8,128)S(1)}, f32[3,784,128]{2,1,0:T(8,128)S(1)}) custom-call(f32[6,784,128]{2,1,0:T(8,128)S(1)} %get-tuple-element.31.s.s_in, f32[3,784,128]{2,1,0:T(8,128)S(1)} %get-tuple-element.37.v_in, f32[784,128]{1,0:T(8,128)S(1)} %get-tuple-element.38.after.b.b_in, ...), custom_call_target="tpu_custom_call", output_to_operand_aliasing={{0}: (0, {}), {1}: (1, {})} | custom-call | flops 10000000 | bytes 1000000 | tf_op jit(solution)/shard_map/pallas_call | solution.py:535
  17.3 0.0 collective-permute-done.2.early_a
  17.3 0.0 collective-permute-done.3.early_b
  17.3 0.1 shard_map.127
  17.4 0.0 collective-permute-done.4.got_a
  17.4 1.9 %collective-permute-done.5.got_b = f32[160,128]{1,0:T(8,128)S(1)} collective-permute-done((f32[160,128]{1,0:T(8,128)S(1)}, f32[160,128]{1,0:T(8,128)S(1)}, u32[]{:S(2)}, u32[]{:S(2)}) %collective-permute-start.5) | collective-permute-done | bytes 81952 | tf_op jit(solution)/shard_map/ppermute | solution.py:554
  19.3 0.7 %shard_map.128 = (f32[6,784,128]{2,1,0:T(8,128)S(1)}, f32[3,784,128]{2,1,0:T(8,128)S(1)}, f32[10,32,128]{2,1,0:T(8,128)S(1)}, f32[10,32,128]{2,1,0:T(8,128)S(1)}) custom-call(f32[6,784,128]{2,1,0:T(8,128)S(1)} %get-tuple-element.48.s_in, f32[3,784,128]{2,1,0:T(8,128)S(1)} %get-tuple-element.49.v_in, ...), custom_call_target="tpu_custom_call", output_to_operand_aliasing={{0}: (0, {}), {1}: (1, {})} | custom-call | flops 10000000 | bytes 1000000 | tf_op jit(solution)/shard_map/pallas_call | solution.py:535
  19.9 0.8 %collective-permute-start.6 = (f32[10,32,128]{2,1,0:T(8,128)S(1)}, f32[10,32,128]{2,1,0:T(8,128)S(1)}, u32[]{:S(2)}, u32[]{:S(2)}) collective-permute-start(f32[10,32,128]{2,1,0:T(8,128)S(1)} %get-tuple-element.56), channel_id=1, source_target_pairs={{0,1},{1,0},{2,3},{3,2},{4,5},{5,4},{6,7},{7,6},{8,9},{9,8},{10,11... | collective-permute-start | bytes 491528 | tf_op jit(solution)/shard_map/ppermute | solution.py:554
  20.8 3.1 %collective-permute-start.7 = (f32[10,32,128]{2,1,0:T(8,128)S(1)}, f32[10,32,128]{2,1,0:T(8,128)S(1)}, u32[]{:S(2)}, u32[]{:S(2)}) collective-permute-start(f32[10,32,128]{2,1,0:T(8,128)S(1)} %get-tuple-element.57), channel_id=1, source_target_pairs={{1,2},{2,1},{3,4},{4,3},{5,6},{6,5},{9,10},{10,9},{11,12},{12,11},... | collective-permute-start | bytes 491528 | tf_op jit(solution)/shard_map/ppermute | solution.py:554
  23.9 0.2 shard_map.129.v_in
  24.1 0.0 collective-permute-done.6.got_a
  24.1 3.3 %collective-permute-done.7.got_b = f32[10,32,128]{2,1,0:T(8,128)S(1)} collective-permute-done((f32[10,32,128]{2,1,0:T(8,128)S(1)}, f32[10,32,128]{2,1,0:T(8,128)S(1)}, u32[]{:S(2)}, u32[]{:S(2)}) %collective-permute-start.7) | collective-permute-done | bytes 163872 | tf_op jit(solution)/shard_map/ppermute | solution.py:554
  27.4 1.8 %shard_map.130 = (f32[6,784,128]{2,1,0:T(8,128)S(1)}, f32[3,784,128]{2,1,0:T(8,128)S(1)}, f32[3,784,128]{2,1,0:T(8,128)S(1)}, f32[3,32,8,128]{3,2,1,0:T(8,128)}, f32[6,32,8,128]{3,2,1,0:T(8,128)}) custom-call(f32[6,784,128]{2,1,0:T(8,128)S(1)} %get-tuple-element.54.s.s_in, ...), custom_call_target="tpu_custom_call", output_to_operand_aliasing={{0}: (0, {}), {1}: (1, {}), {2}: (3, {})} | custom-call | flops 10000000 | bytes 1000000 | tf_op jit(solution)/shard_map/pallas_call | solution.py:535
  (1 shorter events, 0.0 us)
Async XLA Ops:
  2.7 7.2 %collective-permute-start = (f32[12,32,128]{2,1,0:T(8,128)S(1)}, f32[12,32,128]{2,1,0:T(8,128)S(1)}, u32[]{:S(2)}, u32[]{:S(2)}) collective-permute-start(f32[12,32,128]{2,1,0:T(8,128)S(1)} %get-tuple-element.35), channel_id=1, source_target_pairs={{0,1},{1,0},{2,3},{3,2},{4,5},{5,4},{6,7},{7,6},{8,9},{9,8},{10,11... | collective-permute-start | bytes 589832 | tf_op jit(solution)/shard_map/ppermute | solution.py:554
  3.4 7.3 %collective-permute-start.1 = (f32[12,32,128]{2,1,0:T(8,128)S(1)}, f32[12,32,128]{2,1,0:T(8,128)S(1)}, u32[]{:S(2)}, u32[]{:S(2)}) collective-permute-start(f32[12,32,128]{2,1,0:T(8,128)S(1)} %get-tuple-element.36), channel_id=1, source_target_pairs={{1,2},{2,1},{3,4},{4,3},{5,6},{6,5},{9,10},{10,9},{11,12},{12,11},... | collective-permute-start | bytes 589832 | tf_op jit(solution)/shard_map/ppermute | solution.py:554
  6.6 10.7 %collective-permute-start.2 = (f32[32,8,128]{2,1,0:T(8,128)S(1)}, f32[32,8,128]{2,1,0:T(8,128)S(1)}, u32[]{:S(2)}, u32[]{:S(2)}) collective-permute-start(f32[32,8,128]{2,1,0:T(8,128)S(1)} %get-tuple-element.46), channel_id=1, source_target_pairs={{0,8},{8,0},{16,24},{24,16},{1,9},{9,1},{17,25},{25,17},{2,10},{10... | collective-permute-start | bytes 393224 | tf_op jit(solution)/shard_map/ppermute | solution.py:554
  7.8 9.5 %collective-permute-start.3 = (f32[32,8,128]{2,1,0:T(8,128)S(1)}, f32[32,8,128]{2,1,0:T(8,128)S(1)}, u32[]{:S(2)}, u32[]{:S(2)}) collective-permute-start(f32[32,8,128]{2,1,0:T(8,128)S(1)} %get-tuple-element.47), channel_id=1, source_target_pairs={{8,16},{16,8},{9,17},{17,9},{10,18},{18,10},{11,19},{19,11},{12,20... | collective-permute-start | bytes 393224 | tf_op jit(solution)/shard_map/ppermute | solution.py:554
  10.7 3.8 %copy-start = (f32[32,8,128]{2,1,0:T(8,128)S(1)}, f32[32,8,128]{2,1,0:T(8,128)}, u32[]{:S(2)}) copy-start(f32[32,8,128]{2,1,0:T(8,128)} %lame_in.3) | copy-start | bytes 393220
  10.7 3.8 %copy-start.1 = (f32[32,8,128]{2,1,0:T(8,128)S(1)}, f32[32,8,128]{2,1,0:T(8,128)}, u32[]{:S(2)}) copy-start(f32[32,8,128]{2,1,0:T(8,128)} %shear_in.3) | copy-start | bytes 393220
  10.7 3.9 %copy-start.2 = (s32[32,8,128]{2,1,0:T(8,128)S(1)}, s32[32,8,128]{2,1,0:T(8,128)}, u32[]{:S(2)}) copy-start(s32[32,8,128]{2,1,0:T(8,128)} %zone_in.3) | copy-start | bytes 393220
  10.7 3.9 %copy-start.3 = (s32[32,8,128]{2,1,0:T(8,128)S(1)}, s32[32,8,128]{2,1,0:T(8,128)}, u32[]{:S(2)}) copy-start(s32[32,8,128]{2,1,0:T(8,128)} %able_in.3) | copy-start | bytes 393220
  10.7 3.9 %copy-start.4 = (f32[6,16]{1,0:T(8,128)S(1)}, f32[6,16]{1,0:T(8,128)}, u32[]{:S(2)}) copy-start(f32[6,16]{1,0:T(8,128)} %moment.1) | copy-start | bytes 1156
  10.7 3.9 %copy-start.5 = (f32[8]{0:T(128)S(1)}, f32[8]{0:T(128)}, u32[]{:S(2)}) copy-start(f32[8]{0:T(128)} %cohesion.1) | copy-start | bytes 100
  10.7 3.9 %copy-start.6 = (f32[8]{0:T(128)S(1)}, f32[8]{0:T(128)}, u32[]{:S(2)}) copy-start(f32[8]{0:T(128)} %friction.1) | copy-start | bytes 100
  10.7 3.9 %copy-start.7 = (s32[16]{0:T(128)S(1)}, s32[16]{0:T(128)}, u32[]{:S(2)}) copy-start(s32[16]{0:T(128)} %cell.1) | copy-start | bytes 196
  11.0 6.4 %collective-permute-start.4 = (f32[160,128]{1,0:T(8,128)S(1)}, f32[160,128]{1,0:T(8,128)S(1)}, u32[]{:S(2)}, u32[]{:S(2)}) collective-permute-start(f32[160,128]{1,0:T(8,128)S(1)} %get-tuple-element.52.sent_a), channel_id=1, source_target_pairs={{0,8},{8,0},{16,24},{24,16},{1,9},{9,1},{17,25},{25,17},{2,10},{10... | collective-permute-start | bytes 245768 | tf_op jit(solution)/shard_map/ppermute | solution.py:554
  12.3 7.0 %collective-permute-start.5 = (f32[160,128]{1,0:T(8,128)S(1)}, f32[160,128]{1,0:T(8,128)S(1)}, u32[]{:S(2)}, u32[]{:S(2)}) collective-permute-start(f32[160,128]{1,0:T(8,128)S(1)} %get-tuple-element.53.sent_b), channel_id=1, source_target_pairs={{8,16},{16,8},{9,17},{17,9},{10,18},{18,10},{11,19},{19,11},{12,20... | collective-permute-start | bytes 245768 | tf_op jit(solution)/shard_map/ppermute | solution.py:554
  19.9 4.2 %collective-permute-start.6 = (f32[10,32,128]{2,1,0:T(8,128)S(1)}, f32[10,32,128]{2,1,0:T(8,128)S(1)}, u32[]{:S(2)}, u32[]{:S(2)}) collective-permute-start(f32[10,32,128]{2,1,0:T(8,128)S(1)} %get-tuple-element.56), channel_id=1, source_target_pairs={{0,1},{1,0},{2,3},{3,2},{4,5},{5,4},{6,7},{7,6},{8,9},{9,8},{10,11... | collective-permute-start | bytes 491528 | tf_op jit(solution)/shard_map/ppermute | solution.py:554
  20.8 6.6 %collective-permute-start.7 = (f32[10,32,128]{2,1,0:T(8,128)S(1)}, f32[10,32,128]{2,1,0:T(8,128)S(1)}, u32[]{:S(2)}, u32[]{:S(2)}) collective-permute-start(f32[10,32,128]{2,1,0:T(8,128)S(1)} %get-tuple-element.57), channel_id=1, source_target_pairs={{1,2},{2,1},{3,4},{4,3},{5,6},{6,5},{9,10},{10,9},{11,12},{12,11},... | collective-permute-start | bytes 491528 | tf_op jit(solution)/shard_map/ppermute | solution.py:554
